TPU v7x, 768 devices: a whole 4x8x12 slice. The times are simulated.
768 devices in a mesh: gz: 96 (over z, x, core), gy: 8 (over y).
Axes of the slice: x: 4, y: 8, z: 12, core: 2. Of those that a mesh axis runs over, the one named last changes fastest.
Arguments:
- populations: float32 [19, 288, 384, 128], P(None, 'gz', 'gy'), may hold values from 0.1 to 25, as said below
- solute: float32 [7, 288, 384, 128], P(None, 'gz', 'gy'), may hold values from 0.05 to 3, as said below
- pore_mask: int32 [288, 384, 128], P('gz', 'gy'), may hold values from 0 to 2
- mineral_ids: int32 [288, 384, 128], P('gz', 'gy'), may hold values from 0 to 7
- reaction_rates: float32 [8], replicated, may hold values from 0.05 to 0.6
- saturation: float32 [8], replicated, may hold values from 0.5 to 6
Outputs:
- flow_next: float32 [19, 288, 384, 128], P(None, 'gz', 'gy')
- solute_next: float32 [7, 288, 384, 128], P(None, 'gz', 'gy')
Inputs may be any that keep to these rules, and one draw needn't show every extreme that they name: `populations`: every population is positive. `solute`: every population is positive.
All inputs are finite; a program needn't handle non-finite values.
Results may differ from a plain program's by a relative error of at most 0.0003.
Values sent between devices are 32-bit elements; how exact they have to be, the bound alone decides.
No kernel may reach another device: no remote copies, remote signals or barrier semaphores. Data moves between devices by JAX's collectives and lax.ppermute only.
A program may use at most 32 MiB of HBM per device.

v0:
```python
import jax
import jax.numpy as jnp
import numpy as np
from jax import lax
from jax.sharding import PartitionSpec as P

LINKS19 = np.array(
    [
        [0, 0, 0],
        [1, 0, 0],
        [-1, 0, 0],
        [0, 1, 0],
        [0, -1, 0],
        [0, 0, 1],
        [0, 0, -1],
        [1, 1, 0],
        [-1, -1, 0],
        [1, -1, 0],
        [-1, 1, 0],
        [1, 0, 1],
        [-1, 0, -1],
        [1, 0, -1],
        [-1, 0, 1],
        [0, 1, 1],
        [0, -1, -1],
        [0, 1, -1],
        [0, -1, 1],
    ]
)
REVERSE19 = [0, 2, 1, 4, 3, 6, 5, 8, 7, 10, 9, 12, 11, 14, 13, 16, 15, 18, 17]
WEIGHTS19 = np.array([1.0 / 3.0] + [1.0 / 18.0] * 6 + [1.0 / 36.0] * 12)
WEIGHTS7 = np.array([0.25] + [0.125] * 6)
RELAX_FLOW = 1.25
RELAX_SOLUTE = 1.4


def with_halo(cells, sides, width):
    for axis, dim in sides:
        count = lax.axis_size(axis)
        head = lax.slice_in_dim(cells, 0, width, axis=dim)
        tail = lax.slice_in_dim(cells, cells.shape[dim] - width, cells.shape[dim], axis=dim)
        cells = jnp.concatenate(
            [
                lax.ppermute(tail, axis, [(i, (i + 1) % count) for i in range(count)]),
                cells,
                lax.ppermute(head, axis, [((i + 1) % count, i) for i in range(count)]),
            ],
            axis=dim,
        )
    return cells


def with_halo_2(shard, sides, width):
    edges = {}
    for axis, dim in sides:
        count, length = (lax.axis_size(axis), shard.shape[dim])
        up = [(i, (i + 1) % count) for i in range(count)]
        last = lax.slice_in_dim(shard, length - width, length, axis=dim)
        first = lax.slice_in_dim(shard, 0, width, axis=dim)
        edges[dim] = (
            lax.ppermute(last, axis, up),
            lax.ppermute(first, axis, [(b, a) for a, b in up]),
        )
    done = []
    for _, dim in sides:
        low, high = edges[dim]
        around = [(width, width) if d in done else (0, 0) for d in range(shard.ndim)]
        shard = jnp.concatenate([jnp.pad(low, around), shard, jnp.pad(high, around)], axis=dim)
        done.append(dim)
    return shard


def moment(values, lattice):
    link_table = jnp.asarray(lattice, jnp.float32)
    return jnp.tensordot(link_table.T, values, axes=1, precision=lax.Precision.HIGHEST)


def equilibrium(density, velocity, lattice, weights, linear, quadratic, square_term):
    link_table = jnp.asarray(lattice, jnp.float32)
    projected = jnp.tensordot(link_table, velocity, axes=1, precision=lax.Precision.HIGHEST)
    speed = jnp.sum(velocity * velocity, 0)
    scaled = jnp.asarray(weights, jnp.float32)[:, None, None, None]
    return (
        scaled
        * density
        * (1.0 + linear * projected + quadratic * projected * projected - square_term * speed)
    )


def lookup(mineral_ids, values_table):
    kinds = jnp.arange(values_table.shape[0], dtype=jnp.int32)[:, None, None, None]
    return jnp.sum(jnp.where(mineral_ids[None] == kinds, values_table[:, None, None, None], 0.0), 0)


def neighbour(padded, shift_z, shift_y, shift_x, depth_cells, width_cells):
    window = lax.slice_in_dim(padded, 1 - shift_z, 1 - shift_z + depth_cells, axis=0)
    window = lax.slice_in_dim(window, 1 - shift_y, 1 - shift_y + width_cells, axis=1)
    return jnp.roll(window, shift_x, axis=2)


def on_device(populations, solute, pore_mask, mineral_ids, reaction_rates, saturation):
    depth_cells, width_cells = (pore_mask.shape[0], pore_mask.shape[1])
    mask_cycle = with_halo(pore_mask, (("gz", 0), ("gy", 1)), 1)
    row_index = lax.axis_index("gy")
    row_total = lax.axis_size("gy")
    row_ids = lax.broadcasted_iota(jnp.int32, mask_cycle.shape, 1)
    walled = (row_ids == 0) & (row_index == 0) | (row_ids == width_cells + 1) & (
        row_index == row_total - 1
    )
    mask_cycle = jnp.where(walled, 0, mask_cycle)
    sources = []
    for direction in range(19):
        shift_z, shift_y, shift_x = (int(v) for v in LINKS19[direction])
        sources.append(neighbour(mask_cycle, shift_z, shift_y, shift_x, depth_cells, width_cells))
    density = jnp.sum(populations, 0)
    velocity = moment(populations, LINKS19) / density
    balanced = equilibrium(density, velocity, LINKS19, WEIGHTS19, 3.0, 4.5, 1.5)
    relaxed = populations - (populations - balanced) / RELAX_FLOW
    arrived = []
    padded = with_halo(relaxed, (("gz", 1), ("gy", 2)), 1)
    for direction in range(19):
        shift_z, shift_y, shift_x = (int(v) for v in LINKS19[direction])
        arrived.append(
            neighbour(padded[direction], shift_z, shift_y, shift_x, depth_cells, width_cells)
        )
    passed = jnp.stack(
        [jnp.where(sources[d] == 0, relaxed[REVERSE19[d]], arrived[d]) for d in range(19)]
    )
    flow_next = jnp.where(pore_mask[None] == 0, populations, passed)
    density_next = jnp.sum(flow_next, 0)
    velocity_next = jnp.where(pore_mask[None] > 0, moment(flow_next, LINKS19) / density_next, 0.0)
    concentration = jnp.sum(solute, 0)
    rate_cell = lookup(mineral_ids, reaction_rates)
    target = lookup(mineral_ids, saturation)
    reaction = jnp.where(pore_mask == 2, -rate_cell * (concentration - target), 0.0)
    solute_balanced = equilibrium(
        concentration, velocity_next, LINKS19[:7], WEIGHTS7, 4.0, 0.0, 0.0
    )
    weights = jnp.asarray(WEIGHTS7, jnp.float32)[:, None, None, None]
    solute_relaxed = solute - (solute - solute_balanced) / RELAX_SOLUTE + weights * reaction
    solute_pulled = []
    solute_padded = with_halo_2(solute_relaxed, (("gz", 1), ("gy", 2)), 1)
    for direction in range(7):
        shift_z, shift_y, shift_x = (int(v) for v in LINKS19[direction])
        solute_pulled.append(
            neighbour(solute_padded[direction], shift_z, shift_y, shift_x, depth_cells, width_cells)
        )
    solute_moved = [
        jnp.where(sources[d] == 0, solute_relaxed[REVERSE19[d]], solute_pulled[d]) for d in range(7)
    ]
    solute_next = jnp.where(pore_mask[None] == 0, solute, jnp.stack(solute_moved))
    return (flow_next, solute_next)


def solution(mesh):
    return jax.shard_map(
        on_device,
        mesh=mesh,
        in_specs=(
            P(None, "gz", "gy", None),
            P(None, "gz", "gy", None),
            P("gz", "gy", None),
            P("gz", "gy", None),
            P(),
            P(),
        ),
        out_specs=(P(None, "gz", "gy", None), P(None, "gz", "gy", None)),
        check_vma=False,
    )
```

profile of v0, /device:TPU:1, one launch (start us, length us, event | category | flops | bytes accessed | tf_op | source)
XLA Modules:
  0.0 81.6 jit_solution(146000905043192340)
XLA Ops:
  0.6 0.0 copy-start.9
  0.7 1.5 %reduce_sum.63 = f32[3,48,128]{2,1,0:T(8,128)S(1)} reduce(f32[19,3,48,128]{3,2,1,0:T(8,128)} %param.13, f32[]{:T(128)} %constant.21.clone.1), dimensions={0}, to_apply=%region_0.1 | reduce | flops 331776 | bytes 1474564 | tf_op jit(solution)/shard_map/reduce_sum | solution.py:115
  2.2 0.2 copy-done
  2.4 1.5 %multiply_reduce_fusion.1 = (f32[3,48,128]{2,1,0:T(8,128)S(1)}, f32[3,3,48,128]{3,0,2,1:T(4,128)S(1)}) fusion(f32[3,48,128]{2,1,0:T(8,128)S(1)} %reduce_sum.63, f32[19,3,1,1]{0,1,3,2:T(4,128)S(1)} %copy-done.9, f32[19,3,48,128]{3,2,1,0:T(8,128)S(1)} %copy-done), kind=kOutput, calls=%fused_computation.32 | convolution fusion | flops 12754944 | bytes 1769700 | tf_op jit(solution)/shard_map/dot_general | solution.py:75
  3.9 0.0 copy-start.12
  3.9 1.6 %fusion.76 = f32[19,3,48,128]{3,0,2,1:T(8,128)S(1)} fusion(f32[19,3,1,1]{0,1,3,2:T(4,128)S(1)} %copy-done.9, f32[3,3,48,128]{3,0,2,1:T(4,128)S(1)} %get-tuple-element.90), kind=kOutput, calls=%fused_computation.226 | convolution fusion | flops 12607488 | bytes 1622244 | tf_op jit(solution)/shard_map/dot_general | solution.py:80
  5.6 0.6 fusion.9
  6.2 0.0 copy-start.4
  6.2 0.0 copy-start.10
  6.2 0.8 %fusion.71 = (f32[19,1,48,128]{3,2,1,0:T(8,128)S(1)}, f32[19,1,48,128]{3,2,1,0:T(8,128)}) fusion(f32[19,3,48,128]{3,2,1,0:T(8,128)S(1)} %fusion.9), kind=kLoop, calls=%fused_computation.221 | loop fusion | bytes 1867776 | tf_op jit(solution)/shard_map/slice | solution.py:41
  7.0 12.4 %collective-permute-start.5 = (f32[19,1,48,128]{3,2,1,0:T(8,128)}, f32[19,1,48,128]{3,2,1,0:T(8,128)S(1)}, u32[]{:S(2)}, u32[]{:S(2)}) collective-permute-start(f32[19,1,48,128]{3,2,1,0:T(8,128)} %get-tuple-element.51), channel_id=1, source_target_pairs={{8,0},{16,8},{24,16},{32,24},{40,32},{48,40},{56,48},{64,56},{72,6... | collective-permute-start | bytes 1400840 | tf_op jit(solution)/shard_map/ppermute | solution.py:46
  19.4 1.9 %collective-permute-start.4 = (f32[19,1,48,128]{3,2,1,0:T(8,128)S(1)}, f32[19,1,48,128]{3,2,1,0:T(8,128)S(1)}, u32[]{:S(2)}, u32[]{:S(2)}) collective-permute-start(f32[19,1,48,128]{3,2,1,0:T(8,128)S(1)} %get-tuple-element.50), channel_id=1, source_target_pairs={{0,8},{8,16},{16,24},{24,32},{32,40},{40,48},{48,56},{56,64},{64,7... | collective-permute-start | bytes 1400840 | tf_op jit(solution)/shard_map/ppermute | solution.py:44
  21.4 0.6 fusion.75
  22.0 1.9 %collective-permute-start = (s32[1,48,128]{2,1,0:T(8,128)}, s32[1,48,128]{2,1,0:T(8,128)}, u32[]{:S(2)}, u32[]{:S(2)}) collective-permute-start(s32[1,48,128]{2,1,0:T(8,128)} %get-tuple-element.88), channel_id=1, source_target_pairs={{0,8},{8,16},{16,24},{24,32},{32,40},{40,48},{48,56},{56,64},{64,7... | collective-permute-start | bytes 73736 | tf_op jit(solution)/shard_map/ppermute | solution.py:44
  23.9 7.2 %collective-permute-start.1 = (s32[1,48,128]{2,1,0:T(8,128)}, s32[1,48,128]{2,1,0:T(8,128)}, u32[]{:S(2)}, u32[]{:S(2)}) collective-permute-start(s32[1,48,128]{2,1,0:T(8,128)} %get-tuple-element.87), channel_id=1, source_target_pairs={{8,0},{16,8},{24,16},{32,24},{40,32},{48,40},{56,48},{64,56},{72,6... | collective-permute-start | bytes 73736 | tf_op jit(solution)/shard_map/ppermute | solution.py:46
  31.2 0.2 select_reduce_fusion.1
  31.4 0.6 broadcast_compare_fusion
  32.1 0.7 constant_dynamic-update-slice_fusion.2
  32.8 0.7 constant_dynamic-update-slice_fusion
  33.6 5.1 %collective-permute-start.3 = (s32[5,1,128]{2,1,0:T(1,128)S(1)}, s32[5,1,128]{2,1,0:T(1,128)S(1)}, u32[]{:S(2)}, u32[]{:S(2)}) collective-permute-start(s32[5,1,128]{2,1,0:T(1,128)S(1)} %get-tuple-element.84), channel_id=1, source_target_pairs={{1,0},{2,1},{3,2},{4,3},{5,4},{6,5},{7,6},{0,7},{9,8},{10,9},{11,1... | collective-permute-start | bytes 7688 | tf_op jit(solution)/shard_map/ppermute | solution.py:46
  38.7 1.9 %collective-permute-start.2 = (s32[5,1,128]{2,1,0:T(1,128)S(1)}, s32[5,1,128]{2,1,0:T(1,128)S(1)}, u32[]{:S(2)}, u32[]{:S(2)}) collective-permute-start(s32[5,1,128]{2,1,0:T(1,128)S(1)} %get-tuple-element.83), channel_id=1, source_target_pairs={{0,1},{1,2},{2,3},{3,4},{4,5},{5,6},{6,7},{7,0},{8,9},{9,10},{10,1... | collective-permute-start | bytes 7688 | tf_op jit(solution)/shard_map/ppermute | solution.py:44
  40.6 3.6 %collective-permute-done.2 = s32[5,1,128]{2,1,0:T(1,128)S(1)} collective-permute-done((s32[5,1,128]{2,1,0:T(1,128)S(1)}, s32[5,1,128]{2,1,0:T(1,128)S(1)}, u32[]{:S(2)}, u32[]{:S(2)}) %collective-permute-start.2) | collective-permute-done | bytes 2592 | tf_op jit(solution)/shard_map/ppermute | solution.py:44
  44.2 0.1 add_select_fusion
  44.3 0.2 slice_bitcast_fusion.18
  44.5 0.1 pad_maximum_fusion.6
  44.6 1.9 %collective-permute-start.7 = (f32[19,5,1,128]{3,2,1,0:T(1,128)S(1)}, f32[19,5,1,128]{3,2,1,0:T(1,128)S(1)}, u32[]{:S(2)}, u32[]{:S(2)}) collective-permute-start(f32[19,5,1,128]{3,2,1,0:T(1,128)S(1)} %get-tuple-element.49), channel_id=1, source_target_pairs={{1,0},{2,1},{3,2},{4,3},{5,4},{6,5},{7,6},{0,7},{9,8},{10,9},{11,1... | collective-permute-start | bytes 145928 | tf_op jit(solution)/shard_map/ppermute | solution.py:46
  46.5 3.4 %collective-permute-start.6 = (f32[19,5,1,128]{3,2,1,0:T(1,128)S(1)}, f32[19,5,1,128]{3,2,1,0:T(1,128)S(1)}, u32[]{:S(2)}, u32[]{:S(2)}) collective-permute-start(f32[19,5,1,128]{3,2,1,0:T(1,128)S(1)} %get-tuple-element.48), channel_id=1, source_target_pairs={{0,1},{1,2},{2,3},{3,4},{4,5},{5,6},{6,7},{7,0},{8,9},{9,10},{10,1... | collective-permute-start | bytes 145928 | tf_op jit(solution)/shard_map/ppermute | solution.py:44
  49.9 0.2 slice_bitcast_fusion.19
  50.1 2.5 %collective-permute-done.6 = f32[19,5,1,128]{3,2,1,0:T(1,128)S(1)} collective-permute-done((f32[19,5,1,128]{3,2,1,0:T(1,128)S(1)}, f32[19,5,1,128]{3,2,1,0:T(1,128)S(1)}, u32[]{:S(2)}, u32[]{:S(2)}) %collective-permute-start.6) | collective-permute-done | bytes 48672 | tf_op jit(solution)/shard_map/ppermute | solution.py:44
  52.6 0.1 slice_bitcast_fusion.53
  52.7 0.1 slice_bitcast_fusion.52
  52.8 0.1 slice_bitcast_fusion.41
  52.9 0.1 slice_bitcast_fusion.40
  53.0 0.1 slice_bitcast_fusion.37
  53.1 0.1 slice_bitcast_fusion.29
  53.3 0.1 slice_bitcast_fusion.21
  53.4 0.1 slice_bitcast_fusion.17
  53.8 0.1 fusion.59
  53.9 0.1 fusion.58
  54.1 0.1 fusion.49
  54.2 0.1 fusion.48
  54.4 0.1 fusion.47
  54.5 0.1 fusion.46
  54.6 0.1 fusion.45
  54.7 0.1 fusion.44
  54.8 0.1 fusion.43
  54.9 0.1 fusion.42
  55.1 0.6 copy-done.1
  55.7 0.3 fusion.70
  56.0 0.5 copy-done.7
  56.4 1.9 %multiply_reduce_fusion = (f32[3,48,128]{2,1,0:T(8,128)S(1)}, f32[3,3,48,128]{3,0,2,1:T(4,128)S(1)}) fusion(f32[3,48,128]{2,1,0:T(8,128)S(1)} %get-tuple-element.14, f32[19,3,1,1]{0,1,3,2:T(4,128)S(1)} %copy-done.9, f32[19,3,48,128]{3,2,1,0:T(8,128)S(1)} %get-tuple-element.15, pred[3,48,128]{2,1,0:T(8,128)(4,1)S(1)} %copy-done.7), kind=kOutput, calls=%fused_computation.31 | convolution fusion | flops 12810240 | bytes 1788132 | tf_op jit(solution)/shard_map/dot_general | solution.py:75
  58.3 0.8 fusion.77
  59.1 0.3 fusion.28
  59.4 10.9 %collective-permute-start.10 = (f32[7,1,48,128]{3,2,1,0:T(8,128)S(1)}, f32[7,1,48,128]{3,2,1,0:T(8,128)S(1)}, u32[]{:S(2)}, u32[]{:S(2)}) collective-permute-start(f32[7,1,48,128]{3,2,1,0:T(8,128)S(1)} %get-tuple-element.60), channel_id=1, source_target_pairs={{8,0},{16,8},{24,16},{32,24},{40,32},{48,40},{56,48},{64,56},{72,6... | collective-permute-start | bytes 516104 | tf_op jit(solution)/shard_map/ppermute | solution.py:62
  70.3 1.9 %collective-permute-start.9 = (f32[7,1,48,128]{3,2,1,0:T(8,128)S(1)}, f32[7,1,48,128]{3,2,1,0:T(8,128)S(1)}, u32[]{:S(2)}, u32[]{:S(2)}) collective-permute-start(f32[7,1,48,128]{3,2,1,0:T(8,128)S(1)} %get-tuple-element.59), channel_id=1, source_target_pairs={{0,8},{8,16},{16,24},{24,32},{32,40},{40,48},{48,56},{56,64},{64,7... | collective-permute-start | bytes 516104 | tf_op jit(solution)/shard_map/ppermute | solution.py:61
  72.2 1.9 %collective-permute-start.11 = (f32[7,3,1,128]{3,2,1,0:T(1,128)S(1)}, f32[7,3,1,128]{3,2,1,0:T(1,128)S(1)}, u32[]{:S(2)}, u32[]{:S(2)}) collective-permute-start(f32[7,3,1,128]{3,2,1,0:T(1,128)S(1)} %get-tuple-element.62), channel_id=1, source_target_pairs={{1,0},{2,1},{3,2},{4,3},{5,4},{6,5},{7,6},{0,7},{9,8},{10,9},{11,1... | collective-permute-start | bytes 32264 | tf_op jit(solution)/shard_map/ppermute | solution.py:62
  74.2 3.4 %collective-permute-start.8 = (f32[7,3,1,128]{3,2,1,0:T(1,128)S(1)}, f32[7,3,1,128]{3,2,1,0:T(1,128)S(1)}, u32[]{:S(2)}, u32[]{:S(2)}) collective-permute-start(f32[7,3,1,128]{3,2,1,0:T(1,128)S(1)} %get-tuple-element.61), channel_id=1, source_target_pairs={{0,1},{1,2},{2,3},{3,4},{4,5},{5,6},{6,7},{7,0},{8,9},{9,10},{10,1... | collective-permute-start | bytes 32264 | tf_op jit(solution)/shard_map/ppermute | solution.py:61
  77.5 2.5 %collective-permute-done.8 = f32[7,3,1,128]{3,2,1,0:T(1,128)S(1)} collective-permute-done((f32[7,3,1,128]{3,2,1,0:T(1,128)S(1)}, f32[7,3,1,128]{3,2,1,0:T(1,128)S(1)}, u32[]{:S(2)}, u32[]{:S(2)}) %collective-permute-start.8) | collective-permute-done | bytes 10784 | tf_op jit(solution)/shard_map/ppermute | solution.py:61
  80.1 0.1 select_maximum_fusion
  80.3 0.1 slice_bitcast_fusion.10
  80.4 0.1 slice_bitcast_fusion.8
  80.6 0.1 fusion.31
  80.7 0.1 fusion.30
  80.8 0.8 %broadcast_select_fusion.1 = f32[7,3,48,128]{3,2,1,0:T(8,128)} fusion(f32[7,3,48,128]{3,2,1,0:T(8,128)S(1)} %copy-done.2, f32[7,3,48,128]{3,2,1,0:T(8,128)S(1)} %fusion.30, pred[3,48,128]{2,1,0:T(8,128)(4,1)S(1)} %copy-done.5), kind=kLoop, calls=%fused_computation.33 | loop fusion | flops 129024 | bytes 1566720 | tf_op jit(solution)/shard_map/jit(_where)/select_n | solution.py:151
  (67 shorter events, 0.9 us)
Async XLA Ops:
  0.6 1.6 %copy-start.9 = (f32[19,3,1,1]{0,1,3,2:T(4,128)S(1)}, f32[19,3,1,1]{0,1,3,2:T(4,128)}, u32[]{:S(2)}) copy-start(f32[19,3,1,1]{0,1,3,2:T(4,128)} %constant.57) | copy-start | bytes 688
  0.6 1.8 %copy-start = (f32[19,3,48,128]{3,2,1,0:T(8,128)S(1)}, f32[19,3,48,128]{3,2,1,0:T(8,128)}, u32[]{:S(2)}) copy-start(f32[19,3,48,128]{3,2,1,0:T(8,128)} %param.13) | copy-start | bytes 4202500
  3.9 1.7 %copy-start.12 = (f32[19]{0:T(128)S(1)}, f32[19]{0:T(128)}, u32[]{:S(2)}) copy-start(f32[19]{0:T(128)} %constant.15.clone) | copy-start | bytes 232
  6.2 15.2 %copy-start.4 = (s32[3,48,128]{2,1,0:T(8,128)S(1)}, s32[3,48,128]{2,1,0:T(8,128)}, u32[]{:S(2)}) copy-start(s32[3,48,128]{2,1,0:T(8,128)} %param.15) | copy-start | bytes 221188
  6.2 25.0 %copy-start.2 = (f32[7,3,48,128]{3,2,1,0:T(8,128)S(1)}, f32[7,3,48,128]{3,2,1,0:T(8,128)}, u32[]{:S(2)}) copy-start(f32[7,3,48,128]{3,2,1,0:T(8,128)} %param.14) | copy-start | bytes 1548292
  6.2 25.0 %copy-start.6 = (s32[3,48,128]{2,1,0:T(8,128)S(1)}, s32[3,48,128]{2,1,0:T(8,128)}, u32[]{:S(2)}) copy-start(s32[3,48,128]{2,1,0:T(8,128)} %param.16) | copy-start | bytes 221188
  6.2 25.0 %copy-start.10 = (f32[8]{0:T(128)S(1)}, f32[8]{0:T(128)}, u32[]{:S(2)}) copy-start(f32[8]{0:T(128)} %param.17) | copy-start | bytes 100
  6.2 25.0 %copy-start.11 = (f32[8]{0:T(128)S(1)}, f32[8]{0:T(128)}, u32[]{:S(2)}) copy-start(f32[8]{0:T(128)} %param.18) | copy-start | bytes 100
  7.0 37.4 %collective-permute-start.5 = (f32[19,1,48,128]{3,2,1,0:T(8,128)}, f32[19,1,48,128]{3,2,1,0:T(8,128)S(1)}, u32[]{:S(2)}, u32[]{:S(2)}) collective-permute-start(f32[19,1,48,128]{3,2,1,0:T(8,128)} %get-tuple-element.51), channel_id=1, source_target_pairs={{8,0},{16,8},{24,16},{32,24},{40,32},{48,40},{56,48},{64,56},{72,6... | collective-permute-start | bytes 1400840 | tf_op jit(solution)/shard_map/ppermute | solution.py:46
  19.4 25.1 %collective-permute-start.4 = (f32[19,1,48,128]{3,2,1,0:T(8,128)S(1)}, f32[19,1,48,128]{3,2,1,0:T(8,128)S(1)}, u32[]{:S(2)}, u32[]{:S(2)}) collective-permute-start(f32[19,1,48,128]{3,2,1,0:T(8,128)S(1)} %get-tuple-element.50), channel_id=1, source_target_pairs={{0,8},{8,16},{16,24},{24,32},{32,40},{40,48},{48,56},{56,64},{64,7... | collective-permute-start | bytes 1400840 | tf_op jit(solution)/shard_map/ppermute | solution.py:44
  22.0 10.1 %collective-permute-start = (s32[1,48,128]{2,1,0:T(8,128)}, s32[1,48,128]{2,1,0:T(8,128)}, u32[]{:S(2)}, u32[]{:S(2)}) collective-permute-start(s32[1,48,128]{2,1,0:T(8,128)} %get-tuple-element.88), channel_id=1, source_target_pairs={{0,8},{8,16},{16,24},{24,32},{32,40},{40,48},{48,56},{56,64},{64,7... | collective-permute-start | bytes 73736 | tf_op jit(solution)/shard_map/ppermute | solution.py:44
  23.9 8.9 %collective-permute-start.1 = (s32[1,48,128]{2,1,0:T(8,128)}, s32[1,48,128]{2,1,0:T(8,128)}, u32[]{:S(2)}, u32[]{:S(2)}) collective-permute-start(s32[1,48,128]{2,1,0:T(8,128)} %get-tuple-element.87), channel_id=1, source_target_pairs={{8,0},{16,8},{24,16},{32,24},{40,32},{48,40},{56,48},{64,56},{72,6... | collective-permute-start | bytes 73736 | tf_op jit(solution)/shard_map/ppermute | solution.py:46
  33.6 7.0 %collective-permute-start.3 = (s32[5,1,128]{2,1,0:T(1,128)S(1)}, s32[5,1,128]{2,1,0:T(1,128)S(1)}, u32[]{:S(2)}, u32[]{:S(2)}) collective-permute-start(s32[5,1,128]{2,1,0:T(1,128)S(1)} %get-tuple-element.84), channel_id=1, source_target_pairs={{1,0},{2,1},{3,2},{4,3},{5,4},{6,5},{7,6},{0,7},{9,8},{10,9},{11,1... | collective-permute-start | bytes 7688 | tf_op jit(solution)/shard_map/ppermute | solution.py:46
  38.7 5.5 %collective-permute-start.2 = (s32[5,1,128]{2,1,0:T(1,128)S(1)}, s32[5,1,128]{2,1,0:T(1,128)S(1)}, u32[]{:S(2)}, u32[]{:S(2)}) collective-permute-start(s32[5,1,128]{2,1,0:T(1,128)S(1)} %get-tuple-element.83), channel_id=1, source_target_pairs={{0,1},{1,2},{2,3},{3,4},{4,5},{5,6},{6,7},{7,0},{8,9},{9,10},{10,1... | collective-permute-start | bytes 7688 | tf_op jit(solution)/shard_map/ppermute | solution.py:44
  44.6 5.5 %collective-permute-start.7 = (f32[19,5,1,128]{3,2,1,0:T(1,128)S(1)}, f32[19,5,1,128]{3,2,1,0:T(1,128)S(1)}, u32[]{:S(2)}, u32[]{:S(2)}) collective-permute-start(f32[19,5,1,128]{3,2,1,0:T(1,128)S(1)} %get-tuple-element.49), channel_id=1, source_target_pairs={{1,0},{2,1},{3,2},{4,3},{5,4},{6,5},{7,6},{0,7},{9,8},{10,9},{11,1... | collective-permute-start | bytes 145928 | tf_op jit(solution)/shard_map/ppermute | solution.py:46
  46.5 6.0 %collective-permute-start.6 = (f32[19,5,1,128]{3,2,1,0:T(1,128)S(1)}, f32[19,5,1,128]{3,2,1,0:T(1,128)S(1)}, u32[]{:S(2)}, u32[]{:S(2)}) collective-permute-start(f32[19,5,1,128]{3,2,1,0:T(1,128)S(1)} %get-tuple-element.48), channel_id=1, source_target_pairs={{0,1},{1,2},{2,3},{3,4},{4,5},{5,6},{6,7},{7,0},{8,9},{9,10},{10,1... | collective-permute-start | bytes 145928 | tf_op jit(solution)/shard_map/ppermute | solution.py:44
  54.4 1.4 %copy-start.1 = (f32[19,3,48,128]{3,2,1,0:T(8,128)S(1)}, f32[19,3,48,128]{3,2,1,0:T(8,128)}, u32[]{:S(2)}) copy-start(f32[19,3,48,128]{3,2,1,0:T(8,128)} %param.13) | copy-start | bytes 4202500
  54.4 1.3 %copy-start.5 = (pred[3,48,128]{2,1,0:T(8,128)(4,1)S(1)}, pred[3,48,128]{2,1,0:T(8,128)(4,1)}, u32[]{:S(2)}) copy-start(pred[3,48,128]{2,1,0:T(8,128)(4,1)} %get-tuple-element.86) | copy-start | bytes 55300
  55.7 0.7 copy-start.7
  56.0 2.3 %copy-start.3 = (f32[19,3,48,128]{3,2,1,0:T(8,128)}, f32[19,3,48,128]{3,2,1,0:T(8,128)S(1)}, u32[]{:S(2)}) copy-start(f32[19,3,48,128]{3,2,1,0:T(8,128)S(1)} %get-tuple-element.15) | copy-start | bytes 4202500
  56.4 1.9 %copy-start.8 = (f32[7,3,1,1]{0,1,3,2:T(4,128)S(1)}, f32[7,3,1,1]{0,1,3,2:T(4,128)}, u32[]{:S(2)}) copy-start(f32[7,3,1,1]{0,1,3,2:T(4,128)} %constant.58) | copy-start | bytes 256
  56.4 2.7 %copy-start.13 = (f32[7]{0:T(128)S(1)}, f32[7]{0:T(128)}, u32[]{:S(2)}) copy-start(f32[7]{0:T(128)} %constant.48.clone) | copy-start | bytes 88
  59.4 20.7 %collective-permute-start.10 = (f32[7,1,48,128]{3,2,1,0:T(8,128)S(1)}, f32[7,1,48,128]{3,2,1,0:T(8,128)S(1)}, u32[]{:S(2)}, u32[]{:S(2)}) collective-permute-start(f32[7,1,48,128]{3,2,1,0:T(8,128)S(1)} %get-tuple-element.60), channel_id=1, source_target_pairs={{8,0},{16,8},{24,16},{32,24},{40,32},{48,40},{56,48},{64,56},{72,6... | collective-permute-start | bytes 516104 | tf_op jit(solution)/shard_map/ppermute | solution.py:62
  70.3 9.8 %collective-permute-start.9 = (f32[7,1,48,128]{3,2,1,0:T(8,128)S(1)}, f32[7,1,48,128]{3,2,1,0:T(8,128)S(1)}, u32[]{:S(2)}, u32[]{:S(2)}) collective-permute-start(f32[7,1,48,128]{3,2,1,0:T(8,128)S(1)} %get-tuple-element.59), channel_id=1, source_target_pairs={{0,8},{8,16},{16,24},{24,32},{32,40},{40,48},{48,56},{56,64},{64,7... | collective-permute-start | bytes 516104 | tf_op jit(solution)/shard_map/ppermute | solution.py:61
  72.2 5.3 %collective-permute-start.11 = (f32[7,3,1,128]{3,2,1,0:T(1,128)S(1)}, f32[7,3,1,128]{3,2,1,0:T(1,128)S(1)}, u32[]{:S(2)}, u32[]{:S(2)}) collective-permute-start(f32[7,3,1,128]{3,2,1,0:T(1,128)S(1)} %get-tuple-element.62), channel_id=1, source_target_pairs={{1,0},{2,1},{3,2},{4,3},{5,4},{6,5},{7,6},{0,7},{9,8},{10,9},{11,1... | collective-permute-start | bytes 32264 | tf_op jit(solution)/shard_map/ppermute | solution.py:62
  74.2 5.9 %collective-permute-start.8 = (f32[7,3,1,128]{3,2,1,0:T(1,128)S(1)}, f32[7,3,1,128]{3,2,1,0:T(1,128)S(1)}, u32[]{:S(2)}, u32[]{:S(2)}) collective-permute-start(f32[7,3,1,128]{3,2,1,0:T(1,128)S(1)} %get-tuple-element.61), channel_id=1, source_target_pairs={{0,1},{1,2},{2,3},{3,4},{4,5},{5,6},{6,7},{7,0},{8,9},{9,10},{10,1... | collective-permute-start | bytes 32264 | tf_op jit(solution)/shard_map/ppermute | solution.py:61
where the time goes:
time: 82.3 us; the launch traced here: 81.6 us
  starting transfers between devices  53.8 us (65%)
  waiting for transfers between devices  8.65 us (11%)
  other arithmetic  6.42 us (8%)
  matrix products  5.73 us (7%)
  local copies, waits for them, and re-layouts  5.68 us (7%)
  between operations  1.33 us (2%)
    ppermute x4, starting transfers between devices, with_halo(): lax.ppermute(head, axis, [((i + 1) % count, i) for i in range(count)])  26.6 us
    ppermute x2, starting transfers between devices, with_halo_2(): lax.ppermute(first, axis, [(b, a) for a, b in up])  12.8 us
    ppermute x4, starting transfers between devices, with_halo(): lax.ppermute(tail, axis, [(i, (i + 1) % count) for i in range(count)])  9.11 us
    ppermute x4, waiting for transfers between devices, with_halo(): lax.ppermute(tail, axis, [(i, (i + 1) % count) for i in range(count)])  6.09 us
    ppermute x2, starting transfers between devices, with_halo_2(): lax.ppermute(last, axis, up)  5.28 us
    dot_general x2, matrix products, moment(): jnp.tensordot(link_table.T, values, axes=1, precision=lax.Precision.HIGHEST)  3.35 us
    ppermute x2, waiting for transfers between devices, with_halo_2(): lax.ppermute(last, axis, up)  2.55 us
    dot_general x2, matrix products, equilibrium(): jnp.tensordot(link_table, velocity, axes=1, precision=lax.Precision.HIGHEST)  2.38 us
  transfers between devices with their start and end apart: 12, of which 3 were waited for; matrix products, arithmetic and copies ran while one was open for 4% of the time, Pallas kernels for 0%

commit v1 on v0

v1 whole, which is shorter than its diff:
```python
import functools

import jax
import jax.numpy as jnp
import numpy as np
from jax import lax
from jax.experimental import pallas as pl
from jax.experimental.pallas import tpu as pltpu
from jax.sharding import PartitionSpec as P

LINKS = (
    (0, 0, 0),
    (1, 0, 0),
    (-1, 0, 0),
    (0, 1, 0),
    (0, -1, 0),
    (0, 0, 1),
    (0, 0, -1),
    (1, 1, 0),
    (-1, -1, 0),
    (1, -1, 0),
    (-1, 1, 0),
    (1, 0, 1),
    (-1, 0, -1),
    (1, 0, -1),
    (-1, 0, 1),
    (0, 1, 1),
    (0, -1, -1),
    (0, 1, -1),
    (0, -1, 1),
)
REVERSE = (0, 2, 1, 4, 3, 6, 5, 8, 7, 10, 9, 12, 11, 14, 13, 16, 15, 18, 17)
W19 = (1.0 / 3.0,) + (1.0 / 18.0,) * 6 + (1.0 / 36.0,) * 12
W7 = (0.25,) + (0.125,) * 6
UP = tuple(q for q in range(19) if LINKS[q][0] == 1)
DOWN = tuple(q for q in range(19) if LINKS[q][0] == -1)
KEEP = 1.0 - 1.0 / 1.25
GAIN = 1.0 / 1.25
KEEP_S = 1.0 - 1.0 / 1.4
GAIN_S = 1.0 / 1.4
LX = 128
PAD = 8
MAX_VMEM = 16 * 1024 * 1024


def relax(p):
    d = {q: p[q] - p[q + 1] for q in range(1, 19, 2)}
    s = {q: p[q] + p[q + 1] for q in range(1, 19, 2)}
    density = p[0] + (
        ((s[1] + s[3]) + (s[5] + s[7])) + ((s[9] + s[11]) + (s[13] + s[15])) + s[17]
    )
    mz = (d[1] + d[7]) + (d[9] + d[11]) + d[13]
    my = (d[3] + d[7]) + (d[15] + d[17]) - d[9]
    mx = (d[5] + d[11]) + (d[15] - d[13]) - d[17]
    inverse = 1.0 / density
    uz, uy, ux = mz * inverse, my * inverse, mx * inverse
    rest = 1.0 - 1.5 * (uz * uz + uy * uy + ux * ux)
    out = [None] * 19
    scaled = {w: density * (GAIN * w) for w in set(W19)}
    out[0] = KEEP * p[0] + scaled[W19[0]] * rest
    along = {
        1: uz,
        3: uy,
        5: ux,
        7: uz + uy,
        9: uz - uy,
        11: uz + ux,
        13: uz - ux,
        15: uy + ux,
        17: uy - ux,
    }
    for q, e in along.items():
        w = scaled[W19[q]]
        even = w * (rest + 4.5 * (e * e))
        odd = w * (3.0 * e)
        out[q] = KEEP * p[q] + (even + odd)
        out[q + 1] = KEEP * p[q + 1] + (even - odd)
    return out


def solute_terms(s, pore, ids, rates_ref, target_ref):
    total = ((s[0] + s[1]) + (s[2] + s[3])) + ((s[4] + s[5]) + s[6])
    rate = jnp.full(total.shape, rates_ref[0], jnp.float32)
    target = jnp.full(total.shape, target_ref[0], jnp.float32)
    for k in range(1, rates_ref.shape[0]):
        rate = jnp.where(ids == k, rates_ref[k], rate)
        target = jnp.where(ids == k, target_ref[k], target)
    reaction = jnp.where(pore == 2, -rate * (total - target), 0.0)
    return total, reaction


def rolled(value, shift):
    return value if shift == 0 else pltpu.roll(value, shift % LX, axis=1)


def pack_edges(pop, sol, pore, ids, rates, target, up, down):
    width = pop.shape[2]
    for out, first, link, near in ((up, width - 2, 3, 1), (down, 0, 4, 0)):
        rows = slice(first, first + 2)
        for layer in range(3):
            into = slice(2 * layer, 2 * layer + 2)
            for q in range(19):
                out[q, into, :] = pop[q, layer, rows, :]
            kind = pore[layer, rows, :]
            out[19, into, :] = jnp.where(kind > 0, 1.0, 0.0)
            s = [sol[q, layer, rows, :] for q in range(7)]
            total, reaction = solute_terms(s, kind, ids[layer, rows, :], rates, target)
            w = W7[link]
            out[20, into, :] = KEEP_S * s[link] + (w * GAIN_S) * total + w * reaction
            out[21, into, :] = (4.0 * w * GAIN_S) * total
        out[:, 6:8, :] = jnp.zeros((22, 2, LX), jnp.float32)


def streamed(q, layer, row, count, shifted, plain, masks):
    ez, ey, ex = LINKS[q]
    value = shifted(q, layer - ez, row - ey, count)
    if q == 0:
        return value
    open_ = masks(ex, layer - ez, row - ey, count) > 0.0
    return jnp.where(open_, value, plain(REVERSE[q], layer, row, count))


def relax_kernel(
    pop, sol, pore, ids, rates, target, low, high, moved, kept, mask, up, down, edge
):
    width = pop.shape[2]
    tiles = width // 8
    for layer in range(3):
        for t in range(tiles):
            rows, into = slice(8 * t, 8 * t + 8), slice(PAD + 8 * t, PAD + 8 * t + 8)
            out = relax([pop[q, layer, rows, :] for q in range(19)])
            for q in range(19):
                ex = LINKS[q][2]
                moved[q, layer, into, :] = rolled(out[q], ex)
                if ex:
                    kept[q, layer, into, :] = out[q]
            m = jnp.where(pore[layer, rows, :] > 0, 1.0, 0.0)
            for ex in (0, 1, -1):
                mask[ex % 3, layer, into, :] = rolled(m, ex)
    for ref, at in ((low, PAD - 2), (high, PAD + width)):
        p = [ref[q] for q in range(19)]
        m = ref[19]
        p[0] = jnp.where(m > 0.0, p[0], p[0] + 1.0)
        out = relax(p)
        into = slice(at, at + 2)
        for q in range(19):
            ex = LINKS[q][2]
            edge[0, q] = rolled(out[q], ex)
            if ex:
                edge[1, q] = out[q]
        for ex in (0, 1, -1):
            edge[2, ex % 3] = rolled(m, ex)
        for layer in range(3):
            rows = slice(2 * layer, 2 * layer + 2)
            for q in range(19):
                moved[q, layer, into, :] = edge[0, q, rows, :]
                if LINKS[q][2]:
                    kept[q, layer, into, :] = edge[1, q, rows, :]
            for k in range(3):
                mask[k, layer, into, :] = edge[2, k, rows, :]

    def shifted(q, layer, row, count):
        return moved[q, layer, row : row + count, :]

    def plain(q, layer, row, count):
        return (kept if LINKS[q][2] else moved)[q, layer, row : row + count, :]

    def masks(ex, layer, row, count):
        return mask[ex % 3, layer, row : row + count, :]

    for out, layer, sign, cross, link in ((up, 2, 1, UP, 1), (down, 0, -1, DOWN, 2)):
        w = W7[link]
        for t in range(tiles):
            row = PAD + 8 * t
            get = functools.partial(
                streamed, layer=layer, row=row, count=8, shifted=shifted, plain=plain, masks=masks
            )
            away = functools.reduce(jnp.add, [get(q) for q in cross])
            level = functools.reduce(
                jnp.add, [get(q) for q in range(19) if LINKS[q][0] == 0]
            )
            partial = level + away
            rows = slice(8 * t, 8 * t + 8)
            s = [sol[q, layer, rows, :] for q in range(7)]
            total, reaction = solute_terms(
                s, pore[layer, rows, :], ids[layer, rows, :], rates, target
            )
            slope = (4.0 * w * GAIN_S) * total
            base = KEEP_S * s[link] + (w * GAIN_S) * total + w * reaction
            for k, q in enumerate(cross):
                out[k * width + 8 * t : k * width + 8 * t + 8, :] = plain(q, layer, row, 8)
            fields = (masks(0, layer, row, 8), base - slope, partial, slope * (partial + away))
            for k, v in enumerate(fields):
                at = (5 + k) * width + 8 * t
                out[at : at + 8, :] = v
        for k in range(6):
            for side, row in ((0, PAD - 2), (1, PAD + width)):
                at = 9 * width + 4 * k + 2 * side
                v = plain(cross[k], layer, row, 2) if k < 5 else masks(0, layer, row, 2)
                out[at : at + 2, :] = v


def stream_kernel(
    pop,
    sol,
    pore,
    ids,
    rates,
    target,
    low,
    high,
    moved,
    kept,
    mask,
    below,
    above,
    flow,
    solute,
    zmoved,
    zkept,
    zmask,
    plain_s,
    moved_s,
    cross_s,
):
    width = pop.shape[2]
    tiles = width // 8
    sides = ((0, below, UP), (1, above, DOWN))
    for side, ref, links in sides:
        for k in range(6):
            for lo, at in ((0, PAD - 2), (1, PAD + width)):
                src = 9 * width + 4 * k + 2 * lo
                v = ref[src : src + 2, :]
                if k < 5:
                    ex = LINKS[links[k]][2]
                    zmoved[side, k, at : at + 2, :] = rolled(v, ex)
                    if ex:
                        zkept[side, k, at : at + 2, :] = v
                else:
                    for ex in (0, 1, -1):
                        zmask[side, ex % 3, at : at + 2, :] = rolled(v, ex)
            for t in range(tiles):
                at = PAD + 8 * t
                v = ref[k * width + 8 * t : k * width + 8 * t + 8, :]
                if k < 5:
                    ex = LINKS[links[k]][2]
                    zmoved[side, k, at : at + 8, :] = rolled(v, ex)
                    if ex:
                        zkept[side, k, at : at + 8, :] = v
                else:
                    for ex in (0, 1, -1):
                        zmask[side, ex % 3, at : at + 8, :] = rolled(v, ex)

    def shifted(q, layer, row, count):
        if layer == -1:
            return zmoved[0, UP.index(q), row : row + count, :]
        if layer == 3:
            return zmoved[1, DOWN.index(q), row : row + count, :]
        return moved[q, layer, row : row + count, :]

    def plain(q, layer, row, count):
        if layer == -1:
            ref, k = (zkept if LINKS[q][2] else zmoved), UP.index(q)
            return ref[0, k, row : row + count, :]
        if layer == 3:
            ref, k = (zkept if LINKS[q][2] else zmoved), DOWN.index(q)
            return ref[1, k, row : row + count, :]
        return (kept if LINKS[q][2] else moved)[q, layer, row : row + count, :]

    def masks(ex, layer, row, count):
        if layer == -1:
            return zmask[0, ex % 3, row : row + count, :]
        if layer == 3:
            return zmask[1, ex % 3, row : row + count, :]
        return mask[ex % 3, layer, row : row + count, :]

    def sums(f):
        d = {q: f[q] - f[q + 1] for q in range(1, 19, 2)}
        s = {q: f[q] + f[q + 1] for q in range(1, 19, 2)}
        density = f[0] + (
            ((s[1] + s[3]) + (s[5] + s[7])) + ((s[9] + s[11]) + (s[13] + s[15])) + s[17]
        )
        mz = (d[1] + d[7]) + (d[9] + d[11]) + d[13]
        my = (d[3] + d[7]) + (d[15] + d[17]) - d[9]
        mx = (d[5] + d[11]) + (d[15] - d[13]) - d[17]
        return density, mz, my, mx

    def pull(layer, row, count):
        return [
            streamed(q, layer, row, count, shifted, plain, masks) for q in range(19)
        ]

    for side, ref, layer, links in ((0, below, 0, DOWN), (1, above, 2, UP)):
        outside = -1 if side == 0 else 3
        for t in range(tiles):
            row = PAD + 8 * t
            into = functools.reduce(
                jnp.add,
                [streamed(q, outside, row, 8, shifted, plain, masks) for q in links],
            )
            base, partial, weight = (
                ref[(6 + k) * width + 8 * t : (6 + k) * width + 8 * t + 8, :] for k in range(3)
            )
            cross_s[side, 8 * t : 8 * t + 8, :] = base + weight / (partial + into)
    for layer in range(3):
        for ref, row, near, link, sign, part in (
            (low, PAD - 1, 1, 3, 1.0, 1),
            (high, PAD + width, 0, 4, -1.0, 0),
        ):
            density, _, my, _ = sums(pull(layer, row, 1))
            at = 2 * layer + near
            plain_s[link, layer, row : row + 1, :] = ref[20, at : at + 1, :] + sign * (
                ref[21, at : at + 1, :] * (my / density)
            )
        for t in range(tiles):
            row, rows = PAD + 8 * t, slice(8 * t, 8 * t + 8)
            f = pull(layer, row, 8)
            kind = pore[layer, rows, :]
            rock = kind == 0
            for q in range(19):
                flow[q, layer, rows, :] = jnp.where(rock, pop[q, layer, rows, :], f[q])
            density, mz, my, mx = sums(f)
            inverse = jnp.where(rock, 0.0, 1.0 / density)
            s = [sol[q, layer, rows, :] for q in range(7)]
            total, reaction = solute_terms(s, kind, ids[layer, rows, :], rates, target)
            side_term = (W7[1] * GAIN_S) * total + W7[1] * reaction
            slope = (4.0 * W7[1] * GAIN_S) * total * inverse
            into = slice(row, row + 8)
            plain_s[0, layer, into, :] = (
                KEEP_S * s[0] + (W7[0] * GAIN_S) * total + W7[0] * reaction
            )
            for q, m in ((1, mz), (3, my), (5, mx)):
                plain_s[q, layer, into, :] = KEEP_S * s[q] + side_term + slope * m
                plain_s[q + 1, layer, into, :] = KEEP_S * s[q + 1] + side_term - slope * m
            for q in (5, 6):
                ex = LINKS[q][2]
                moved_s[q - 5, layer, into, :] = rolled(plain_s[q, layer, into, :], ex)
    for layer in range(3):
        for t in range(tiles):
            row, rows = PAD + 8 * t, slice(8 * t, 8 * t + 8)
            rock = pore[layer, rows, :] == 0
            for q in range(7):
                ez, ey, ex = LINKS[q]
                src = layer - ez
                if q == 0:
                    value = plain_s[0, layer, row : row + 8, :]
                else:
                    if src == -1:
                        value = cross_s[0, rows, :]
                    elif src == 3:
                        value = cross_s[1, rows, :]
                    elif ex:
                        value = moved_s[q - 5, layer, row : row + 8, :]
                    else:
                        value = plain_s[q, src, row - ey : row - ey + 8, :]
                    open_ = masks(ex, src, row - ey, 8) > 0.0
                    value = jnp.where(open_, value, plain_s[REVERSE[q], layer, row : row + 8, :])
                solute[q, layer, rows, :] = jnp.where(rock, sol[q, layer, rows, :], value)


VMEM = pl.BlockSpec(memory_space=pltpu.VMEM)
SMEM = pl.BlockSpec(memory_space=pltpu.SMEM)


def call(kernel, operands, specs, outs, scratch=(), flops=1_000_000):
    return pl.pallas_call(
        kernel,
        out_shape=[jax.ShapeDtypeStruct(s, jnp.float32) for s in outs],
        in_specs=list(specs),
        out_specs=[VMEM] * len(outs),
        scratch_shapes=[pltpu.VMEM(s, jnp.float32) for s in scratch],
        compiler_params=pltpu.CompilerParams(vmem_limit_bytes=MAX_VMEM),
        cost_estimate=pl.CostEstimate(flops=flops, bytes_accessed=1_000_000, transcendentals=0),
    )(*operands)


def on_device(populations, solute, pore_mask, mineral_ids, reaction_rates, saturation):
    width = pore_mask.shape[1]
    padded = width + 2 * PAD
    cells = (populations, solute, pore_mask, mineral_ids, reaction_rates, saturation)
    kinds = [VMEM] * 4 + [SMEM] * 2
    gz, gy = lax.axis_size("gz"), lax.axis_size("gy")
    edges = call(pack_edges, cells, kinds, [(22, 8, LX)] * 2)
    low = lax.ppermute(edges[0], "gy", [(i, i + 1) for i in range(gy - 1)])
    high = lax.ppermute(edges[1], "gy", [(i + 1, i) for i in range(gy - 1)])
    rows = 9 * width + 24
    moved, kept, mask, up, down = call(
        relax_kernel,
        cells + (low, high),
        kinds + [VMEM] * 2,
        [(19, 3, padded, LX), (19, 3, padded, LX), (3, 3, padded, LX), (rows, LX), (rows, LX)],
        [(3, 19, 8, LX)],
    )
    below = lax.ppermute(up, "gz", [(i, (i + 1) % gz) for i in range(gz)])
    above = lax.ppermute(down, "gz", [((i + 1) % gz, i) for i in range(gz)])
    return tuple(
        call(
            stream_kernel,
            cells + (low, high, moved, kept, mask, below, above),
            kinds + [VMEM] * 7,
            [populations.shape, solute.shape],
            [
                (2, 5, padded, LX),
                (2, 5, padded, LX),
                (2, 3, padded, LX),
                (7, 3, padded, LX),
                (2, 3, padded, LX),
                (2, width, LX),
            ],
        )
    )


def solution(mesh):
    cells = P(None, "gz", "gy", None)
    return jax.shard_map(
        on_device,
        mesh=mesh,
        in_specs=(cells, cells, P("gz", "gy", None), P("gz", "gy", None), P(), P()),
        out_specs=(cells, cells),
        check_vma=False,
    )
```

time: 82.3 us -> 43.8 us (0.53)
  the two profiles are of different devices: /device:TPU:1 before, /device:TPU:24 now
where the time goes in v1:
time: 43.8 us; the launch traced here: 43.4 us
  starting transfers between devices  23.3 us (53%)
  waiting for transfers between devices  9.27 us (21%)
  local copies, waits for them, and re-layouts  5.46 us (12%)
  Pallas kernels  4.66 us (11%)
  between operations  0.69 us (2%)
    ppermute x1, starting transfers between devices, on_device(): above = lax.ppermute(down, 'gz', [((i + 1) % gz, i) for i in range(gz)])  14.8 us
    ppermute x1, waiting for transfers between devices, on_device(): high = lax.ppermute(edges[1], 'gy', [(i + 1, i) for i in range(gy - 1)])  5.52 us
    unnamed x12, local copies, waits for them, and re-layouts  5.46 us
    ppermute x1, starting transfers between devices, on_device(): low = lax.ppermute(edges[0], 'gy', [(i, i + 1) for i in range(gy - 1)])  4.7 us
    pallas_call x3, Pallas kernels, call(): pl.pallas_call(kernel, out_shape=[jax.ShapeDtypeStruct(s, jnp.float32) fo...  4.66 us
    ppermute x1, starting transfers between devices, on_device(): high = lax.ppermute(edges[1], 'gy', [(i + 1, i) for i in range(gy - 1)])  1.92 us
    ppermute x1, starting transfers between devices, on_device(): below = lax.ppermute(up, 'gz', [(i, (i + 1) % gz) for i in range(gz)])  1.92 us
    ppermute x1, waiting for transfers between devices, on_device(): below = lax.ppermute(up, 'gz', [(i, (i + 1) % gz) for i in range(gz)])  1.81 us
  transfers between devices with their start and end apart: 4, of which 4 were waited for; matrix products, arithmetic and copies ran while one was open for 0% of the time, Pallas kernels for 0%

profile of v1, /device:TPU:24, one launch (start us, length us, event | category | flops | bytes accessed | tf_op | source)
XLA Modules:
  0.0 43.4 jit_solution(1313842847794434772)
XLA Ops:
  0.6 0.0 copy-start
  0.6 1.3 %copy-done = f32[19,3,48,128]{3,2,1,0:T(8,128)S(1)} copy-done((f32[19,3,48,128]{3,2,1,0:T(8,128)S(1)}, f32[19,3,48,128]{3,2,1,0:T(8,128)}, u32[]{:S(2)}) %copy-start) | copy-done | bytes 1400856
  2.0 0.0 copy-start.1
  2.0 1.0 %copy-done.1 = f32[7,3,48,128]{3,2,1,0:T(8,128)S(1)} copy-done((f32[7,3,48,128]{3,2,1,0:T(8,128)S(1)}, f32[7,3,48,128]{3,2,1,0:T(8,128)}, u32[]{:S(2)}) %copy-start.1) | copy-done | bytes 516120
  3.0 0.0 copy-start.2
  3.0 0.9 %copy-done.2 = s32[3,48,128]{2,1,0:T(8,128)S(1)} copy-done((s32[3,48,128]{2,1,0:T(8,128)S(1)}, s32[3,48,128]{2,1,0:T(8,128)}, u32[]{:S(2)}) %copy-start.2) | copy-done | bytes 73752
  3.9 0.0 copy-start.3
  3.9 0.9 %copy-done.3 = s32[3,48,128]{2,1,0:T(8,128)S(1)} copy-done((s32[3,48,128]{2,1,0:T(8,128)S(1)}, s32[3,48,128]{2,1,0:T(8,128)}, u32[]{:S(2)}) %copy-start.3) | copy-done | bytes 73752
  4.8 0.0 copy-start.4
  4.8 0.7 %copy-done.4 = f32[8]{0:T(128)S(1)} copy-done((f32[8]{0:T(128)S(1)}, f32[8]{0:T(128)}, u32[]{:S(2)}) %copy-start.4) | copy-done | bytes 56
  5.4 0.0 copy-start.5
  5.4 0.7 %copy-done.5 = f32[8]{0:T(128)S(1)} copy-done((f32[8]{0:T(128)S(1)}, f32[8]{0:T(128)}, u32[]{:S(2)}) %copy-start.5) | copy-done | bytes 56
  6.1 0.6 %shard_map.77 = (f32[22,8,128]{2,1,0:T(8,128)S(1)}, f32[22,8,128]{2,1,0:T(8,128)S(1)}) custom-call(f32[19,3,48,128]{3,2,1,0:T(8,128)S(1)} %copy-done, f32[7,3,48,128]{3,2,1,0:T(8,128)S(1)} %copy-done.1, s32[3,48,128]{2,1,0:T(8,128)S(1)} %copy-done.2, s32[3,48,128]{2,1,0:T(8,128)S(1)} %copy-done.3, f32[8]{0:T(128)S(1)} %copy-done.4, f32[8]{0:T(128)S(1)} %copy-done.5), custom_call_target="tpu_custom_call" | custom-call | flops 1000000 | bytes 1000000 | tf_op jit(solution)/shard_map/pallas_call | solution.py:366
  6.7 4.7 %collective-permute-start = (f32[22,8,128]{2,1,0:T(8,128)S(1)}, f32[22,8,128]{2,1,0:T(8,128)S(1)}, u32[]{:S(2)}, u32[]{:S(2)}) collective-permute-start(f32[22,8,128]{2,1,0:T(8,128)S(1)} %get-tuple-element.9), channel_id=1, source_target_pairs={{0,1},{1,2},{2,3},{3,4},{4,5},{5,6},{6,7},{8,9},{9,10},{10,11},{11... | collective-permute-start | bytes 270344 | tf_op jit(solution)/shard_map/ppermute | solution.py:384
  11.4 1.9 %collective-permute-start.1 = (f32[22,8,128]{2,1,0:T(8,128)S(1)}, f32[22,8,128]{2,1,0:T(8,128)S(1)}, u32[]{:S(2)}, u32[]{:S(2)}) collective-permute-start(f32[22,8,128]{2,1,0:T(8,128)S(1)} %get-tuple-element.10), channel_id=1, source_target_pairs={{1,0},{2,1},{3,2},{4,3},{5,4},{6,5},{7,6},{9,8},{10,9},{11,10},{12... | collective-permute-start | bytes 270344 | tf_op jit(solution)/shard_map/ppermute | solution.py:385
  13.4 0.2 collective-permute-done.low
  13.5 5.5 %collective-permute-done.1.high = f32[22,8,128]{2,1,0:T(8,128)S(1)} collective-permute-done((f32[22,8,128]{2,1,0:T(8,128)S(1)}, f32[22,8,128]{2,1,0:T(8,128)S(1)}, u32[]{:S(2)}, u32[]{:S(2)}) %collective-permute-start.1) | collective-permute-done | bytes 90144 | tf_op jit(solution)/shard_map/ppermute | solution.py:385
  19.1 1.4 %shard_map.78 = (f32[19,3,64,128]{3,2,1,0:T(8,128)S(1)}, f32[19,3,64,128]{3,2,1,0:T(8,128)S(1)}, f32[3,3,64,128]{3,2,1,0:T(8,128)S(1)}, f32[456,128]{1,0:T(8,128)S(1)}, f32[456,128]{1,0:T(8,128)S(1)}) custom-call(f32[19,3,48,128]{3,2,1,0:T(8,128)S(1)} %copy-done, f32[7,3,48,128]{3,2,1,0:T(8,128)S(1)} %copy-done.1, s32[3,48,128]{2,1,0:T(8,128)S(1)} %copy-done.2, ...), custom_call_target="tpu_custom_call" | custom-call | flops 1000000 | bytes 1000000 | tf_op jit(solution)/shard_map/pallas_call | solution.py:366
  20.5 1.9 %collective-permute-start.2 = (f32[456,128]{1,0:T(8,128)S(1)}, f32[456,128]{1,0:T(8,128)S(1)}, u32[]{:S(2)}, u32[]{:S(2)}) collective-permute-start(f32[456,128]{1,0:T(8,128)S(1)} %get-tuple-element.14), channel_id=1, source_target_pairs={{0,8},{8,16},{16,24},{24,32},{32,40},{40,48},{48,56},{56,64},{64,7... | collective-permute-start | bytes 700424 | tf_op jit(solution)/shard_map/ppermute | solution.py:394
  22.4 14.8 %collective-permute-start.3 = (f32[456,128]{1,0:T(8,128)S(1)}, f32[456,128]{1,0:T(8,128)S(1)}, u32[]{:S(2)}, u32[]{:S(2)}) collective-permute-start(f32[456,128]{1,0:T(8,128)S(1)} %get-tuple-element.15), channel_id=1, source_target_pairs={{8,0},{16,8},{24,16},{32,24},{40,32},{48,40},{56,48},{64,56},{72,6... | collective-permute-start | bytes 700424 | tf_op jit(solution)/shard_map/ppermute | solution.py:395
  37.2 1.8 %collective-permute-done.2.below = f32[456,128]{1,0:T(8,128)S(1)} collective-permute-done((f32[456,128]{1,0:T(8,128)S(1)}, f32[456,128]{1,0:T(8,128)S(1)}, u32[]{:S(2)}, u32[]{:S(2)}) %collective-permute-start.2) | collective-permute-done | bytes 233504 | tf_op jit(solution)/shard_map/ppermute | solution.py:394
  39.0 1.8 %collective-permute-done.3.above = f32[456,128]{1,0:T(8,128)S(1)} collective-permute-done((f32[456,128]{1,0:T(8,128)S(1)}, f32[456,128]{1,0:T(8,128)S(1)}, u32[]{:S(2)}, u32[]{:S(2)}) %collective-permute-start.3) | collective-permute-done | bytes 233504 | tf_op jit(solution)/shard_map/ppermute | solution.py:395
  40.8 2.6 %shard_map.79 = (f32[19,3,48,128]{3,2,1,0:T(8,128)}, f32[7,3,48,128]{3,2,1,0:T(8,128)}) custom-call(f32[19,3,48,128]{3,2,1,0:T(8,128)S(1)} %copy-done, f32[7,3,48,128]{3,2,1,0:T(8,128)S(1)} %copy-done.1, s32[3,48,128]{2,1,0:T(8,128)S(1)} %copy-done.2, s32[3,48,128]{2,1,0:T(8,128)S(1)} %copy-done.3, f32[8]{0:T(128)S(1)} %copy-done.4, f32[8]{0:T(128)S(1)} %copy-done.5, ...), custom_call_target="tpu_custom_call" | custom-call | flops 1000000 | bytes 1000000 | tf_op jit(solution)/shard_map/pallas_call | solution.py:366
Async XLA Ops:
  0.6 1.3 %copy-start = (f32[19,3,48,128]{3,2,1,0:T(8,128)S(1)}, f32[19,3,48,128]{3,2,1,0:T(8,128)}, u32[]{:S(2)}) copy-start(f32[19,3,48,128]{3,2,1,0:T(8,128)} %pop.5) | copy-start | bytes 4202500
  2.0 1.0 %copy-start.1 = (f32[7,3,48,128]{3,2,1,0:T(8,128)S(1)}, f32[7,3,48,128]{3,2,1,0:T(8,128)}, u32[]{:S(2)}) copy-start(f32[7,3,48,128]{3,2,1,0:T(8,128)} %sol.5) | copy-start | bytes 1548292
  3.0 0.9 %copy-start.2 = (s32[3,48,128]{2,1,0:T(8,128)S(1)}, s32[3,48,128]{2,1,0:T(8,128)}, u32[]{:S(2)}) copy-start(s32[3,48,128]{2,1,0:T(8,128)} %pore.5) | copy-start | bytes 221188
  3.9 0.9 %copy-start.3 = (s32[3,48,128]{2,1,0:T(8,128)S(1)}, s32[3,48,128]{2,1,0:T(8,128)}, u32[]{:S(2)}) copy-start(s32[3,48,128]{2,1,0:T(8,128)} %ids.5) | copy-start | bytes 221188
  4.8 0.7 %copy-start.4 = (f32[8]{0:T(128)S(1)}, f32[8]{0:T(128)}, u32[]{:S(2)}) copy-start(f32[8]{0:T(128)} %rates.5) | copy-start | bytes 100
  5.4 0.7 %copy-start.5 = (f32[8]{0:T(128)S(1)}, f32[8]{0:T(128)}, u32[]{:S(2)}) copy-start(f32[8]{0:T(128)} %target.5) | copy-start | bytes 100
  6.7 6.8 %collective-permute-start = (f32[22,8,128]{2,1,0:T(8,128)S(1)}, f32[22,8,128]{2,1,0:T(8,128)S(1)}, u32[]{:S(2)}, u32[]{:S(2)}) collective-permute-start(f32[22,8,128]{2,1,0:T(8,128)S(1)} %get-tuple-element.9), channel_id=1, source_target_pairs={{0,1},{1,2},{2,3},{3,4},{4,5},{5,6},{6,7},{8,9},{9,10},{10,11},{11... | collective-permute-start | bytes 270344 | tf_op jit(solution)/shard_map/ppermute | solution.py:384
  11.4 7.6 %collective-permute-start.1 = (f32[22,8,128]{2,1,0:T(8,128)S(1)}, f32[22,8,128]{2,1,0:T(8,128)S(1)}, u32[]{:S(2)}, u32[]{:S(2)}) collective-permute-start(f32[22,8,128]{2,1,0:T(8,128)S(1)} %get-tuple-element.10), channel_id=1, source_target_pairs={{1,0},{2,1},{3,2},{4,3},{5,4},{6,5},{7,6},{9,8},{10,9},{11,10},{12... | collective-permute-start | bytes 270344 | tf_op jit(solution)/shard_map/ppermute | solution.py:385
  20.5 18.5 %collective-permute-start.2 = (f32[456,128]{1,0:T(8,128)S(1)}, f32[456,128]{1,0:T(8,128)S(1)}, u32[]{:S(2)}, u32[]{:S(2)}) collective-permute-start(f32[456,128]{1,0:T(8,128)S(1)} %get-tuple-element.14), channel_id=1, source_target_pairs={{0,8},{8,16},{16,24},{24,32},{32,40},{40,48},{48,56},{56,64},{64,7... | collective-permute-start | bytes 700424 | tf_op jit(solution)/shard_map/ppermute | solution.py:394
  22.4 18.4 %collective-permute-start.3 = (f32[456,128]{1,0:T(8,128)S(1)}, f32[456,128]{1,0:T(8,128)S(1)}, u32[]{:S(2)}, u32[]{:S(2)}) collective-permute-start(f32[456,128]{1,0:T(8,128)S(1)} %get-tuple-element.15), channel_id=1, source_target_pairs={{8,0},{16,8},{24,16},{32,24},{40,32},{48,40},{56,48},{64,56},{72,6... | collective-permute-start | bytes 700424 | tf_op jit(solution)/shard_map/ppermute | solution.py:395

commit v2 on v1

v2 whole, which is shorter than its diff:
```python
import functools

import jax
import jax.numpy as jnp
import numpy as np
from jax import lax
from jax.experimental import pallas as pl
from jax.experimental.pallas import tpu as pltpu
from jax.sharding import PartitionSpec as P

LINKS = (
    (0, 0, 0),
    (1, 0, 0),
    (-1, 0, 0),
    (0, 1, 0),
    (0, -1, 0),
    (0, 0, 1),
    (0, 0, -1),
    (1, 1, 0),
    (-1, -1, 0),
    (1, -1, 0),
    (-1, 1, 0),
    (1, 0, 1),
    (-1, 0, -1),
    (1, 0, -1),
    (-1, 0, 1),
    (0, 1, 1),
    (0, -1, -1),
    (0, 1, -1),
    (0, -1, 1),
)
REVERSE = (0, 2, 1, 4, 3, 6, 5, 8, 7, 10, 9, 12, 11, 14, 13, 16, 15, 18, 17)
W19 = (1.0 / 3.0,) + (1.0 / 18.0,) * 6 + (1.0 / 36.0,) * 12
W7 = (0.25,) + (0.125,) * 6
UP = tuple(q for q in range(19) if LINKS[q][0] == 1)
DOWN = tuple(q for q in range(19) if LINKS[q][0] == -1)
KEEP = 1.0 - 1.0 / 1.25
GAIN = 1.0 / 1.25
KEEP_S = 1.0 - 1.0 / 1.4
GAIN_S = 1.0 / 1.4
LX = 128
PAD = 8
MAX_VMEM = 12 * 1024 * 1024
NEAR = 23
FAR_ROWS = 3 * NEAR
EDGE_ROWS = 88
SPAN = 4


def relax(p):
    d = {q: p[q] - p[q + 1] for q in range(1, 19, 2)}
    s = {q: p[q] + p[q + 1] for q in range(1, 19, 2)}
    density = p[0] + (
        ((s[1] + s[3]) + (s[5] + s[7])) + ((s[9] + s[11]) + (s[13] + s[15])) + s[17]
    )
    mz = (d[1] + d[7]) + (d[9] + d[11]) + d[13]
    my = (d[3] + d[7]) + (d[15] + d[17]) - d[9]
    mx = (d[5] + d[11]) + (d[15] - d[13]) - d[17]
    inverse = 1.0 / density
    uz, uy, ux = mz * inverse, my * inverse, mx * inverse
    rest = 1.0 - 1.5 * (uz * uz + uy * uy + ux * ux)
    out = [None] * 19
    scaled = {w: density * (GAIN * w) for w in set(W19)}
    out[0] = KEEP * p[0] + scaled[W19[0]] * rest
    along = {
        1: uz,
        3: uy,
        5: ux,
        7: uz + uy,
        9: uz - uy,
        11: uz + ux,
        13: uz - ux,
        15: uy + ux,
        17: uy - ux,
    }
    for q, e in along.items():
        w = scaled[W19[q]]
        even = w * (rest + 4.5 * (e * e))
        odd = w * (3.0 * e)
        out[q] = KEEP * p[q] + (even + odd)
        out[q + 1] = KEEP * p[q + 1] + (even - odd)
    return out


def solute_terms(s, pore, ids, rates_ref, target_ref):
    total = ((s[0] + s[1]) + (s[2] + s[3])) + ((s[4] + s[5]) + s[6])
    rate = jnp.full(total.shape, rates_ref[0], jnp.float32)
    target = jnp.full(total.shape, target_ref[0], jnp.float32)
    for k in range(1, rates_ref.shape[0]):
        rate = jnp.where(ids == k, rates_ref[k], rate)
        target = jnp.where(ids == k, target_ref[k], target)
    reaction = jnp.where(pore == 2, -rate * (total - target), 0.0)
    return total, reaction


def rolled(value, shift):
    return value if shift == 0 else pltpu.roll(value, shift % LX, axis=1)


def sums(f):
    d = {q: f[q] - f[q + 1] for q in range(1, 19, 2)}
    s = {q: f[q] + f[q + 1] for q in range(1, 19, 2)}
    density = f[0] + (
        ((s[1] + s[3]) + (s[5] + s[7])) + ((s[9] + s[11]) + (s[13] + s[15])) + s[17]
    )
    mz = (d[1] + d[7]) + (d[9] + d[11]) + d[13]
    my = (d[3] + d[7]) + (d[15] + d[17]) - d[9]
    mx = (d[5] + d[11]) + (d[15] - d[13]) - d[17]
    return density, mz, my, mx


def add_all(values):
    values = list(values)
    while len(values) > 1:
        values = [
            values[i] + values[i + 1] if i + 1 < len(values) else values[i]
            for i in range(0, len(values), 2)
        ]
    return values[0]


def toward(sign):
    return tuple(q for q in range(19) if LINKS[q][1] == sign)


def pack_edges(pop, sol, pore, ids, up, down, epop, esol, epore, eids, erel, sems):
    width = pop.shape[2]
    copies = []
    for side, first in ((0, width - 8), (1, 0)):
        rows = pl.ds(first, 8)
        for k, (src, dst) in enumerate(
            (
                (pop.at[:, :, rows, :], epop),
                (sol.at[:, :, rows, :], esol),
                (pore.at[:, rows, :], epore),
                (ids.at[:, rows, :], eids),
            )
        ):
            copy = pltpu.make_async_copy(src, dst.at[side], sems.at[side, k])
            copy.start()
            copies.append(copy)
    for copy in copies:
        copy.wait()
    for side, out, near, far, link, sign in ((0, up, 7, 6, 3, 1), (1, down, 0, 1, 4, -1)):
        for layer in range(3):
            rel = relax([epop[side, q, layer] for q in range(19)])
            for q in range(19):
                erel[side, layer, q] = rel[q]
            kind = epore[side, layer].astype(jnp.float32)
            erel[side, layer, 19] = kind
            erel[side, layer, 20] = eids[side, layer].astype(jnp.float32)
            erel[side, layer, 21] = add_all(esol[side, q, layer] for q in range(7))
            erel[side, layer, 22] = esol[side, link, layer]
        for layer in range(3):
            for k in range(NEAR):
                at = 3 * k + layer
                out[at : at + 1, :] = erel[side, layer, k, near : near + 1, :]
            for k, q in enumerate(toward(sign) + (19,)):
                at = FAR_ROWS + 3 * k + layer
                out[at : at + 1, :] = erel[side, layer, q, far : far + 1, :]
        out[EDGE_ROWS - 1 : EDGE_ROWS, :] = jnp.zeros((1, LX), jnp.float32)


def relax_kernel(pop, sol, pore, ids, rates, target, moved, kept, mask, chem):
    width = pop.shape[2]
    for layer in range(3):
        for t in range(width // 8):
            rows, into = slice(8 * t, 8 * t + 8), slice(PAD + 8 * t, PAD + 8 * t + 8)
            out = relax([pop[q, layer, rows, :] for q in range(19)])
            for q in range(19):
                ex = LINKS[q][2]
                moved[q, layer, into, :] = rolled(out[q], ex)
                if ex:
                    kept[q, layer, into, :] = out[q]
            kind = pore[layer, rows, :]
            m = jnp.where(kind > 0, 1.0, 0.0)
            for ex in (0, 1, -1):
                mask[ex % 3, layer, into, :] = rolled(m, ex)
            s = [sol[q, layer, rows, :] for q in range(7)]
            total, reaction = solute_terms(s, kind, ids[layer, rows, :], rates, target)
            chem[0, layer, rows, :] = total
            chem[1, layer, rows, :] = reaction


def streamed(q, layer, row, count, shifted, plain, masks):
    ez, ey, ex = LINKS[q]
    value = shifted(q, layer - ez, row - ey, count)
    if q == 0:
        return value
    open_ = masks(ex, layer - ez, row - ey, count) > 0.0
    return jnp.where(open_, value, plain(REVERSE[q], layer, row, count))


def readers(moved, kept, mask):
    def shifted(q, layer, row, count):
        return moved[q, layer, row : row + count, :]

    def plain(q, layer, row, count):
        return (kept if LINKS[q][2] else moved)[q, layer, row : row + count, :]

    def masks(ex, layer, row, count):
        return mask[ex % 3, layer, row : row + count, :]

    return shifted, plain, masks


def by_parity(body, first, second):
    odd = lax.rem(lax.axis_index("gz"), 2)

    @pl.when(odd == 0)
    def _():
        body(first, second)

    @pl.when(odd == 1)
    def _():
        body(second, first)


def face_kernel(
    moved_in, kept_in, mask_in, low, high, sol, chem, moved, kept, mask, across, on_chip, turned
):
    del moved_in, kept_in, mask_in
    width = sol.shape[2]
    for side, ref, near, far, sign in (
        (0, low, PAD - 1, PAD - 2, 1),
        (1, high, PAD + width, PAD + width + 1, -1),
    ):
        for t in range(EDGE_ROWS // 8):
            v = ref[8 * t : 8 * t + 8, :]
            turned[side, 0, 8 * t : 8 * t + 8, :] = rolled(v, 1)
            turned[side, 1, 8 * t : 8 * t + 8, :] = rolled(v, -1)

        def line(at, ex):
            if ex == 0:
                return ref[at : at + 1, :]
            return turned[side, 0 if ex == 1 else 1, at : at + 1, :]

        for layer in range(3):
            for row, start, links in (
                (near, 0, tuple(range(19))),
                (far, FAR_ROWS, toward(sign)),
            ):
                into = slice(row, row + 1)
                for k, q in enumerate(links):
                    at, ex = start + 3 * k + layer, LINKS[q][2]
                    moved[q, layer, into, :] = line(at, ex)
                    if ex:
                        kept[q, layer, into, :] = line(at, 0)
                at = start + 3 * len(links) + layer
                for ex in (0, 1, -1):
                    mask[ex % 3, layer, into, :] = line(at, ex)
    shifted, plain, masks = readers(moved, kept, mask)

    def emit(up, down):
        span = width + SPAN
        for out, layer, cross, link in ((up, 2, UP, 1), (down, 0, DOWN, 2)):
            w = W7[link]
            for t in range(width // 8):
                row, rows = PAD + 8 * t, slice(8 * t, 8 * t + 8)
                get = functools.partial(
                    streamed,
                    layer=layer,
                    row=row,
                    count=8,
                    shifted=shifted,
                    plain=plain,
                    masks=masks,
                )
                away = add_all(get(q) for q in cross)
                level = add_all(get(q) for q in range(19) if LINKS[q][0] == 0)
                partial = level + away
                total, reaction = chem[0, layer, rows, :], chem[1, layer, rows, :]
                slope = (4.0 * w * GAIN_S) * total
                base = KEEP_S * sol[link, layer, rows, :] + (w * GAIN_S) * total + w * reaction
                for k, v in enumerate((base - slope, partial, slope * (partial + away))):
                    at = 6 * span + k * width + 8 * t
                    out[at : at + 8, :] = v
            for k in range(6):
                at = k * span
                pieces = [(PAD - 2, 2, 0)]
                pieces += [(PAD + 8 * t, 8, 2 + 8 * t) for t in range(width // 8)]
                pieces += [(PAD + width, 2, 2 + width)]
                for row, count, to in pieces:
                    v = plain(cross[k], layer, row, count) if k < 5 else masks(0, layer, row, count)
                    out[at + to : at + to + count, :] = v

    by_parity(emit, on_chip, across)


def inner_kernel(
    pop,
    sol,
    pore,
    chem,
    moved,
    kept,
    mask,
    low,
    high,
    rates,
    target,
    flow,
    part,
    edge_part,
    edge_chem,
    middle,
    middle_moved,
    buffer,
    sems,
):
    width = pop.shape[2]
    tiles = width // 8
    shifted, plain, masks = readers(moved, kept, mask)
    zero8 = jnp.zeros((8, LX), jnp.float32)
    zero1 = jnp.zeros((1, LX), jnp.float32)

    def pull(layer, row, count, zero):
        return [
            streamed(q, layer, row, count, shifted, plain, masks)
            if 0 <= layer - LINKS[q][0] <= 2
            else zero
            for q in range(19)
        ]

    copies = []
    for layer in (1, 0, 2):
        for t in range(tiles):
            row, rows = PAD + 8 * t, slice(8 * t, 8 * t + 8)
            f = pull(layer, row, 8, zero8)
            rock = pore[layer, rows, :] == 0
            for q in range(19):
                if 0 <= layer - LINKS[q][0] <= 2:
                    buffer[q, layer, rows, :] = jnp.where(rock, pop[q, layer, rows, :], f[q])
            density, mz, my, mx = sums(f)
            if layer != 1:
                for k, v in enumerate((density, mz, my, mx)):
                    part[layer // 2, k, rows, :] = v
                continue
            relaxed = relax_solute(
                [sol[q, layer, rows, :] for q in range(7)],
                chem[0, layer, rows, :],
                chem[1, layer, rows, :],
                jnp.where(rock, 0.0, 1.0 / density),
                (mz, my, mx),
            )
            into = slice(row, row + 8)
            for q in range(7):
                middle[q, into, :] = relaxed[q]
            middle_moved[0, rows, :] = rolled(relaxed[5], 1)
            middle_moved[1, rows, :] = rolled(relaxed[6], -1)
        inside = [q for q in range(19) if 0 <= layer - LINKS[q][0] <= 2]
        if layer == 1:
            copies.append(pltpu.make_async_copy(buffer.at[:, 1], flow.at[:, 1], sems.at[0]))
            copies[-1].start()
        else:
            for q in inside:
                copies.append(
                    pltpu.make_async_copy(
                        buffer.at[q, layer], flow.at[q, layer], sems.at[1 + (layer // 2) * 19 + q]
                    )
                )
                copies[-1].start()
    for side, ref, row, link, sign in (
        (0, low, PAD - 1, 3, 1.0),
        (1, high, PAD + width, 4, -1.0),
    ):
        w = W7[link]
        for layer in range(3):
            kind, mineral, total, own = (
                ref[3 * k + layer : 3 * k + layer + 1, :] for k in range(19, 23)
            )
            rate = jnp.full((1, LX), rates[0], jnp.float32)
            goal = jnp.full((1, LX), target[0], jnp.float32)
            for k in range(1, rates.shape[0]):
                rate = jnp.where(mineral == float(k), rates[k], rate)
                goal = jnp.where(mineral == float(k), target[k], goal)
            reaction = jnp.where(kind == 2.0, -rate * (total - goal), 0.0)
            base = KEEP_S * own + (w * GAIN_S) * total + w * reaction
            slope = (sign * 4.0 * w * GAIN_S) * total
            density, _, my, _ = sums(pull(layer, row, 1, zero1))
            if layer == 1:
                middle[link, row : row + 1, :] = base + slope * (my / density)
            else:
                at = 2 * side + layer // 2
                edge_part[0, at : at + 1, :] = density
                edge_part[1, at : at + 1, :] = my
                edge_chem[0, at : at + 1, :] = base
                edge_chem[1, at : at + 1, :] = slope
    for copy in copies:
        copy.wait()


def relax_solute(s, total, reaction, inverse, momenta):
    common = (W7[1] * GAIN_S) * total + W7[1] * reaction
    slope = (4.0 * W7[1] * GAIN_S) * total * inverse
    out = [KEEP_S * s[0] + (W7[0] * GAIN_S) * total + W7[0] * reaction]
    for q, m in zip((1, 3, 5), momenta):
        out.append(KEEP_S * s[q] + common + slope * m)
        out.append(KEEP_S * s[q + 1] + common - slope * m)
    return out


def outer_kernel(
    pop,
    sol,
    pore,
    chem,
    moved,
    kept,
    mask,
    part,
    edge_part,
    edge_chem,
    middle,
    middle_moved,
    across,
    on_chip,
    flow_in,
    flow,
    solute,
    faces,
    faces_moved,
    cross_s,
    fbuf,
    sbuf,
    sems,
):
    del flow_in
    width = pop.shape[2]
    tiles = width // 8
    span = width + SPAN
    own = readers(moved, kept, mask)

    def body(above, below):
        def value(q, layer, row, count):
            ref, links = (below, UP) if layer == -1 else (above, DOWN)
            at = links.index(q) * span + row - PAD + 2
            return ref[at : at + count, :]

        def shifted(q, layer, row, count):
            if 0 <= layer <= 2:
                return own[0](q, layer, row, count)
            return rolled(value(q, layer, row, count), LINKS[q][2])

        def plain(q, layer, row, count):
            if 0 <= layer <= 2:
                return own[1](q, layer, row, count)
            return value(q, layer, row, count)

        def masks(ex, layer, row, count):
            if 0 <= layer <= 2:
                return own[2](ex, layer, row, count)
            at = 5 * span + row - PAD + 2
            return rolled((below if layer == -1 else above)[at : at + count, :], ex)

        copies = []

        def send(src, dst):
            copies.append(pltpu.make_async_copy(src, dst, sems.at[len(copies)]))
            copies[-1].start()

        for side, ref, layer, outside, enter, leave in (
            (0, below, 0, -1, UP, DOWN),
            (1, above, 2, 3, DOWN, UP),
        ):
            sign = 1.0 if side == 0 else -1.0
            for t in range(tiles):
                row, rows = PAD + 8 * t, slice(8 * t, 8 * t + 8)
                rock = pore[layer, rows, :] == 0
                f = {q: streamed(q, layer, row, 8, shifted, plain, masks) for q in enter}
                for k, q in enumerate(enter):
                    fbuf[side, k, rows, :] = jnp.where(rock, pop[q, layer, rows, :], f[q])
                density, mz, my, mx = (part[side, k, rows, :] for k in range(4))
                arrived = add_all(f.values())
                density = density + arrived
                mz = mz + sign * arrived
                for q in enter:
                    _, ey, ex = LINKS[q]
                    if ey:
                        my = my + f[q] if ey == 1 else my - f[q]
                    if ex:
                        mx = mx + f[q] if ex == 1 else mx - f[q]
                relaxed = relax_solute(
                    [sol[q, layer, rows, :] for q in range(7)],
                    chem[0, layer, rows, :],
                    chem[1, layer, rows, :],
                    jnp.where(rock, 0.0, 1.0 / density),
                    (mz, my, mx),
                )
                into = slice(row, row + 8)
                for q in range(7):
                    faces[q, side, into, :] = relaxed[q]
                faces_moved[0, side, rows, :] = rolled(relaxed[5], 1)
                faces_moved[1, side, rows, :] = rolled(relaxed[6], -1)
                back = add_all(
                    streamed(q, outside, row, 8, shifted, plain, masks) for q in leave
                )
                base, partial, weight = (
                    ref[6 * span + k * width + 8 * t : 6 * span + k * width + 8 * t + 8, :]
                    for k in range(3)
                )
                cross_s[side, rows, :] = base + weight / (partial + back)
            for k, q in enumerate(enter):
                send(fbuf.at[side, k], flow.at[q, layer])
            for end, row, link in ((0, PAD - 1, 3), (1, PAD + width, 4)):
                at = 2 * end + side
                line = slice(at, at + 1)
                f = {q: streamed(q, layer, row, 1, shifted, plain, masks) for q in enter}
                density = edge_part[0, line, :] + add_all(f.values())
                my = edge_part[1, line, :]
                for q in enter:
                    if LINKS[q][1]:
                        my = my + f[q] if LINKS[q][1] == 1 else my - f[q]
                faces[link, side, row : row + 1, :] = edge_chem[0, line, :] + edge_chem[
                    1, line, :
                ] * (my / density)

        def solute_at(q, layer, row, count):
            if layer == 1:
                return middle[q, row : row + count, :]
            return faces[q, layer // 2, row : row + count, :]

        for layer in (1, 0, 2):
            for t in range(tiles):
                row, rows = PAD + 8 * t, slice(8 * t, 8 * t + 8)
                rock = pore[layer, rows, :] == 0
                for q in range(7):
                    ez, ey, ex = LINKS[q]
                    src = layer - ez
                    if src == -1:
                        v = cross_s[0, rows, :]
                    elif src == 3:
                        v = cross_s[1, rows, :]
                    elif ex and layer == 1:
                        v = middle_moved[q - 5, rows, :]
                    elif ex:
                        v = faces_moved[q - 5, layer // 2, rows, :]
                    else:
                        v = solute_at(q, src, row - ey, 8)
                    if q:
                        open_ = masks(ex, src, row - ey, 8) > 0.0
                        v = jnp.where(open_, v, solute_at(REVERSE[q], layer, row, 8))
                    sbuf[q, layer, rows, :] = jnp.where(rock, sol[q, layer, rows, :], v)
            send(sbuf.at[:, layer], solute.at[:, layer])
        for copy in copies:
            copy.wait()

    by_parity(body, on_chip, across)


VMEM = pl.BlockSpec(memory_space=pltpu.VMEM)
SMEM = pl.BlockSpec(memory_space=pltpu.SMEM)
ANY = pl.BlockSpec(memory_space=pl.ANY)
HBM = pl.BlockSpec(memory_space=pltpu.HBM)
DMA = pltpu.SemaphoreType.DMA


def call(kernel, operands, specs, outs, scratch=(), aliases=None, flops=1_000_000):
    return pl.pallas_call(
        kernel,
        out_shape=[jax.ShapeDtypeStruct(s, jnp.float32) for s, _ in outs],
        in_specs=list(specs),
        out_specs=[spec for _, spec in outs],
        scratch_shapes=[pltpu.VMEM(s, jnp.float32) if isinstance(s, tuple) else s for s in scratch],
        input_output_aliases=aliases or {},
        compiler_params=pltpu.CompilerParams(vmem_limit_bytes=MAX_VMEM),
        cost_estimate=pl.CostEstimate(flops=flops, bytes_accessed=1_000_000, transcendentals=0),
        name=kernel.__name__,
    )(*operands)


def on_device(populations, solute, pore_mask, mineral_ids, reaction_rates, saturation):
    width = pore_mask.shape[1]
    padded = width + 2 * PAD
    cells = (populations, solute, pore_mask, mineral_ids)
    tables = (reaction_rates, saturation)
    gz, gy = lax.axis_size("gz"), lax.axis_size("gy")
    edges = call(
        pack_edges,
        tuple(pltpu.with_memory_space_constraint(v, pltpu.HBM) for v in cells),
        [HBM] * 4,
        [((EDGE_ROWS, LX), VMEM)] * 2,
        [
            (2, 19, 3, 8, LX),
            (2, 7, 3, 8, LX),
            pltpu.VMEM((2, 3, 8, LX), jnp.int32),
            pltpu.VMEM((2, 3, 8, LX), jnp.int32),
            (2, 3, NEAR, 8, LX),
            DMA((2, 4)),
        ],
    )
    low = lax.ppermute(edges[0], "gy", [(i, i + 1) for i in range(gy - 1)])
    high = lax.ppermute(edges[1], "gy", [(i + 1, i) for i in range(gy - 1)])
    whole = ((19, 3, padded, LX), VMEM)
    masks = ((3, 3, padded, LX), VMEM)
    moved, kept, mask, chem = call(
        relax_kernel,
        cells + tables,
        [VMEM] * 4 + [SMEM] * 2,
        [whole, whole, masks, ((2, 3, width, LX), VMEM)],
        flops=6_000_000,
    )
    rows = 9 * width + 6 * SPAN
    moved, kept, mask, across, on_chip = call(
        face_kernel,
        (moved, kept, mask, low, high, solute, chem),
        [VMEM] * 7,
        [whole, whole, masks, ((rows, LX), VMEM), ((rows, LX), VMEM)],
        [(2, 2, EDGE_ROWS, LX)],
        {0: 0, 1: 1, 2: 2},
    )
    across = lax.ppermute(
        across, "gz", [(i, (i + 1 if i % 2 else i - 1) % gz) for i in range(gz)]
    )
    on_chip = lax.ppermute(on_chip, "gz", [(i, i + 1 - 2 * (i % 2)) for i in range(gz)])
    flow, part, edge_part, edge_chem, middle, middle_moved = call(
        inner_kernel,
        cells[:3] + (chem, moved, kept, mask, low, high) + tables,
        [VMEM] * 9 + [SMEM] * 2,
        [
            (populations.shape, ANY),
            ((2, 4, width, LX), VMEM),
            ((2, 8, LX), VMEM),
            ((2, 8, LX), VMEM),
            ((7, padded, LX), VMEM),
            ((2, width, LX), VMEM),
        ],
        [(19, 3, width, LX), DMA((39,))],
        flops=6_000_000,
    )
    return tuple(
        call(
            outer_kernel,
            cells[:3]
            + (chem, moved, kept, mask, part, edge_part, edge_chem, middle, middle_moved)
            + (across, on_chip, flow),
            [VMEM] * 14 + [ANY],
            [(populations.shape, ANY), (solute.shape, ANY)],
            [
                (7, 2, padded, LX),
                (2, 2, width, LX),
                (2, width, LX),
                (2, 5, width, LX),
                (7, 3, width, LX),
                DMA((13,)),
            ],
            {14: 0},
        )
    )


def solution(mesh):
    cells = P(None, "gz", "gy", None)
    return jax.shard_map(
        on_device,
        mesh=mesh,
        in_specs=(cells, cells, P("gz", "gy", None), P("gz", "gy", None), P(), P()),
        out_specs=(cells, cells),
        check_vma=False,
    )
```

time: 43.8 us -> 35.5 us (0.81)
  the two profiles are of different devices: /device:TPU:24 before, /device:TPU:25 now
where the time goes in v2:
time: 35.5 us; the launch traced here: 35.3 us
  starting transfers between devices  25.1 us (71%)
  Pallas kernels  6.52 us (18%)
  waiting for transfers between devices  2.78 us (8%)
  between operations  0.81 us (2%)
    ppermute x1, starting transfers between devices, on_device(): lax.ppermute(on_chip, 'gz', [(i, i + 1 - 2 * (i % 2)) for i in range(gz)])  13.7 us
    pallas_call x5, Pallas kernels, call(): pl.pallas_call(kernel, out_shape=[jax.ShapeDtypeStruct(s, jnp.float32) fo...  6.52 us
    ppermute x1, starting transfers between devices, on_device(): lax.ppermute(across, 'gz', [(i, (i + 1 if i % 2 else i - 1) % gz) for i i...  5.11 us
    ppermute x1, starting transfers between devices, on_device(): low = lax.ppermute(edges[0], 'gy', [(i, i + 1) for i in range(gy - 1)])  4.42 us
    ppermute x1, waiting for transfers between devices, on_device(): high = lax.ppermute(edges[1], 'gy', [(i + 1, i) for i in range(gy - 1)])  2.77 us
    ppermute x1, starting transfers between devices, on_device(): high = lax.ppermute(edges[1], 'gy', [(i + 1, i) for i in range(gy - 1)])  1.92 us
  transfers between devices with their start and end apart: 4, of which 1 were waited for; matrix products, arithmetic and copies ran while one was open for 0% of the time, Pallas kernels for 9%

profile of v2, /device:TPU:25, one launch (start us, length us, event | category | flops | bytes accessed | tf_op | source)
XLA Modules:
  0.0 35.3 jit_solution(17569539917424699405)
XLA Ops:
  0.6 0.0 copy-start.1
  0.6 0.0 copy-start.2
  0.7 0.0 copy-start
  0.7 0.0 copy-start.3
  0.7 0.0 copy-start.5
  0.7 0.0 copy-start.4
  0.7 1.6 %pack_edges.1 = (f32[88,128]{1,0:T(8,128)S(1)}, f32[88,128]{1,0:T(8,128)S(1)}) custom-call(f32[19,3,48,128]{3,2,1,0:T(8,128)} %pop.7, f32[7,3,48,128]{3,2,1,0:T(8,128)} %sol.9, s32[3,48,128]{2,1,0:T(8,128)} %pore.7, s32[3,48,128]{2,1,0:T(8,128)} %ids.3), custom_call_target="tpu_custom_call" | custom-call | flops 1000000 | bytes 1000000 | tf_op jit(solution)/shard_map/pack_edges/pallas_call | solution.py:559
  2.3 4.4 %collective-permute-start = (f32[88,128]{1,0:T(8,128)S(1)}, f32[88,128]{1,0:T(8,128)S(1)}, u32[]{:S(2)}, u32[]{:S(2)}) collective-permute-start(f32[88,128]{1,0:T(8,128)S(1)} %get-tuple-element.23), channel_id=1, source_target_pairs={{0,1},{1,2},{2,3},{3,4},{4,5},{5,6},{6,7},{8,9},{9,10},{10,11},{11... | collective-permute-start | bytes 135176 | tf_op jit(solution)/shard_map/ppermute | solution.py:592
  6.7 1.9 %collective-permute-start.1 = (f32[88,128]{1,0:T(8,128)S(1)}, f32[88,128]{1,0:T(8,128)S(1)}, u32[]{:S(2)}, u32[]{:S(2)}) collective-permute-start(f32[88,128]{1,0:T(8,128)S(1)} %get-tuple-element.24), channel_id=1, source_target_pairs={{1,0},{2,1},{3,2},{4,3},{5,4},{6,5},{7,6},{9,8},{10,9},{11,10},{12... | collective-permute-start | bytes 135176 | tf_op jit(solution)/shard_map/ppermute | solution.py:593
  8.7 0.0 copy-done.1
  8.7 0.0 copy-done.2
  8.7 0.0 copy-done
  8.7 0.0 copy-done.3
  8.7 0.0 copy-done.5
  8.7 0.0 copy-done.4
  8.7 1.2 %relax_kernel.1 = (f32[19,3,64,128]{3,2,1,0:T(8,128)S(1)}, f32[19,3,64,128]{3,2,1,0:T(8,128)S(1)}, f32[3,3,64,128]{3,2,1,0:T(8,128)S(1)}, f32[2,3,48,128]{3,2,1,0:T(8,128)S(1)}) custom-call(f32[19,3,48,128]{3,2,1,0:T(8,128)S(1)} %copy-done, f32[7,3,48,128]{3,2,1,0:T(8,128)S(1)} %copy-done.1, s32[3,48,128]{2,1,0:T(8,128)S(1)} %copy-done.2, ...), custom_call_target="tpu_custom_call" | custom-call | flops 6000000 | bytes 1000000 | tf_op jit(solution)/shard_map/relax_kernel/pallas_call | solution.py:559
  9.9 0.0 collective-permute-done.low
  10.0 2.8 %collective-permute-done.1.high = f32[88,128]{1,0:T(8,128)S(1)} collective-permute-done((f32[88,128]{1,0:T(8,128)S(1)}, f32[88,128]{1,0:T(8,128)S(1)}, u32[]{:S(2)}, u32[]{:S(2)}) %collective-permute-start.1) | collective-permute-done | bytes 45088 | tf_op jit(solution)/shard_map/ppermute | solution.py:593
  12.7 0.3 face_kernel.1
  13.1 5.1 %collective-permute-start.2 = (f32[456,128]{1,0:T(8,128)S(1)}, f32[456,128]{1,0:T(8,128)S(1)}, u32[]{:S(2)}, u32[]{:S(2)}) collective-permute-start(f32[456,128]{1,0:T(8,128)S(1)} %get-tuple-element.33), channel_id=1, source_target_pairs={{0,760},{8,16},{16,8},{24,32},{32,24},{40,48},{48,40},{56,64},{64,... | collective-permute-start | bytes 700424 | tf_op jit(solution)/shard_map/ppermute | solution.py:612
  18.2 13.7 %collective-permute-start.3 = (f32[456,128]{1,0:T(8,128)S(1)}, f32[456,128]{1,0:T(8,128)S(1)}, u32[]{:S(2)}, u32[]{:S(2)}) collective-permute-start(f32[456,128]{1,0:T(8,128)S(1)} %get-tuple-element.34), channel_id=1, source_target_pairs={{0,8},{8,0},{16,24},{24,16},{32,40},{40,32},{48,56},{56,48},{64,72... | collective-permute-start | bytes 700424 | tf_op jit(solution)/shard_map/ppermute | solution.py:615
  31.9 2.1 %inner_kernel.1 = (f32[19,3,48,128]{3,2,1,0:T(8,128)}, f32[2,4,48,128]{3,2,1,0:T(8,128)S(1)}, f32[2,8,128]{2,1,0:T(8,128)S(1)}, f32[2,8,128]{2,1,0:T(8,128)S(1)}...) custom-call(f32[19,3,48,128]{3,2,1,0:T(8,128)S(1)} %copy-done, f32[7,3,48,128]{3,2,1,0:T(8,128)S(1)} %copy-done.1, ...), custom_call_target="tpu_custom_call" | custom-call | flops 6000000 | bytes 1000000 | tf_op jit(solution)/shard_map/inner_kernel/pallas_call | solution.py:559
  34.0 0.0 collective-permute-done.2.across
  34.0 0.0 collective-permute-done.3.on_chip
  34.0 1.3 %outer_kernel.1 = (f32[19,3,48,128]{3,2,1,0:T(8,128)}, f32[7,3,48,128]{3,2,1,0:T(8,128)}) custom-call(f32[19,3,48,128]{3,2,1,0:T(8,128)S(1)} %copy-done, f32[7,3,48,128]{3,2,1,0:T(8,128)S(1)} %copy-done.1, s32[3,48,128]{2,1,0:T(8,128)S(1)} %copy-done.2, f32[2,3,48,128]{3,2,1,0:T(8,128)S(1)} %get-tuple-element.19.chem, ...), custom_call_target="tpu_custom_call", output_to_operand_aliasing={{0}: (14, {})} | custom-call | flops 1000000 | bytes 1000000 | tf_op jit(solution)/shard_map/outer_kernel/pallas_call | solution.py:559
Async XLA Ops:
  0.6 8.0 %copy-start.1 = (f32[7,3,48,128]{3,2,1,0:T(8,128)S(1)}, f32[7,3,48,128]{3,2,1,0:T(8,128)}, u32[]{:S(2)}) copy-start(f32[7,3,48,128]{3,2,1,0:T(8,128)} %sol.9) | copy-start | bytes 1548292
  0.6 8.0 %copy-start.2 = (s32[3,48,128]{2,1,0:T(8,128)S(1)}, s32[3,48,128]{2,1,0:T(8,128)}, u32[]{:S(2)}) copy-start(s32[3,48,128]{2,1,0:T(8,128)} %pore.7) | copy-start | bytes 221188
  0.7 8.0 %copy-start = (f32[19,3,48,128]{3,2,1,0:T(8,128)S(1)}, f32[19,3,48,128]{3,2,1,0:T(8,128)}, u32[]{:S(2)}) copy-start(f32[19,3,48,128]{3,2,1,0:T(8,128)} %pop.7) | copy-start | bytes 4202500
  0.7 8.0 %copy-start.3 = (s32[3,48,128]{2,1,0:T(8,128)S(1)}, s32[3,48,128]{2,1,0:T(8,128)}, u32[]{:S(2)}) copy-start(s32[3,48,128]{2,1,0:T(8,128)} %ids.3) | copy-start | bytes 221188
  0.7 8.0 %copy-start.5 = (f32[8]{0:T(128)S(1)}, f32[8]{0:T(128)}, u32[]{:S(2)}) copy-start(f32[8]{0:T(128)} %target.3) | copy-start | bytes 100
  0.7 8.0 %copy-start.4 = (f32[8]{0:T(128)S(1)}, f32[8]{0:T(128)}, u32[]{:S(2)}) copy-start(f32[8]{0:T(128)} %rates.3) | copy-start | bytes 100
  2.3 7.6 %collective-permute-start = (f32[88,128]{1,0:T(8,128)S(1)}, f32[88,128]{1,0:T(8,128)S(1)}, u32[]{:S(2)}, u32[]{:S(2)}) collective-permute-start(f32[88,128]{1,0:T(8,128)S(1)} %get-tuple-element.23), channel_id=1, source_target_pairs={{0,1},{1,2},{2,3},{3,4},{4,5},{5,6},{6,7},{8,9},{9,10},{10,11},{11... | collective-permute-start | bytes 135176 | tf_op jit(solution)/shard_map/ppermute | solution.py:592
  6.7 6.0 %collective-permute-start.1 = (f32[88,128]{1,0:T(8,128)S(1)}, f32[88,128]{1,0:T(8,128)S(1)}, u32[]{:S(2)}, u32[]{:S(2)}) collective-permute-start(f32[88,128]{1,0:T(8,128)S(1)} %get-tuple-element.24), channel_id=1, source_target_pairs={{1,0},{2,1},{3,2},{4,3},{5,4},{6,5},{7,6},{9,8},{10,9},{11,10},{12... | collective-permute-start | bytes 135176 | tf_op jit(solution)/shard_map/ppermute | solution.py:593
  13.1 20.9 %collective-permute-start.2 = (f32[456,128]{1,0:T(8,128)S(1)}, f32[456,128]{1,0:T(8,128)S(1)}, u32[]{:S(2)}, u32[]{:S(2)}) collective-permute-start(f32[456,128]{1,0:T(8,128)S(1)} %get-tuple-element.33), channel_id=1, source_target_pairs={{0,760},{8,16},{16,8},{24,32},{32,24},{40,48},{48,40},{56,64},{64,... | collective-permute-start | bytes 700424 | tf_op jit(solution)/shard_map/ppermute | solution.py:612
  18.2 15.8 %collective-permute-start.3 = (f32[456,128]{1,0:T(8,128)S(1)}, f32[456,128]{1,0:T(8,128)S(1)}, u32[]{:S(2)}, u32[]{:S(2)}) collective-permute-start(f32[456,128]{1,0:T(8,128)S(1)} %get-tuple-element.34), channel_id=1, source_target_pairs={{0,8},{8,0},{16,24},{24,16},{32,40},{40,32},{48,56},{56,48},{64,72... | collective-permute-start | bytes 700424 | tf_op jit(solution)/shard_map/ppermute | solution.py:615

commit v3 on v2

--- a/solution.py
+++ b/solution.py
@@ -123,11 +123,25 @@
     return tuple(q for q in range(19) if LINKS[q][1] == sign)
 
 
-def pack_edges(pop, sol, pore, ids, up, down, epop, esol, epore, eids, erel, sems):
+def either(condition, when_true, when_false):
+    pl.when(condition)(when_true)
+    pl.when(jnp.logical_not(condition))(when_false)
+
+
+def upper_half():
+    return lax.axis_index("gz") >= lax.axis_size("gz") // 2
+
+
+def by_parity(body, first, second):
+    even = lax.rem(lax.axis_index("gz"), 2) == 0
+    either(even, lambda: body(first, second), lambda: body(second, first))
+
+
+def pack_edges(pop, sol, pore, ids, first, second, epop, esol, epore, eids, erel, sems):
     width = pop.shape[2]
     copies = []
-    for side, first in ((0, width - 8), (1, 0)):
-        rows = pl.ds(first, 8)
+    for side, start in ((0, width - 8), (1, 0)):
+        rows = pl.ds(start, 8)
         for k, (src, dst) in enumerate(
             (
                 (pop.at[:, :, rows, :], epop),
@@ -141,7 +155,7 @@
             copies.append(copy)
     for copy in copies:
         copy.wait()
-    for side, out, near, far, link, sign in ((0, up, 7, 6, 3, 1), (1, down, 0, 1, 4, -1)):
+    for side, link in ((0, 3), (1, 4)):
         for layer in range(3):
             rel = relax([epop[side, q, layer] for q in range(19)])
             for q in range(19):
@@ -151,18 +165,26 @@
             erel[side, layer, 20] = eids[side, layer].astype(jnp.float32)
             erel[side, layer, 21] = add_all(esol[side, q, layer] for q in range(7))
             erel[side, layer, 22] = esol[side, link, layer]
-        for layer in range(3):
-            for k in range(NEAR):
-                at = 3 * k + layer
-                out[at : at + 1, :] = erel[side, layer, k, near : near + 1, :]
-            for k, q in enumerate(toward(sign) + (19,)):
-                at = FAR_ROWS + 3 * k + layer
-                out[at : at + 1, :] = erel[side, layer, q, far : far + 1, :]
-        out[EDGE_ROWS - 1 : EDGE_ROWS, :] = jnp.zeros((1, LX), jnp.float32)
-
-
-def relax_kernel(pop, sol, pore, ids, rates, target, moved, kept, mask, chem):
+
+    def emit(up, down):
+        for side, out, near, far, sign in ((0, up, 7, 6, 1), (1, down, 0, 1, -1)):
+            for layer in range(3):
+                for k in range(NEAR):
+                    at = 3 * k + layer
+                    out[at : at + 1, :] = erel[side, layer, k, near : near + 1, :]
+                for k, q in enumerate(toward(sign) + (19,)):
+                    at = FAR_ROWS + 3 * k + layer
+                    out[at : at + 1, :] = erel[side, layer, q, far : far + 1, :]
+            out[EDGE_ROWS - 1 : EDGE_ROWS, :] = jnp.zeros((1, LX), jnp.float32)
+
+    either(upper_half(), lambda: emit(second, first), lambda: emit(first, second))
+
+
+def relax_kernel(pop, sol, pore, ids, rates, target, moved, kept, mask, chem, table):
     width = pop.shape[2]
+    for k in range(rates.shape[0]):
+        for at, ref in ((k, rates), (k + rates.shape[0], target)):
+            table[at : at + 1, :] = jnp.full((1, LX), ref[k], jnp.float32)
     for layer in range(3):
         for t in range(width // 8):
             rows, into = slice(8 * t, 8 * t + 8), slice(PAD + 8 * t, PAD + 8 * t + 8)
@@ -204,35 +226,42 @@
     return shifted, plain, masks
 
 
-def by_parity(body, first, second):
-    odd = lax.rem(lax.axis_index("gz"), 2)
-
-    @pl.when(odd == 0)
-    def _():
-        body(first, second)
-
-    @pl.when(odd == 1)
-    def _():
-        body(second, first)
-
-
 def face_kernel(
-    moved_in, kept_in, mask_in, low, high, sol, chem, moved, kept, mask, across, on_chip, turned
+    moved_in,
+    kept_in,
+    mask_in,
+    first,
+    second,
+    sol,
+    chem,
+    moved,
+    kept,
+    mask,
+    across,
+    on_chip,
+    edges,
+    turned,
 ):
     del moved_in, kept_in, mask_in
     width = sol.shape[2]
-    for side, ref, near, far, sign in (
-        (0, low, PAD - 1, PAD - 2, 1),
-        (1, high, PAD + width, PAD + width + 1, -1),
+    upper = upper_half()
+    for t in range(EDGE_ROWS // 8):
+        rows = slice(8 * t, 8 * t + 8)
+        for side, v in (
+            (0, jnp.where(upper, second[rows, :], first[rows, :])),
+            (1, jnp.where(upper, first[rows, :], second[rows, :])),
+        ):
+            edges[side, rows, :] = v
+            turned[side, 0, rows, :] = rolled(v, 1)
+            turned[side, 1, rows, :] = rolled(v, -1)
+    for side, near, far, sign in (
+        (0, PAD - 1, PAD - 2, 1),
+        (1, PAD + width, PAD + width + 1, -1),
     ):
-        for t in range(EDGE_ROWS // 8):
-            v = ref[8 * t : 8 * t + 8, :]
-            turned[side, 0, 8 * t : 8 * t + 8, :] = rolled(v, 1)
-            turned[side, 1, 8 * t : 8 * t + 8, :] = rolled(v, -1)
 
         def line(at, ex):
             if ex == 0:
-                return ref[at : at + 1, :]
+                return edges[side, at : at + 1, :]
             return turned[side, 0 if ex == 1 else 1, at : at + 1, :]
 
         for layer in range(3):
@@ -295,18 +324,14 @@
     moved,
     kept,
     mask,
-    low,
-    high,
-    rates,
-    target,
+    edges,
+    table,
     flow,
     part,
     edge_part,
     edge_chem,
     middle,
     middle_moved,
-    buffer,
-    sems,
 ):
     width = pop.shape[2]
     tiles = width // 8
@@ -322,7 +347,6 @@
             for q in range(19)
         ]
 
-    copies = []
     for layer in (1, 0, 2):
         for t in range(tiles):
             row, rows = PAD + 8 * t, slice(8 * t, 8 * t + 8)
@@ -330,7 +354,7 @@
             rock = pore[layer, rows, :] == 0
             for q in range(19):
                 if 0 <= layer - LINKS[q][0] <= 2:
-                    buffer[q, layer, rows, :] = jnp.where(rock, pop[q, layer, rows, :], f[q])
+                    flow[q, layer, rows, :] = jnp.where(rock, pop[q, layer, rows, :], f[q])
             density, mz, my, mx = sums(f)
             if layer != 1:
                 for k, v in enumerate((density, mz, my, mx)):
@@ -348,32 +372,17 @@
                 middle[q, into, :] = relaxed[q]
             middle_moved[0, rows, :] = rolled(relaxed[5], 1)
             middle_moved[1, rows, :] = rolled(relaxed[6], -1)
-        inside = [q for q in range(19) if 0 <= layer - LINKS[q][0] <= 2]
-        if layer == 1:
-            copies.append(pltpu.make_async_copy(buffer.at[:, 1], flow.at[:, 1], sems.at[0]))
-            copies[-1].start()
-        else:
-            for q in inside:
-                copies.append(
-                    pltpu.make_async_copy(
-                        buffer.at[q, layer], flow.at[q, layer], sems.at[1 + (layer // 2) * 19 + q]
-                    )
-                )
-                copies[-1].start()
-    for side, ref, row, link, sign in (
-        (0, low, PAD - 1, 3, 1.0),
-        (1, high, PAD + width, 4, -1.0),
-    ):
+    for side, row, link, sign in ((0, PAD - 1, 3, 1.0), (1, PAD + width, 4, -1.0)):
         w = W7[link]
         for layer in range(3):
             kind, mineral, total, own = (
-                ref[3 * k + layer : 3 * k + layer + 1, :] for k in range(19, 23)
+                edges[side, 3 * k + layer : 3 * k + layer + 1, :] for k in range(19, 23)
             )
-            rate = jnp.full((1, LX), rates[0], jnp.float32)
-            goal = jnp.full((1, LX), target[0], jnp.float32)
-            for k in range(1, rates.shape[0]):
-                rate = jnp.where(mineral == float(k), rates[k], rate)
-                goal = jnp.where(mineral == float(k), target[k], goal)
+            kinds = table.shape[0] // 2
+            rate, goal = table[0:1, :], table[kinds : kinds + 1, :]
+            for k in range(1, kinds):
+                rate = jnp.where(mineral == float(k), table[k : k + 1, :], rate)
+                goal = jnp.where(mineral == float(k), table[kinds + k : kinds + k + 1, :], goal)
             reaction = jnp.where(kind == 2.0, -rate * (total - goal), 0.0)
             base = KEEP_S * own + (w * GAIN_S) * total + w * reaction
             slope = (sign * 4.0 * w * GAIN_S) * total
@@ -386,8 +395,6 @@
                 edge_part[1, at : at + 1, :] = my
                 edge_chem[0, at : at + 1, :] = base
                 edge_chem[1, at : at + 1, :] = slope
-    for copy in copies:
-        copy.wait()
 
 
 def relax_solute(s, total, reaction, inverse, momenta):
@@ -415,7 +422,7 @@
     middle_moved,
     across,
     on_chip,
-    flow_in,
+    inner_flow,
     flow,
     solute,
     faces,
@@ -425,11 +432,25 @@
     sbuf,
     sems,
 ):
-    del flow_in
     width = pop.shape[2]
     tiles = width // 8
     span = width + SPAN
     own = readers(moved, kept, mask)
+    early = []
+    for layer in (1, 0, 2):
+        local = [q for q in range(19) if 0 <= layer - LINKS[q][0] <= 2]
+        start = 0
+        while start < len(local):
+            stop = start
+            while stop + 1 < len(local) and local[stop + 1] == local[stop] + 1:
+                stop += 1
+            links = pl.ds(local[start], local[stop] - local[start] + 1)
+            copy = pltpu.make_async_copy(
+                inner_flow.at[links, layer], flow.at[links, layer], sems.at[len(early)]
+            )
+            copy.start()
+            early.append(copy)
+            start = stop + 1
 
     def body(above, below):
         def value(q, layer, row, count):
@@ -456,7 +477,7 @@
         copies = []
 
         def send(src, dst):
-            copies.append(pltpu.make_async_copy(src, dst, sems.at[len(copies)]))
+            copies.append(pltpu.make_async_copy(src, dst, sems.at[len(early) + len(copies)]))
             copies[-1].start()
 
         for side, ref, layer, outside, enter, leave in (
@@ -546,6 +567,8 @@
             copy.wait()
 
     by_parity(body, on_chip, across)
+    for copy in early:
+        copy.wait()
 
 
 VMEM = pl.BlockSpec(memory_space=pltpu.VMEM)
@@ -575,7 +598,7 @@
     cells = (populations, solute, pore_mask, mineral_ids)
     tables = (reaction_rates, saturation)
     gz, gy = lax.axis_size("gz"), lax.axis_size("gy")
-    edges = call(
+    first, second = call(
         pack_edges,
         tuple(pltpu.with_memory_space_constraint(v, pltpu.HBM) for v in cells),
         [HBM] * 4,
@@ -589,23 +612,44 @@
             DMA((2, 4)),
         ],
     )
-    low = lax.ppermute(edges[0], "gy", [(i, i + 1) for i in range(gy - 1)])
-    high = lax.ppermute(edges[1], "gy", [(i + 1, i) for i in range(gy - 1)])
+    def pairs(upward):
+        found = []
+        for place in range(gz * gy):
+            ends = (place, place + 1)
+            if ends[1] % gy:
+                found.append(ends if upward == (place < gz // 2 * gy) else ends[::-1])
+        return found
+
+    first = lax.ppermute(first, ("gz", "gy"), pairs(True))
+    second = lax.ppermute(second, ("gz", "gy"), pairs(False))
     whole = ((19, 3, padded, LX), VMEM)
     masks = ((3, 3, padded, LX), VMEM)
-    moved, kept, mask, chem = call(
+    moved, kept, mask, chem, table = call(
         relax_kernel,
         cells + tables,
         [VMEM] * 4 + [SMEM] * 2,
-        [whole, whole, masks, ((2, 3, width, LX), VMEM)],
+        [
+            whole,
+            whole,
+            masks,
+            ((2, 3, width, LX), VMEM),
+            ((2 * reaction_rates.shape[0], LX), VMEM),
+        ],
         flops=6_000_000,
     )
     rows = 9 * width + 6 * SPAN
-    moved, kept, mask, across, on_chip = call(
+    moved, kept, mask, across, on_chip, edges = call(
         face_kernel,
-        (moved, kept, mask, low, high, solute, chem),
+        (moved, kept, mask, first, second, solute, chem),
         [VMEM] * 7,
-        [whole, whole, masks, ((rows, LX), VMEM), ((rows, LX), VMEM)],
+        [
+            whole,
+            whole,
+            masks,
+            ((rows, LX), VMEM),
+            ((rows, LX), VMEM),
+            ((2, EDGE_ROWS, LX), VMEM),
+        ],
         [(2, 2, EDGE_ROWS, LX)],
         {0: 0, 1: 1, 2: 2},
     )
@@ -615,17 +659,16 @@
     on_chip = lax.ppermute(on_chip, "gz", [(i, i + 1 - 2 * (i % 2)) for i in range(gz)])
     flow, part, edge_part, edge_chem, middle, middle_moved = call(
         inner_kernel,
-        cells[:3] + (chem, moved, kept, mask, low, high) + tables,
-        [VMEM] * 9 + [SMEM] * 2,
+        (populations, solute, pore_mask, chem, moved, kept, mask, edges, table),
+        [VMEM] * 9,
         [
-            (populations.shape, ANY),
+            (populations.shape, VMEM),
             ((2, 4, width, LX), VMEM),
             ((2, 8, LX), VMEM),
             ((2, 8, LX), VMEM),
             ((7, padded, LX), VMEM),
             ((2, width, LX), VMEM),
         ],
-        [(19, 3, width, LX), DMA((39,))],
         flops=6_000_000,
     )
     return tuple(
@@ -634,7 +677,7 @@
             cells[:3]
             + (chem, moved, kept, mask, part, edge_part, edge_chem, middle, middle_moved)
             + (across, on_chip, flow),
-            [VMEM] * 14 + [ANY],
+            [VMEM] * 15,
             [(populations.shape, ANY), (solute.shape, ANY)],
             [
                 (7, 2, padded, LX),
@@ -642,9 +685,8 @@
                 (2, width, LX),
                 (2, 5, width, LX),
                 (7, 3, width, LX),
-                DMA((13,)),
+                DMA((26,)),
             ],
-            {14: 0},
         )
     )
 

time: 35.5 us -> 32.3 us (0.910)
  the two profiles are of different devices: /device:TPU:25 before, /device:TPU:33 now
where the time goes in v3:
time: 32.3 us; the launch traced here: 32.1 us
  starting transfers between devices  25.5 us (79%)
  Pallas kernels  5.13 us (16%)
  between operations  0.8 us (2%)
  waiting for transfers between devices  0.58 us (2%)
    ppermute x1, starting transfers between devices, on_device(): lax.ppermute(on_chip, 'gz', [(i, i + 1 - 2 * (i % 2)) for i in range(gz)])  14.4 us
    pallas_call x5, Pallas kernels, call(): pl.pallas_call(kernel, out_shape=[jax.ShapeDtypeStruct(s, jnp.float32) fo...  5.13 us
    ppermute x1, starting transfers between devices, on_device(): lax.ppermute(across, 'gz', [(i, (i + 1 if i % 2 else i - 1) % gz) for i i...  4.61 us
    ppermute x1, starting transfers between devices, on_device(): second = lax.ppermute(second, ('gz', 'gy'), pairs(False))  4.19 us
    ppermute x1, starting transfers between devices, on_device(): first = lax.ppermute(first, ('gz', 'gy'), pairs(True))  2.31 us
  transfers between devices with their start and end apart: 4, of which 1 were waited for; matrix products, arithmetic and copies ran while one was open for 0% of the time, Pallas kernels for 5%

profile of v3, /device:TPU:33, one launch (start us, length us, event | category | flops | bytes accessed | tf_op | source)
XLA Modules:
  0.0 32.1 jit_solution(16033483619149508165)
XLA Ops:
  0.6 0.0 copy-start.1
  0.6 0.0 copy-start.2
  0.7 0.0 copy-start
  0.7 0.0 copy-start.3
  0.7 0.0 copy-start.5
  0.7 0.0 copy-start.4
  0.7 1.6 %pack_edges.1 = (f32[88,128]{1,0:T(8,128)S(1)}, f32[88,128]{1,0:T(8,128)S(1)}) custom-call(f32[19,3,48,128]{3,2,1,0:T(8,128)} %pop.7, f32[7,3,48,128]{3,2,1,0:T(8,128)} %sol.9, s32[3,48,128]{2,1,0:T(8,128)} %pore.7, s32[3,48,128]{2,1,0:T(8,128)} %ids.3), custom_call_target="tpu_custom_call" | custom-call | flops 1000000 | bytes 1000000 | tf_op jit(solution)/shard_map/pack_edges/pallas_call | solution.py:582
  2.3 2.3 %collective-permute-start = (f32[88,128]{1,0:T(8,128)S(1)}, f32[88,128]{1,0:T(8,128)S(1)}, u32[]{:S(2)}, u32[]{:S(2)}) collective-permute-start(f32[88,128]{1,0:T(8,128)S(1)} %get-tuple-element.25), channel_id=1, source_target_pairs={{0,1},{1,2},{2,3},{3,4},{4,5},{5,6},{6,7},{8,9},{9,10},{10,11},{11... | collective-permute-start | bytes 135176 | tf_op jit(solution)/shard_map/ppermute | solution.py:623
  4.6 4.2 %collective-permute-start.1 = (f32[88,128]{1,0:T(8,128)S(1)}, f32[88,128]{1,0:T(8,128)S(1)}, u32[]{:S(2)}, u32[]{:S(2)}) collective-permute-start(f32[88,128]{1,0:T(8,128)S(1)} %get-tuple-element.26), channel_id=1, source_target_pairs={{1,0},{2,1},{3,2},{4,3},{5,4},{6,5},{7,6},{9,8},{10,9},{11,10},{12... | collective-permute-start | bytes 135176 | tf_op jit(solution)/shard_map/ppermute | solution.py:624
  8.8 0.0 copy-done.1
  8.8 0.0 copy-done.2
  8.8 0.0 copy-done
  8.8 0.0 copy-done.3
  8.8 0.0 copy-done.5
  8.9 0.0 copy-done.4
  8.9 1.2 %relax_kernel.1 = (f32[19,3,64,128]{3,2,1,0:T(8,128)S(1)}, f32[19,3,64,128]{3,2,1,0:T(8,128)S(1)}, f32[3,3,64,128]{3,2,1,0:T(8,128)S(1)}, f32[2,3,48,128]{3,2,1,0:T(8,128)S(1)}, f32[16,128]{1,0:T(8,128)S(1)}) custom-call(f32[19,3,48,128]{3,2,1,0:T(8,128)S(1)} %copy-done, f32[7,3,48,128]{3,2,1,0:T(8,128)S(1)} %copy-done.1, s32[3,48,128]{2,1,0:T(8,128)S(1)} %copy-done.2, ...), custom_call_target="tpu_custom_call" | custom-call | flops 6000000 | bytes 1000000 | tf_op jit(solution)/shard_map/relax_kernel/pallas_call | solution.py:582
  10.1 0.0 collective-permute-done.first
  10.1 0.0 collective-permute-done.1.second
  10.1 0.3 face_kernel.1
  10.4 4.6 %collective-permute-start.2 = (f32[456,128]{1,0:T(8,128)S(1)}, f32[456,128]{1,0:T(8,128)S(1)}, u32[]{:S(2)}, u32[]{:S(2)}) collective-permute-start(f32[456,128]{1,0:T(8,128)S(1)} %get-tuple-element.37), channel_id=1, source_target_pairs={{0,760},{8,16},{16,8},{24,32},{32,24},{40,48},{48,40},{56,64},{64,... | collective-permute-start | bytes 700424 | tf_op jit(solution)/shard_map/ppermute | solution.py:656
  15.0 14.4 %collective-permute-start.3 = (f32[456,128]{1,0:T(8,128)S(1)}, f32[456,128]{1,0:T(8,128)S(1)}, u32[]{:S(2)}, u32[]{:S(2)}) collective-permute-start(f32[456,128]{1,0:T(8,128)S(1)} %get-tuple-element.38), channel_id=1, source_target_pairs={{0,8},{8,0},{16,24},{24,16},{32,40},{40,32},{48,56},{56,48},{64,72... | collective-permute-start | bytes 700424 | tf_op jit(solution)/shard_map/ppermute | solution.py:659
  29.5 0.5 %inner_kernel.1 = (f32[19,3,48,128]{3,2,1,0:T(8,128)S(1)}, f32[2,4,48,128]{3,2,1,0:T(8,128)S(1)}, f32[2,8,128]{2,1,0:T(8,128)S(1)}, f32[2,8,128]{2,1,0:T(8,128)S...) custom-call(f32[19,3,48,128]{3,2,1,0:T(8,128)S(1)} %copy-done, f32[7,3,48,128]{3,2,1,0:T(8,128)S(1)} %copy-done.1, ...), custom_call_target="tpu_custom_call" | custom-call | flops 6000000 | bytes 1000000 | tf_op jit(solution)/shard_map/inner_kernel/pallas_call | solution.py:582
  30.0 0.0 collective-permute-done.2.across
  30.0 0.6 %collective-permute-done.3.on_chip = f32[456,128]{1,0:T(8,128)S(1)} collective-permute-done((f32[456,128]{1,0:T(8,128)S(1)}, f32[456,128]{1,0:T(8,128)S(1)}, u32[]{:S(2)}, u32[]{:S(2)}) %collective-permute-start.3) | collective-permute-done | bytes 233504 | tf_op jit(solution)/shard_map/ppermute | solution.py:659
  30.6 1.5 %outer_kernel.1 = (f32[19,3,48,128]{3,2,1,0:T(8,128)}, f32[7,3,48,128]{3,2,1,0:T(8,128)}) custom-call(f32[19,3,48,128]{3,2,1,0:T(8,128)S(1)} %copy-done, f32[7,3,48,128]{3,2,1,0:T(8,128)S(1)} %copy-done.1, s32[3,48,128]{2,1,0:T(8,128)S(1)} %copy-done.2, f32[2,3,48,128]{3,2,1,0:T(8,128)S(1)} %get-tuple-element.21.chem, ...), custom_call_target="tpu_custom_call" | custom-call | flops 1000000 | bytes 1000000 | tf_op jit(solution)/shard_map/outer_kernel/pallas_call | solution.py:582
Async XLA Ops:
  0.6 8.2 %copy-start.1 = (f32[7,3,48,128]{3,2,1,0:T(8,128)S(1)}, f32[7,3,48,128]{3,2,1,0:T(8,128)}, u32[]{:S(2)}) copy-start(f32[7,3,48,128]{3,2,1,0:T(8,128)} %sol.9) | copy-start | bytes 1548292
  0.6 8.2 %copy-start.2 = (s32[3,48,128]{2,1,0:T(8,128)S(1)}, s32[3,48,128]{2,1,0:T(8,128)}, u32[]{:S(2)}) copy-start(s32[3,48,128]{2,1,0:T(8,128)} %pore.7) | copy-start | bytes 221188
  0.7 8.2 %copy-start = (f32[19,3,48,128]{3,2,1,0:T(8,128)S(1)}, f32[19,3,48,128]{3,2,1,0:T(8,128)}, u32[]{:S(2)}) copy-start(f32[19,3,48,128]{3,2,1,0:T(8,128)} %pop.7) | copy-start | bytes 4202500
  0.7 8.2 %copy-start.3 = (s32[3,48,128]{2,1,0:T(8,128)S(1)}, s32[3,48,128]{2,1,0:T(8,128)}, u32[]{:S(2)}) copy-start(s32[3,48,128]{2,1,0:T(8,128)} %ids.3) | copy-start | bytes 221188
  0.7 8.2 %copy-start.5 = (f32[8]{0:T(128)S(1)}, f32[8]{0:T(128)}, u32[]{:S(2)}) copy-start(f32[8]{0:T(128)} %target.1) | copy-start | bytes 100
  0.7 8.2 %copy-start.4 = (f32[8]{0:T(128)S(1)}, f32[8]{0:T(128)}, u32[]{:S(2)}) copy-start(f32[8]{0:T(128)} %rates.1) | copy-start | bytes 100
  2.3 7.8 %collective-permute-start = (f32[88,128]{1,0:T(8,128)S(1)}, f32[88,128]{1,0:T(8,128)S(1)}, u32[]{:S(2)}, u32[]{:S(2)}) collective-permute-start(f32[88,128]{1,0:T(8,128)S(1)} %get-tuple-element.25), channel_id=1, source_target_pairs={{0,1},{1,2},{2,3},{3,4},{4,5},{5,6},{6,7},{8,9},{9,10},{10,11},{11... | collective-permute-start | bytes 135176 | tf_op jit(solution)/shard_map/ppermute | solution.py:623
  4.6 5.5 %collective-permute-start.1 = (f32[88,128]{1,0:T(8,128)S(1)}, f32[88,128]{1,0:T(8,128)S(1)}, u32[]{:S(2)}, u32[]{:S(2)}) collective-permute-start(f32[88,128]{1,0:T(8,128)S(1)} %get-tuple-element.26), channel_id=1, source_target_pairs={{1,0},{2,1},{3,2},{4,3},{5,4},{6,5},{7,6},{9,8},{10,9},{11,10},{12... | collective-permute-start | bytes 135176 | tf_op jit(solution)/shard_map/ppermute | solution.py:624
  10.4 19.6 %collective-permute-start.2 = (f32[456,128]{1,0:T(8,128)S(1)}, f32[456,128]{1,0:T(8,128)S(1)}, u32[]{:S(2)}, u32[]{:S(2)}) collective-permute-start(f32[456,128]{1,0:T(8,128)S(1)} %get-tuple-element.37), channel_id=1, source_target_pairs={{0,760},{8,16},{16,8},{24,32},{32,24},{40,48},{48,40},{56,64},{64,... | collective-permute-start | bytes 700424 | tf_op jit(solution)/shard_map/ppermute | solution.py:656
  15.0 15.5 %collective-permute-start.3 = (f32[456,128]{1,0:T(8,128)S(1)}, f32[456,128]{1,0:T(8,128)S(1)}, u32[]{:S(2)}, u32[]{:S(2)}) collective-permute-start(f32[456,128]{1,0:T(8,128)S(1)} %get-tuple-element.38), channel_id=1, source_target_pairs={{0,8},{8,0},{16,24},{24,16},{32,40},{40,32},{48,56},{56,48},{64,72... | collective-permute-start | bytes 700424 | tf_op jit(solution)/shard_map/ppermute | solution.py:659

commit v4 on v3

--- a/solution.py
+++ b/solution.py
@@ -82,15 +82,19 @@
     return out
 
 
-def solute_terms(s, pore, ids, rates_ref, target_ref):
+def pick(ids, table):
+    kinds = table.shape[0] // 2
+    rate, goal = table[0:1, :], table[kinds : kinds + 1, :]
+    for k in range(1, kinds):
+        rate = jnp.where(ids == k, table[k : k + 1, :], rate)
+        goal = jnp.where(ids == k, table[kinds + k : kinds + k + 1, :], goal)
+    return rate, goal
+
+
+def solute_terms(s, pore, ids, table):
     total = ((s[0] + s[1]) + (s[2] + s[3])) + ((s[4] + s[5]) + s[6])
-    rate = jnp.full(total.shape, rates_ref[0], jnp.float32)
-    target = jnp.full(total.shape, target_ref[0], jnp.float32)
-    for k in range(1, rates_ref.shape[0]):
-        rate = jnp.where(ids == k, rates_ref[k], rate)
-        target = jnp.where(ids == k, target_ref[k], target)
-    reaction = jnp.where(pore == 2, -rate * (total - target), 0.0)
-    return total, reaction
+    rate, goal = pick(ids, table)
+    return total, jnp.where(pore == 2, -rate * (total - goal), 0.0)
 
 
 def rolled(value, shift):
@@ -137,23 +141,44 @@
     either(even, lambda: body(first, second), lambda: body(second, first))
 
 
-def pack_edges(pop, sol, pore, ids, first, second, epop, esol, epore, eids, erel, sems):
+def pack_edges(
+    pop,
+    sol,
+    pore,
+    ids,
+    rates,
+    target,
+    first,
+    second,
+    table,
+    epop,
+    esol,
+    epore,
+    eids,
+    erel,
+    srates,
+    starget,
+    sems,
+):
     width = pop.shape[2]
-    copies = []
-    for side, start in ((0, width - 8), (1, 0)):
-        rows = pl.ds(start, 8)
-        for k, (src, dst) in enumerate(
-            (
-                (pop.at[:, :, rows, :], epop),
-                (sol.at[:, :, rows, :], esol),
-                (pore.at[:, rows, :], epore),
-                (ids.at[:, rows, :], eids),
-            )
+    for side, start, to in ((0, width - 2, 6), (1, 0, 0)):
+        rows, into = pl.ds(start, 2), pl.ds(to, 2)
+        for src, dst in (
+            (pop.at[:, :, rows, :], epop.at[side, :, :, into, :]),
+            (sol.at[:, :, rows, :], esol.at[side, :, :, into, :]),
+            (pore.at[:, rows, :], epore.at[side, :, into, :]),
+            (ids.at[:, rows, :], eids.at[side, :, into, :]),
         ):
-            copy = pltpu.make_async_copy(src, dst.at[side], sems.at[side, k])
-            copy.start()
-            copies.append(copy)
-    for copy in copies:
+            pltpu.make_async_copy(src, dst, sems.at[0]).start()
+    constants = [
+        pltpu.make_async_copy(rates, srates, sems.at[1]),
+        pltpu.make_async_copy(target, starget, sems.at[2]),
+    ]
+    for copy in constants:
+        copy.start()
+    every = erel.at[0, :, pl.ds(0, 14)]
+    pltpu.make_async_copy(every, every, sems.at[0]).wait()
+    for copy in constants:
         copy.wait()
     for side, link in ((0, 3), (1, 4)):
         for layer in range(3):
@@ -178,13 +203,14 @@
             out[EDGE_ROWS - 1 : EDGE_ROWS, :] = jnp.zeros((1, LX), jnp.float32)
 
     either(upper_half(), lambda: emit(second, first), lambda: emit(first, second))
-
-
-def relax_kernel(pop, sol, pore, ids, rates, target, moved, kept, mask, chem, table):
+    kinds = srates.shape[0]
+    for k in range(kinds):
+        for at, ref in ((k, srates), (k + kinds, starget)):
+            table[at : at + 1, :] = jnp.full((1, LX), ref[k], jnp.float32)
+
+
+def relax_kernel(pop, sol, pore, ids, table, moved, kept, mask, chem):
     width = pop.shape[2]
-    for k in range(rates.shape[0]):
-        for at, ref in ((k, rates), (k + rates.shape[0], target)):
-            table[at : at + 1, :] = jnp.full((1, LX), ref[k], jnp.float32)
     for layer in range(3):
         for t in range(width // 8):
             rows, into = slice(8 * t, 8 * t + 8), slice(PAD + 8 * t, PAD + 8 * t + 8)
@@ -199,7 +225,7 @@
             for ex in (0, 1, -1):
                 mask[ex % 3, layer, into, :] = rolled(m, ex)
             s = [sol[q, layer, rows, :] for q in range(7)]
-            total, reaction = solute_terms(s, kind, ids[layer, rows, :], rates, target)
+            total, reaction = solute_terms(s, kind, ids[layer, rows, :], table)
             chem[0, layer, rows, :] = total
             chem[1, layer, rows, :] = reaction
 
@@ -327,11 +353,14 @@
     edges,
     table,
     flow,
+    outer_flow,
     part,
     edge_part,
     edge_chem,
     middle,
     middle_moved,
+    buffer,
+    sem,
 ):
     width = pop.shape[2]
     tiles = width // 8
@@ -354,7 +383,11 @@
             rock = pore[layer, rows, :] == 0
             for q in range(19):
                 if 0 <= layer - LINKS[q][0] <= 2:
-                    flow[q, layer, rows, :] = jnp.where(rock, pop[q, layer, rows, :], f[q])
+                    v = jnp.where(rock, pop[q, layer, rows, :], f[q])
+                    if layer == 1:
+                        buffer[q, rows, :] = v
+                    else:
+                        outer_flow[q, layer // 2, rows, :] = v
             density, mz, my, mx = sums(f)
             if layer != 1:
                 for k, v in enumerate((density, mz, my, mx)):
@@ -372,17 +405,16 @@
                 middle[q, into, :] = relaxed[q]
             middle_moved[0, rows, :] = rolled(relaxed[5], 1)
             middle_moved[1, rows, :] = rolled(relaxed[6], -1)
+        if layer == 1:
+            copy = pltpu.make_async_copy(buffer, flow.at[:, 1], sem)
+            copy.start()
     for side, row, link, sign in ((0, PAD - 1, 3, 1.0), (1, PAD + width, 4, -1.0)):
         w = W7[link]
         for layer in range(3):
             kind, mineral, total, own = (
                 edges[side, 3 * k + layer : 3 * k + layer + 1, :] for k in range(19, 23)
             )
-            kinds = table.shape[0] // 2
-            rate, goal = table[0:1, :], table[kinds : kinds + 1, :]
-            for k in range(1, kinds):
-                rate = jnp.where(mineral == float(k), table[k : k + 1, :], rate)
-                goal = jnp.where(mineral == float(k), table[kinds + k : kinds + k + 1, :], goal)
+            rate, goal = pick(mineral, table)
             reaction = jnp.where(kind == 2.0, -rate * (total - goal), 0.0)
             base = KEEP_S * own + (w * GAIN_S) * total + w * reaction
             slope = (sign * 4.0 * w * GAIN_S) * total
@@ -395,6 +427,7 @@
                 edge_part[1, at : at + 1, :] = my
                 edge_chem[0, at : at + 1, :] = base
                 edge_chem[1, at : at + 1, :] = slope
+    copy.wait()
 
 
 def relax_solute(s, total, reaction, inverse, momenta):
@@ -422,7 +455,8 @@
     middle_moved,
     across,
     on_chip,
-    inner_flow,
+    outer_flow,
+    flow_in,
     flow,
     solute,
     faces,
@@ -432,12 +466,12 @@
     sbuf,
     sems,
 ):
+    del flow_in
     width = pop.shape[2]
     tiles = width // 8
     span = width + SPAN
     own = readers(moved, kept, mask)
-    early = []
-    for layer in (1, 0, 2):
+    for layer in (0, 2):
         local = [q for q in range(19) if 0 <= layer - LINKS[q][0] <= 2]
         start = 0
         while start < len(local):
@@ -445,11 +479,9 @@
             while stop + 1 < len(local) and local[stop + 1] == local[stop] + 1:
                 stop += 1
             links = pl.ds(local[start], local[stop] - local[start] + 1)
-            copy = pltpu.make_async_copy(
-                inner_flow.at[links, layer], flow.at[links, layer], sems.at[len(early)]
-            )
-            copy.start()
-            early.append(copy)
+            pltpu.make_async_copy(
+                outer_flow.at[links, layer // 2], flow.at[links, layer], sems.at[0]
+            ).start()
             start = stop + 1
 
     def body(above, below):
@@ -473,12 +505,6 @@
                 return own[2](ex, layer, row, count)
             at = 5 * span + row - PAD + 2
             return rolled((below if layer == -1 else above)[at : at + count, :], ex)
-
-        copies = []
-
-        def send(src, dst):
-            copies.append(pltpu.make_async_copy(src, dst, sems.at[len(early) + len(copies)]))
-            copies[-1].start()
 
         for side, ref, layer, outside, enter, leave in (
             (0, below, 0, -1, UP, DOWN),
@@ -522,7 +548,7 @@
                 )
                 cross_s[side, rows, :] = base + weight / (partial + back)
             for k, q in enumerate(enter):
-                send(fbuf.at[side, k], flow.at[q, layer])
+                pltpu.make_async_copy(fbuf.at[side, k], flow.at[q, layer], sems.at[0]).start()
             for end, row, link in ((0, PAD - 1, 3), (1, PAD + width, 4)):
                 at = 2 * end + side
                 line = slice(at, at + 1)
@@ -562,17 +588,14 @@
                         open_ = masks(ex, src, row - ey, 8) > 0.0
                         v = jnp.where(open_, v, solute_at(REVERSE[q], layer, row, 8))
                     sbuf[q, layer, rows, :] = jnp.where(rock, sol[q, layer, rows, :], v)
-            send(sbuf.at[:, layer], solute.at[:, layer])
-        for copy in copies:
-            copy.wait()
+            pltpu.make_async_copy(sbuf.at[:, layer], solute.at[:, layer], sems.at[1]).start()
 
     by_parity(body, on_chip, across)
-    for copy in early:
-        copy.wait()
+    pltpu.make_async_copy(outer_flow, flow.at[:, pl.ds(0, 2)], sems.at[0]).wait()
+    pltpu.make_async_copy(sbuf, solute, sems.at[1]).wait()
 
 
 VMEM = pl.BlockSpec(memory_space=pltpu.VMEM)
-SMEM = pl.BlockSpec(memory_space=pltpu.SMEM)
 ANY = pl.BlockSpec(memory_space=pl.ANY)
 HBM = pl.BlockSpec(memory_space=pltpu.HBM)
 DMA = pltpu.SemaphoreType.DMA
@@ -598,18 +621,21 @@
     cells = (populations, solute, pore_mask, mineral_ids)
     tables = (reaction_rates, saturation)
     gz, gy = lax.axis_size("gz"), lax.axis_size("gy")
-    first, second = call(
+    kinds = reaction_rates.shape
+    first, second, table = call(
         pack_edges,
-        tuple(pltpu.with_memory_space_constraint(v, pltpu.HBM) for v in cells),
-        [HBM] * 4,
-        [((EDGE_ROWS, LX), VMEM)] * 2,
+        tuple(pltpu.with_memory_space_constraint(v, pltpu.HBM) for v in cells + tables),
+        [HBM] * 6,
+        [((EDGE_ROWS, LX), VMEM)] * 2 + [((2 * kinds[0], LX), VMEM)],
         [
             (2, 19, 3, 8, LX),
             (2, 7, 3, 8, LX),
             pltpu.VMEM((2, 3, 8, LX), jnp.int32),
             pltpu.VMEM((2, 3, 8, LX), jnp.int32),
             (2, 3, NEAR, 8, LX),
-            DMA((2, 4)),
+            pltpu.SMEM(kinds, jnp.float32),
+            pltpu.SMEM(kinds, jnp.float32),
+            DMA((3,)),
         ],
     )
     def pairs(upward):
@@ -624,16 +650,15 @@
     second = lax.ppermute(second, ("gz", "gy"), pairs(False))
     whole = ((19, 3, padded, LX), VMEM)
     masks = ((3, 3, padded, LX), VMEM)
-    moved, kept, mask, chem, table = call(
+    moved, kept, mask, chem = call(
         relax_kernel,
-        cells + tables,
-        [VMEM] * 4 + [SMEM] * 2,
+        cells + (table,),
+        [VMEM] * 5,
         [
             whole,
             whole,
             masks,
             ((2, 3, width, LX), VMEM),
-            ((2 * reaction_rates.shape[0], LX), VMEM),
         ],
         flops=6_000_000,
     )
@@ -657,18 +682,20 @@
         across, "gz", [(i, (i + 1 if i % 2 else i - 1) % gz) for i in range(gz)]
     )
     on_chip = lax.ppermute(on_chip, "gz", [(i, i + 1 - 2 * (i % 2)) for i in range(gz)])
-    flow, part, edge_part, edge_chem, middle, middle_moved = call(
+    flow, outer_flow, part, edge_part, edge_chem, middle, middle_moved = call(
         inner_kernel,
         (populations, solute, pore_mask, chem, moved, kept, mask, edges, table),
         [VMEM] * 9,
         [
-            (populations.shape, VMEM),
+            (populations.shape, ANY),
+            ((19, 2, width, LX), VMEM),
             ((2, 4, width, LX), VMEM),
             ((2, 8, LX), VMEM),
             ((2, 8, LX), VMEM),
             ((7, padded, LX), VMEM),
             ((2, width, LX), VMEM),
         ],
+        [(19, width, LX), DMA],
         flops=6_000_000,
     )
     return tuple(
@@ -676,8 +703,8 @@
             outer_kernel,
             cells[:3]
             + (chem, moved, kept, mask, part, edge_part, edge_chem, middle, middle_moved)
-            + (across, on_chip, flow),
-            [VMEM] * 15,
+            + (across, on_chip, outer_flow, flow),
+            [VMEM] * 15 + [ANY],
             [(populations.shape, ANY), (solute.shape, ANY)],
             [
                 (7, 2, padded, LX),
@@ -685,8 +712,9 @@
                 (2, width, LX),
                 (2, 5, width, LX),
                 (7, 3, width, LX),
-                DMA((26,)),
+                DMA((2,)),
             ],
+            {15: 0},
         )
     )
 

time: 32.3 us -> 31.7 us (0.981)
  Pallas kernels: 5.13 us -> 4.47 us
    pallas_call x5, Pallas kernels: 5.13 us -> 4.47 us  [call(): pl.pallas_call(kernel, out_shape=[jax.ShapeDtypeStruct(s, jnp.float32) fo...]
    ppermute x1, waiting for transfers between devices: 0.57 us -> 0.06 us  [on_device(): lax.ppermute(on_chip, 'gz', [(i, i + 1 - 2 * (i % 2)) for i in range(gz)])]
    ppermute x1, waiting for transfers between devices: 0.01 us -> 0.39 us  [on_device(): second = lax.ppermute(second, ('gz', 'gy'), pairs(False))]
  transfers between devices with their start and end apart: 4 -> 4, of which waited for: 1 -> 2; matrix products, arithmetic and copies ran while one was open for 0% -> 0% of each run, Pallas kernels for 5% -> 5%
where the time goes in v4:
time: 31.7 us; the launch traced here: 31.5 us
  starting transfers between devices  25.8 us (81%)
  Pallas kernels  4.47 us (14%)
  between operations  0.76 us (2%)
  waiting for transfers between devices  0.46 us (1%)
    ppermute x1, starting transfers between devices, on_device(): lax.ppermute(on_chip, 'gz', [(i, i + 1 - 2 * (i % 2)) for i in range(gz)])  14.4 us
    ppermute x1, starting transfers between devices, on_device(): lax.ppermute(across, 'gz', [(i, (i + 1 if i % 2 else i - 1) % gz) for i i...  4.82 us
    pallas_call x5, Pallas kernels, call(): pl.pallas_call(kernel, out_shape=[jax.ShapeDtypeStruct(s, jnp.float32) fo...  4.47 us
    ppermute x1, starting transfers between devices, on_device(): second = lax.ppermute(second, ('gz', 'gy'), pairs(False))  4.19 us
    ppermute x1, starting transfers between devices, on_device(): first = lax.ppermute(first, ('gz', 'gy'), pairs(True))  2.31 us
  transfers between devices with their start and end apart: 4, of which 2 were waited for; matrix products, arithmetic and copies ran while one was open for 0% of the time, Pallas kernels for 5%

profile of v4, /device:TPU:33, one launch (start us, length us, event | category | flops | bytes accessed | tf_op | source)
XLA Modules:
  0.0 31.5 jit_solution(8838835823727212787)
XLA Ops:
  0.6 0.0 copy-start.1
  0.6 0.0 copy-start.2
  0.7 0.0 copy-start
  0.7 0.0 copy-start.3
  0.7 1.3 %pack_edges.1 = (f32[88,128]{1,0:T(8,128)S(1)}, f32[88,128]{1,0:T(8,128)S(1)}, f32[16,128]{1,0:T(8,128)S(1)}) custom-call(f32[19,3,48,128]{3,2,1,0:T(8,128)} %pop.7, f32[7,3,48,128]{3,2,1,0:T(8,128)} %sol.9, s32[3,48,128]{2,1,0:T(8,128)} %pore.7, s32[3,48,128]{2,1,0:T(8,128)} %ids.3, f32[8]{0:T(128)} %rates.1, f32[8]{0:T(128)} %target.1), custom_call_target="tpu_custom_call" | custom-call | flops 1000000 | bytes 1000000 | tf_op jit(solution)/shard_map/pack_edges/pallas_call | solution.py:605
  2.0 2.3 %collective-permute-start = (f32[88,128]{1,0:T(8,128)S(1)}, f32[88,128]{1,0:T(8,128)S(1)}, u32[]{:S(2)}, u32[]{:S(2)}) collective-permute-start(f32[88,128]{1,0:T(8,128)S(1)} %get-tuple-element.27), channel_id=1, source_target_pairs={{0,1},{1,2},{2,3},{3,4},{4,5},{5,6},{6,7},{8,9},{9,10},{10,11},{11... | collective-permute-start | bytes 135176 | tf_op jit(solution)/shard_map/ppermute | solution.py:649
  4.3 4.2 %collective-permute-start.1 = (f32[88,128]{1,0:T(8,128)S(1)}, f32[88,128]{1,0:T(8,128)S(1)}, u32[]{:S(2)}, u32[]{:S(2)}) collective-permute-start(f32[88,128]{1,0:T(8,128)S(1)} %get-tuple-element.28), channel_id=1, source_target_pairs={{1,0},{2,1},{3,2},{4,3},{5,4},{6,5},{7,6},{9,8},{10,9},{11,10},{12... | collective-permute-start | bytes 135176 | tf_op jit(solution)/shard_map/ppermute | solution.py:650
  8.5 0.0 copy-done.1
  8.5 0.0 copy-done.2
  8.5 0.0 copy-done
  8.5 0.0 copy-done.3
  8.5 0.7 %relax_kernel.1 = (f32[19,3,64,128]{3,2,1,0:T(8,128)S(1)}, f32[19,3,64,128]{3,2,1,0:T(8,128)S(1)}, f32[3,3,64,128]{3,2,1,0:T(8,128)S(1)}, f32[2,3,48,128]{3,2,1,0:T(8,128)S(1)}) custom-call(f32[19,3,48,128]{3,2,1,0:T(8,128)S(1)} %copy-done, f32[7,3,48,128]{3,2,1,0:T(8,128)S(1)} %copy-done.1, s32[3,48,128]{2,1,0:T(8,128)S(1)} %copy-done.2, ...), custom_call_target="tpu_custom_call" | custom-call | flops 6000000 | bytes 1000000 | tf_op jit(solution)/shard_map/relax_kernel/pallas_call | solution.py:605
  9.2 0.0 collective-permute-done.first
  9.2 0.4 %collective-permute-done.1.second = f32[88,128]{1,0:T(8,128)S(1)} collective-permute-done((f32[88,128]{1,0:T(8,128)S(1)}, f32[88,128]{1,0:T(8,128)S(1)}, u32[]{:S(2)}, u32[]{:S(2)}) %collective-permute-start.1) | collective-permute-done | bytes 45088 | tf_op jit(solution)/shard_map/ppermute | solution.py:650
  9.6 0.3 %face_kernel.1 = (f32[19,3,64,128]{3,2,1,0:T(8,128)S(1)}, f32[19,3,64,128]{3,2,1,0:T(8,128)S(1)}, f32[3,3,64,128]{3,2,1,0:T(8,128)S(1)}, f32[456,128]{1,0:T(8,12...) custom-call(f32[19,3,64,128]{3,2,1,0:T(8,128)S(1)} %get-tuple-elemen, ...), custom_call_target="tpu_custom_call", output_to_operand_aliasing={{0}: (0, {}), {1}: (1, {}), {2}: (2, {})} | custom-call | flops 1000000 | bytes 1000000 | tf_op jit(solution)/shard_map/face_kernel/pallas_call | solution.py:605
  9.9 4.8 %collective-permute-start.2 = (f32[456,128]{1,0:T(8,128)S(1)}, f32[456,128]{1,0:T(8,128)S(1)}, u32[]{:S(2)}, u32[]{:S(2)}) collective-permute-start(f32[456,128]{1,0:T(8,128)S(1)} %get-tuple-element.38), channel_id=1, source_target_pairs={{0,760},{8,16},{16,8},{24,32},{32,24},{40,48},{48,40},{56,64},{64,... | collective-permute-start | bytes 700424 | tf_op jit(solution)/shard_map/ppermute | solution.py:681
  14.8 14.4 %collective-permute-start.3 = (f32[456,128]{1,0:T(8,128)S(1)}, f32[456,128]{1,0:T(8,128)S(1)}, u32[]{:S(2)}, u32[]{:S(2)}) collective-permute-start(f32[456,128]{1,0:T(8,128)S(1)} %get-tuple-element.39), channel_id=1, source_target_pairs={{0,8},{8,0},{16,24},{24,16},{32,40},{40,32},{48,56},{56,48},{64,72... | collective-permute-start | bytes 700424 | tf_op jit(solution)/shard_map/ppermute | solution.py:684
  29.2 1.0 %inner_kernel.1 = (f32[19,3,48,128]{3,2,1,0:T(8,128)}, f32[19,2,48,128]{3,2,1,0:T(8,128)S(1)}, f32[2,4,48,128]{3,2,1,0:T(8,128)S(1)}, f32[2,8,128]{2,1,0:T(8,128...) custom-call(f32[19,3,48,128]{3,2,1,0:T(8,128)S(1)} %copy-done, ...), custom_call_target="tpu_custom_call" | custom-call | flops 6000000 | bytes 1000000 | tf_op jit(solution)/shard_map/inner_kernel/pallas_call | solution.py:605
  30.2 0.0 collective-permute-done.2.across
  30.2 0.1 collective-permute-done.3.on_chip
  30.3 1.2 %outer_kernel.1 = (f32[19,3,48,128]{3,2,1,0:T(8,128)}, f32[7,3,48,128]{3,2,1,0:T(8,128)}) custom-call(f32[19,3,48,128]{3,2,1,0:T(8,128)S(1)} %copy-done, f32[7,3,48,128]{3,2,1,0:T(8,128)S(1)} %copy-done.1, s32[3,48,128]{2,1,0:T(8,128)S(1)} %copy-done.2, f32[2,3,48,128]{3,2,1,0:T(8,128)S(1)} %get-tuple-element.23.chem, ...), custom_call_target="tpu_custom_call", output_to_operand_aliasing={{0}: (15, {})} | custom-call | flops 1000000 | bytes 1000000 | tf_op jit(solution)/shard_map/outer_kernel/pallas_call | solution.py:605
Async XLA Ops:
  0.6 7.9 %copy-start.1 = (f32[7,3,48,128]{3,2,1,0:T(8,128)S(1)}, f32[7,3,48,128]{3,2,1,0:T(8,128)}, u32[]{:S(2)}) copy-start(f32[7,3,48,128]{3,2,1,0:T(8,128)} %sol.9) | copy-start | bytes 1548292
  0.6 7.9 %copy-start.2 = (s32[3,48,128]{2,1,0:T(8,128)S(1)}, s32[3,48,128]{2,1,0:T(8,128)}, u32[]{:S(2)}) copy-start(s32[3,48,128]{2,1,0:T(8,128)} %pore.7) | copy-start | bytes 221188
  0.7 7.9 %copy-start = (f32[19,3,48,128]{3,2,1,0:T(8,128)S(1)}, f32[19,3,48,128]{3,2,1,0:T(8,128)}, u32[]{:S(2)}) copy-start(f32[19,3,48,128]{3,2,1,0:T(8,128)} %pop.7) | copy-start | bytes 4202500
  0.7 7.9 %copy-start.3 = (s32[3,48,128]{2,1,0:T(8,128)S(1)}, s32[3,48,128]{2,1,0:T(8,128)}, u32[]{:S(2)}) copy-start(s32[3,48,128]{2,1,0:T(8,128)} %ids.3) | copy-start | bytes 221188
  2.0 7.2 %collective-permute-start = (f32[88,128]{1,0:T(8,128)S(1)}, f32[88,128]{1,0:T(8,128)S(1)}, u32[]{:S(2)}, u32[]{:S(2)}) collective-permute-start(f32[88,128]{1,0:T(8,128)S(1)} %get-tuple-element.27), channel_id=1, source_target_pairs={{0,1},{1,2},{2,3},{3,4},{4,5},{5,6},{6,7},{8,9},{9,10},{10,11},{11... | collective-permute-start | bytes 135176 | tf_op jit(solution)/shard_map/ppermute | solution.py:649
  4.3 5.3 %collective-permute-start.1 = (f32[88,128]{1,0:T(8,128)S(1)}, f32[88,128]{1,0:T(8,128)S(1)}, u32[]{:S(2)}, u32[]{:S(2)}) collective-permute-start(f32[88,128]{1,0:T(8,128)S(1)} %get-tuple-element.28), channel_id=1, source_target_pairs={{1,0},{2,1},{3,2},{4,3},{5,4},{6,5},{7,6},{9,8},{10,9},{11,10},{12... | collective-permute-start | bytes 135176 | tf_op jit(solution)/shard_map/ppermute | solution.py:650
  9.9 20.3 %collective-permute-start.2 = (f32[456,128]{1,0:T(8,128)S(1)}, f32[456,128]{1,0:T(8,128)S(1)}, u32[]{:S(2)}, u32[]{:S(2)}) collective-permute-start(f32[456,128]{1,0:T(8,128)S(1)} %get-tuple-element.38), channel_id=1, source_target_pairs={{0,760},{8,16},{16,8},{24,32},{32,24},{40,48},{48,40},{56,64},{64,... | collective-permute-start | bytes 700424 | tf_op jit(solution)/shard_map/ppermute | solution.py:681
  14.8 15.5 %collective-permute-start.3 = (f32[456,128]{1,0:T(8,128)S(1)}, f32[456,128]{1,0:T(8,128)S(1)}, u32[]{:S(2)}, u32[]{:S(2)}) collective-permute-start(f32[456,128]{1,0:T(8,128)S(1)} %get-tuple-element.39), channel_id=1, source_target_pairs={{0,8},{8,0},{16,24},{24,16},{32,40},{40,32},{48,56},{56,48},{64,72... | collective-permute-start | bytes 700424 | tf_op jit(solution)/shard_map/ppermute | solution.py:684

commit v5 on v4

--- a/solution.py
+++ b/solution.py
@@ -209,108 +209,15 @@
             table[at : at + 1, :] = jnp.full((1, LX), ref[k], jnp.float32)
 
 
-def relax_kernel(pop, sol, pore, ids, table, moved, kept, mask, chem):
-    width = pop.shape[2]
-    for layer in range(3):
-        for t in range(width // 8):
-            rows, into = slice(8 * t, 8 * t + 8), slice(PAD + 8 * t, PAD + 8 * t + 8)
-            out = relax([pop[q, layer, rows, :] for q in range(19)])
-            for q in range(19):
-                ex = LINKS[q][2]
-                moved[q, layer, into, :] = rolled(out[q], ex)
-                if ex:
-                    kept[q, layer, into, :] = out[q]
-            kind = pore[layer, rows, :]
-            m = jnp.where(kind > 0, 1.0, 0.0)
-            for ex in (0, 1, -1):
-                mask[ex % 3, layer, into, :] = rolled(m, ex)
-            s = [sol[q, layer, rows, :] for q in range(7)]
-            total, reaction = solute_terms(s, kind, ids[layer, rows, :], table)
-            chem[0, layer, rows, :] = total
-            chem[1, layer, rows, :] = reaction
-
-
-def streamed(q, layer, row, count, shifted, plain, masks):
-    ez, ey, ex = LINKS[q]
-    value = shifted(q, layer - ez, row - ey, count)
-    if q == 0:
-        return value
-    open_ = masks(ex, layer - ez, row - ey, count) > 0.0
-    return jnp.where(open_, value, plain(REVERSE[q], layer, row, count))
-
-
-def readers(moved, kept, mask):
-    def shifted(q, layer, row, count):
-        return moved[q, layer, row : row + count, :]
-
-    def plain(q, layer, row, count):
-        return (kept if LINKS[q][2] else moved)[q, layer, row : row + count, :]
-
-    def masks(ex, layer, row, count):
-        return mask[ex % 3, layer, row : row + count, :]
-
-    return shifted, plain, masks
-
-
-def face_kernel(
-    moved_in,
-    kept_in,
-    mask_in,
-    first,
-    second,
-    sol,
-    chem,
-    moved,
-    kept,
-    mask,
-    across,
-    on_chip,
-    edges,
-    turned,
-):
-    del moved_in, kept_in, mask_in
+def face_payload(sol, chem, moved, kept, mask, across, on_chip, tiles, at_edges):
     width = sol.shape[2]
-    upper = upper_half()
-    for t in range(EDGE_ROWS // 8):
-        rows = slice(8 * t, 8 * t + 8)
-        for side, v in (
-            (0, jnp.where(upper, second[rows, :], first[rows, :])),
-            (1, jnp.where(upper, first[rows, :], second[rows, :])),
-        ):
-            edges[side, rows, :] = v
-            turned[side, 0, rows, :] = rolled(v, 1)
-            turned[side, 1, rows, :] = rolled(v, -1)
-    for side, near, far, sign in (
-        (0, PAD - 1, PAD - 2, 1),
-        (1, PAD + width, PAD + width + 1, -1),
-    ):
-
-        def line(at, ex):
-            if ex == 0:
-                return edges[side, at : at + 1, :]
-            return turned[side, 0 if ex == 1 else 1, at : at + 1, :]
-
-        for layer in range(3):
-            for row, start, links in (
-                (near, 0, tuple(range(19))),
-                (far, FAR_ROWS, toward(sign)),
-            ):
-                into = slice(row, row + 1)
-                for k, q in enumerate(links):
-                    at, ex = start + 3 * k + layer, LINKS[q][2]
-                    moved[q, layer, into, :] = line(at, ex)
-                    if ex:
-                        kept[q, layer, into, :] = line(at, 0)
-                at = start + 3 * len(links) + layer
-                for ex in (0, 1, -1):
-                    mask[ex % 3, layer, into, :] = line(at, ex)
+    span = width + SPAN
     shifted, plain, masks = readers(moved, kept, mask)
 
     def emit(up, down):
-        span = width + SPAN
         for out, layer, cross, link in ((up, 2, UP, 1), (down, 0, DOWN, 2)):
             w = W7[link]
-            for t in range(width // 8):
+            for t in tiles:
                 row, rows = PAD + 8 * t, slice(8 * t, 8 * t + 8)
                 get = functools.partial(
                     streamed,
@@ -330,16 +237,119 @@
                 for k, v in enumerate((base - slope, partial, slope * (partial + away))):
                     at = 6 * span + k * width + 8 * t
                     out[at : at + 8, :] = v
+            if at_edges:
+                pieces = [(PAD - 2, 2, 0), (PAD + width, 2, 2 + width)]
+            else:
+                pieces = [(PAD + 8 * t, 8, 2 + 8 * t) for t in range(width // 8)]
             for k in range(6):
-                at = k * span
-                pieces = [(PAD - 2, 2, 0)]
-                pieces += [(PAD + 8 * t, 8, 2 + 8 * t) for t in range(width // 8)]
-                pieces += [(PAD + width, 2, 2 + width)]
                 for row, count, to in pieces:
                     v = plain(cross[k], layer, row, count) if k < 5 else masks(0, layer, row, count)
-                    out[at + to : at + to + count, :] = v
+                    out[k * span + to : k * span + to + count, :] = v
 
     by_parity(emit, on_chip, across)
+
+
+def relax_kernel(pop, sol, pore, ids, table, moved, kept, mask, chem, across, on_chip):
+    width = pop.shape[2]
+    for layer in range(3):
+        for t in range(width // 8):
+            rows, into = slice(8 * t, 8 * t + 8), slice(PAD + 8 * t, PAD + 8 * t + 8)
+            out = relax([pop[q, layer, rows, :] for q in range(19)])
+            for q in range(19):
+                ex = LINKS[q][2]
+                moved[q, layer, into, :] = rolled(out[q], ex)
+                if ex:
+                    kept[q, layer, into, :] = out[q]
+            kind = pore[layer, rows, :]
+            m = jnp.where(kind > 0, 1.0, 0.0)
+            for ex in (0, 1, -1):
+                mask[ex % 3, layer, into, :] = rolled(m, ex)
+            s = [sol[q, layer, rows, :] for q in range(7)]
+            total, reaction = solute_terms(s, kind, ids[layer, rows, :], table)
+            chem[0, layer, rows, :] = total
+            chem[1, layer, rows, :] = reaction
+    face_payload(
+        sol, chem, moved, kept, mask, across, on_chip, range(1, width // 8 - 1), False
+    )
+
+
+def streamed(q, layer, row, count, shifted, plain, masks):
+    ez, ey, ex = LINKS[q]
+    value = shifted(q, layer - ez, row - ey, count)
+    if q == 0:
+        return value
+    open_ = masks(ex, layer - ez, row - ey, count) > 0.0
+    return jnp.where(open_, value, plain(REVERSE[q], layer, row, count))
+
+
+def readers(moved, kept, mask):
+    def shifted(q, layer, row, count):
+        return moved[q, layer, row : row + count, :]
+
+    def plain(q, layer, row, count):
+        return (kept if LINKS[q][2] else moved)[q, layer, row : row + count, :]
+
+    def masks(ex, layer, row, count):
+        return mask[ex % 3, layer, row : row + count, :]
+
+    return shifted, plain, masks
+
+
+def face_kernel(
+    moved_in,
+    kept_in,
+    mask_in,
+    across_in,
+    on_chip_in,
+    first,
+    second,
+    sol,
+    chem,
+    moved,
+    kept,
+    mask,
+    across,
+    on_chip,
+    edges,
+    turned,
+):
+    del moved_in, kept_in, mask_in, across_in, on_chip_in
+    width = sol.shape[2]
+    upper = upper_half()
+    for t in range(EDGE_ROWS // 8):
+        rows = slice(8 * t, 8 * t + 8)
+        for side, v in (
+            (0, jnp.where(upper, second[rows, :], first[rows, :])),
+            (1, jnp.where(upper, first[rows, :], second[rows, :])),
+        ):
+            edges[side, rows, :] = v
+            turned[side, 0, rows, :] = rolled(v, 1)
+            turned[side, 1, rows, :] = rolled(v, -1)
+    for side, near, far, sign in (
+        (0, PAD - 1, PAD - 2, 1),
+        (1, PAD + width, PAD + width + 1, -1),
+    ):
+
+        def line(at, ex):
+            if ex == 0:
+                return edges[side, at : at + 1, :]
+            return turned[side, 0 if ex == 1 else 1, at : at + 1, :]
+
+        for layer in range(3):
+            for row, start, links in (
+                (near, 0, tuple(range(19))),
+                (far, FAR_ROWS, toward(sign)),
+            ):
+                into = slice(row, row + 1)
+                for k, q in enumerate(links):
+                    at, ex = start + 3 * k + layer, LINKS[q][2]
+                    moved[q, layer, into, :] = line(at, ex)
+                    if ex:
+                        kept[q, layer, into, :] = line(at, 0)
+                at = start + 3 * len(links) + layer
+                for ex in (0, 1, -1):
+                    mask[ex % 3, layer, into, :] = line(at, ex)
+    face_payload(sol, chem, moved, kept, mask, across, on_chip, (0, width // 8 - 1), True)
 
 
 def inner_kernel(
@@ -648,9 +658,10 @@
 
     first = lax.ppermute(first, ("gz", "gy"), pairs(True))
     second = lax.ppermute(second, ("gz", "gy"), pairs(False))
+    rows = 9 * width + 6 * SPAN
     whole = ((19, 3, padded, LX), VMEM)
     masks = ((3, 3, padded, LX), VMEM)
-    moved, kept, mask, chem = call(
+    moved, kept, mask, chem, across, on_chip = call(
         relax_kernel,
         cells + (table,),
         [VMEM] * 5,
@@ -659,14 +670,15 @@
             whole,
             masks,
             ((2, 3, width, LX), VMEM),
+            ((rows, LX), VMEM),
+            ((rows, LX), VMEM),
         ],
         flops=6_000_000,
     )
-    rows = 9 * width + 6 * SPAN
     moved, kept, mask, across, on_chip, edges = call(
         face_kernel,
-        (moved, kept, mask, first, second, solute, chem),
-        [VMEM] * 7,
+        (moved, kept, mask, across, on_chip, first, second, solute, chem),
+        [VMEM] * 9,
         [
             whole,
             whole,
@@ -676,7 +688,7 @@
             ((2, EDGE_ROWS, LX), VMEM),
         ],
         [(2, 2, EDGE_ROWS, LX)],
-        {0: 0, 1: 1, 2: 2},
+        {k: k for k in range(5)},
     )
     across = lax.ppermute(
         across, "gz", [(i, (i + 1 if i % 2 else i - 1) % gz) for i in range(gz)]

time: 31.7 us -> 31.6 us (level)
  transfers between devices with their start and end apart: 4 -> 4, of which waited for: 2 -> 2; matrix products, arithmetic and copies ran while one was open for 0% -> 0% of each run, Pallas kernels for 5% -> 6%
where the time goes in v5:
time: 31.6 us; the launch traced here: 31.3 us
  starting transfers between devices  25.8 us (82%)
  Pallas kernels  4.48 us (14%)
  between operations  0.77 us (2%)
  waiting for transfers between devices  0.33 us (1%)
    ppermute x1, starting transfers between devices, on_device(): lax.ppermute(on_chip, 'gz', [(i, i + 1 - 2 * (i % 2)) for i in range(gz)])  14.4 us
    ppermute x1, starting transfers between devices, on_device(): lax.ppermute(across, 'gz', [(i, (i + 1 if i % 2 else i - 1) % gz) for i i...  4.82 us
    pallas_call x5, Pallas kernels, call(): pl.pallas_call(kernel, out_shape=[jax.ShapeDtypeStruct(s, jnp.float32) fo...  4.48 us
    ppermute x1, starting transfers between devices, on_device(): second = lax.ppermute(second, ('gz', 'gy'), pairs(False))  4.19 us
    ppermute x1, starting transfers between devices, on_device(): first = lax.ppermute(first, ('gz', 'gy'), pairs(True))  2.31 us
  transfers between devices with their start and end apart: 4, of which 2 were waited for; matrix products, arithmetic and copies ran while one was open for 0% of the time, Pallas kernels for 6%

profile of v5, /device:TPU:33, one launch (start us, length us, event | category | flops | bytes accessed | tf_op | source)
XLA Modules:
  0.0 31.3 jit_solution(17738562449641209031)
XLA Ops:
  0.6 0.0 copy-start.1
  0.6 0.0 copy-start.2
  0.7 0.0 copy-start
  0.7 0.0 copy-start.3
  0.7 1.3 %pack_edges.1 = (f32[88,128]{1,0:T(8,128)S(1)}, f32[88,128]{1,0:T(8,128)S(1)}, f32[16,128]{1,0:T(8,128)S(1)}) custom-call(f32[19,3,48,128]{3,2,1,0:T(8,128)} %pop.7, f32[7,3,48,128]{3,2,1,0:T(8,128)} %sol.9, s32[3,48,128]{2,1,0:T(8,128)} %pore.7, s32[3,48,128]{2,1,0:T(8,128)} %ids.3, f32[8]{0:T(128)} %rates.1, f32[8]{0:T(128)} %target.1), custom_call_target="tpu_custom_call" | custom-call | flops 1000000 | bytes 1000000 | tf_op jit(solution)/shard_map/pack_edges/pallas_call | solution.py:615
  2.0 2.3 %collective-permute-start = (f32[88,128]{1,0:T(8,128)S(1)}, f32[88,128]{1,0:T(8,128)S(1)}, u32[]{:S(2)}, u32[]{:S(2)}) collective-permute-start(f32[88,128]{1,0:T(8,128)S(1)} %get-tuple-element.31), channel_id=1, source_target_pairs={{0,1},{1,2},{2,3},{3,4},{4,5},{5,6},{6,7},{8,9},{9,10},{10,11},{11... | collective-permute-start | bytes 135176 | tf_op jit(solution)/shard_map/ppermute | solution.py:659
  4.3 4.2 %collective-permute-start.1 = (f32[88,128]{1,0:T(8,128)S(1)}, f32[88,128]{1,0:T(8,128)S(1)}, u32[]{:S(2)}, u32[]{:S(2)}) collective-permute-start(f32[88,128]{1,0:T(8,128)S(1)} %get-tuple-element.32), channel_id=1, source_target_pairs={{1,0},{2,1},{3,2},{4,3},{5,4},{6,5},{7,6},{9,8},{10,9},{11,10},{12... | collective-permute-start | bytes 135176 | tf_op jit(solution)/shard_map/ppermute | solution.py:660
  8.5 0.0 copy-done.1
  8.5 0.0 copy-done.2
  8.5 0.0 copy-done
  8.5 0.0 copy-done.3
  8.5 0.8 %relax_kernel.1 = (f32[19,3,64,128]{3,2,1,0:T(8,128)S(1)}, f32[19,3,64,128]{3,2,1,0:T(8,128)S(1)}, f32[3,3,64,128]{3,2,1,0:T(8,128)S(1)}, f32[2,3,48,128]{3,2,1,...) custom-call(f32[19,3,48,128]{3,2,1,0:T(8,128)S(1)} %copy-done, f32[7,3,48,128]{3,2,1,0:T(8,128)S(1)} %copy-done.1, ...), custom_call_target="tpu_custom_call" | custom-call | flops 6000000 | bytes 1000000 | tf_op jit(solution)/shard_map/relax_kernel/pallas_call | solution.py:615
  9.3 0.0 collective-permute-done.first
  9.4 0.3 collective-permute-done.1.second
  9.6 0.2 face_kernel.1
  9.8 4.8 %collective-permute-start.2 = (f32[456,128]{1,0:T(8,128)S(1)}, f32[456,128]{1,0:T(8,128)S(1)}, u32[]{:S(2)}, u32[]{:S(2)}) collective-permute-start(f32[456,128]{1,0:T(8,128)S(1)} %get-tuple-element.42), channel_id=1, source_target_pairs={{0,760},{8,16},{16,8},{24,32},{32,24},{40,48},{48,40},{56,64},{64,... | collective-permute-start | bytes 700424 | tf_op jit(solution)/shard_map/ppermute | solution.py:693
  14.6 14.4 %collective-permute-start.3 = (f32[456,128]{1,0:T(8,128)S(1)}, f32[456,128]{1,0:T(8,128)S(1)}, u32[]{:S(2)}, u32[]{:S(2)}) collective-permute-start(f32[456,128]{1,0:T(8,128)S(1)} %get-tuple-element.43), channel_id=1, source_target_pairs={{0,8},{8,0},{16,24},{24,16},{32,40},{40,32},{48,56},{56,48},{64,72... | collective-permute-start | bytes 700424 | tf_op jit(solution)/shard_map/ppermute | solution.py:696
  29.1 1.0 %inner_kernel.1 = (f32[19,3,48,128]{3,2,1,0:T(8,128)}, f32[19,2,48,128]{3,2,1,0:T(8,128)S(1)}, f32[2,4,48,128]{3,2,1,0:T(8,128)S(1)}, f32[2,8,128]{2,1,0:T(8,128...) custom-call(f32[19,3,48,128]{3,2,1,0:T(8,128)S(1)} %copy-done, ...), custom_call_target="tpu_custom_call" | custom-call | flops 6000000 | bytes 1000000 | tf_op jit(solution)/shard_map/inner_kernel/pallas_call | solution.py:615
  30.1 0.0 collective-permute-done.2.across
  30.1 0.1 collective-permute-done.3.on_chip
  30.2 1.2 %outer_kernel.1 = (f32[19,3,48,128]{3,2,1,0:T(8,128)}, f32[7,3,48,128]{3,2,1,0:T(8,128)}) custom-call(f32[19,3,48,128]{3,2,1,0:T(8,128)S(1)} %copy-done, f32[7,3,48,128]{3,2,1,0:T(8,128)S(1)} %copy-done.1, s32[3,48,128]{2,1,0:T(8,128)S(1)} %copy-done.2, f32[2,3,48,128]{3,2,1,0:T(8,128)S(1)} %get-tuple-element.25.chem, ...), custom_call_target="tpu_custom_call", output_to_operand_aliasing={{0}: (15, {})} | custom-call | flops 1000000 | bytes 1000000 | tf_op jit(solution)/shard_map/outer_kernel/pallas_call | solution.py:615
Async XLA Ops:
  0.6 7.9 %copy-start.1 = (f32[7,3,48,128]{3,2,1,0:T(8,128)S(1)}, f32[7,3,48,128]{3,2,1,0:T(8,128)}, u32[]{:S(2)}) copy-start(f32[7,3,48,128]{3,2,1,0:T(8,128)} %sol.9) | copy-start | bytes 1548292
  0.6 7.9 %copy-start.2 = (s32[3,48,128]{2,1,0:T(8,128)S(1)}, s32[3,48,128]{2,1,0:T(8,128)}, u32[]{:S(2)}) copy-start(s32[3,48,128]{2,1,0:T(8,128)} %pore.7) | copy-start | bytes 221188
  0.7 7.9 %copy-start = (f32[19,3,48,128]{3,2,1,0:T(8,128)S(1)}, f32[19,3,48,128]{3,2,1,0:T(8,128)}, u32[]{:S(2)}) copy-start(f32[19,3,48,128]{3,2,1,0:T(8,128)} %pop.7) | copy-start | bytes 4202500
  0.7 7.9 %copy-start.3 = (s32[3,48,128]{2,1,0:T(8,128)S(1)}, s32[3,48,128]{2,1,0:T(8,128)}, u32[]{:S(2)}) copy-start(s32[3,48,128]{2,1,0:T(8,128)} %ids.3) | copy-start | bytes 221188
  2.0 7.4 %collective-permute-start = (f32[88,128]{1,0:T(8,128)S(1)}, f32[88,128]{1,0:T(8,128)S(1)}, u32[]{:S(2)}, u32[]{:S(2)}) collective-permute-start(f32[88,128]{1,0:T(8,128)S(1)} %get-tuple-element.31), channel_id=1, source_target_pairs={{0,1},{1,2},{2,3},{3,4},{4,5},{5,6},{6,7},{8,9},{9,10},{10,11},{11... | collective-permute-start | bytes 135176 | tf_op jit(solution)/shard_map/ppermute | solution.py:659
  4.3 5.3 %collective-permute-start.1 = (f32[88,128]{1,0:T(8,128)S(1)}, f32[88,128]{1,0:T(8,128)S(1)}, u32[]{:S(2)}, u32[]{:S(2)}) collective-permute-start(f32[88,128]{1,0:T(8,128)S(1)} %get-tuple-element.32), channel_id=1, source_target_pairs={{1,0},{2,1},{3,2},{4,3},{5,4},{6,5},{7,6},{9,8},{10,9},{11,10},{12... | collective-permute-start | bytes 135176 | tf_op jit(solution)/shard_map/ppermute | solution.py:660
  9.8 20.3 %collective-permute-start.2 = (f32[456,128]{1,0:T(8,128)S(1)}, f32[456,128]{1,0:T(8,128)S(1)}, u32[]{:S(2)}, u32[]{:S(2)}) collective-permute-start(f32[456,128]{1,0:T(8,128)S(1)} %get-tuple-element.42), channel_id=1, source_target_pairs={{0,760},{8,16},{16,8},{24,32},{32,24},{40,48},{48,40},{56,64},{64,... | collective-permute-start | bytes 700424 | tf_op jit(solution)/shard_map/ppermute | solution.py:693
  14.6 15.5 %collective-permute-start.3 = (f32[456,128]{1,0:T(8,128)S(1)}, f32[456,128]{1,0:T(8,128)S(1)}, u32[]{:S(2)}, u32[]{:S(2)}) collective-permute-start(f32[456,128]{1,0:T(8,128)S(1)} %get-tuple-element.43), channel_id=1, source_target_pairs={{0,8},{8,0},{16,24},{24,16},{32,40},{40,32},{48,56},{56,48},{64,72... | collective-permute-start | bytes 700424 | tf_op jit(solution)/shard_map/ppermute | solution.py:696

commit v6 on v5

--- a/solution.py
+++ b/solution.py
@@ -44,7 +44,6 @@
 NEAR = 23
 FAR_ROWS = 3 * NEAR
 EDGE_ROWS = 88
-SPAN = 4
 
 
 def relax(p):
@@ -161,45 +160,47 @@
     sems,
 ):
     width = pop.shape[2]
-    for side, start, to in ((0, width - 2, 6), (1, 0, 0)):
-        rows, into = pl.ds(start, 2), pl.ds(to, 2)
-        for src, dst in (
-            (pop.at[:, :, rows, :], epop.at[side, :, :, into, :]),
-            (sol.at[:, :, rows, :], esol.at[side, :, :, into, :]),
-            (pore.at[:, rows, :], epore.at[side, :, into, :]),
-            (ids.at[:, rows, :], eids.at[side, :, into, :]),
-        ):
-            pltpu.make_async_copy(src, dst, sems.at[0]).start()
+    for side, start in ((0, width - 2), (1, 0)):
+        rows = pl.ds(start, 2)
+        for layer in range(3):
+            into = pl.ds(2 * layer, 2)
+            for src, dst in (
+                (pop.at[:, layer, rows, :], epop.at[side, :, into, :]),
+                (sol.at[:, layer, rows, :], esol.at[side, :, into, :]),
+                (pore.at[layer, rows, :], epore.at[side, into, :]),
+                (ids.at[layer, rows, :], eids.at[side, into, :]),
+            ):
+                pltpu.make_async_copy(src, dst, sems.at[0]).start()
     constants = [
         pltpu.make_async_copy(rates, srates, sems.at[1]),
         pltpu.make_async_copy(target, starget, sems.at[2]),
     ]
     for copy in constants:
         copy.start()
-    every = erel.at[0, :, pl.ds(0, 14)]
+    every = erel.at[:, pl.ds(0, 21)]
     pltpu.make_async_copy(every, every, sems.at[0]).wait()
     for copy in constants:
         copy.wait()
     for side, link in ((0, 3), (1, 4)):
-        for layer in range(3):
-            rel = relax([epop[side, q, layer] for q in range(19)])
-            for q in range(19):
-                erel[side, layer, q] = rel[q]
-            kind = epore[side, layer].astype(jnp.float32)
-            erel[side, layer, 19] = kind
-            erel[side, layer, 20] = eids[side, layer].astype(jnp.float32)
-            erel[side, layer, 21] = add_all(esol[side, q, layer] for q in range(7))
-            erel[side, layer, 22] = esol[side, link, layer]
+        rel = relax([epop[side, q] for q in range(19)])
+        for q in range(19):
+            erel[side, q] = rel[q]
+        erel[side, 19] = epore[side].astype(jnp.float32)
+        erel[side, 20] = eids[side].astype(jnp.float32)
+        erel[side, 21] = add_all(esol[side, q] for q in range(7))
+        erel[side, 22] = esol[side, link]
 
     def emit(up, down):
-        for side, out, near, far, sign in ((0, up, 7, 6, 1), (1, down, 0, 1, -1)):
+        for side, out, near, far, sign in ((0, up, 1, 0, 1), (1, down, 0, 1, -1)):
             for layer in range(3):
+                row = 2 * layer + near
                 for k in range(NEAR):
                     at = 3 * k + layer
-                    out[at : at + 1, :] = erel[side, layer, k, near : near + 1, :]
+                    out[at : at + 1, :] = erel[side, k, row : row + 1, :]
+                row = 2 * layer + far
                 for k, q in enumerate(toward(sign) + (19,)):
                     at = FAR_ROWS + 3 * k + layer
-                    out[at : at + 1, :] = erel[side, layer, q, far : far + 1, :]
+                    out[at : at + 1, :] = erel[side, q, row : row + 1, :]
             out[EDGE_ROWS - 1 : EDGE_ROWS, :] = jnp.zeros((1, LX), jnp.float32)
 
     either(upper_half(), lambda: emit(second, first), lambda: emit(first, second))
@@ -209,9 +210,18 @@
             table[at : at + 1, :] = jnp.full((1, LX), ref[k], jnp.float32)
 
 
+def place(k, links, row, width):
+    if k == 5:
+        return 5 * (width + 2) + row - (PAD - 2)
+    return k * (width + 2) + row - (PAD - 1 - LINKS[links[k]][1])
+
+
+def field(k, row, width):
+    return 6 * width + 14 + k * width + row - PAD
+
+
 def face_payload(sol, chem, moved, kept, mask, across, on_chip, tiles, at_edges):
     width = sol.shape[2]
-    span = width + SPAN
     shifted, plain, masks = readers(moved, kept, mask)
 
     def emit(up, down):
@@ -235,16 +245,20 @@
                 slope = (4.0 * w * GAIN_S) * total
                 base = KEEP_S * sol[link, layer, rows, :] + (w * GAIN_S) * total + w * reaction
                 for k, v in enumerate((base - slope, partial, slope * (partial + away))):
-                    at = 6 * span + k * width + 8 * t
+                    at = field(k, row, width)
                     out[at : at + 8, :] = v
-            if at_edges:
-                pieces = [(PAD - 2, 2, 0), (PAD + width, 2, 2 + width)]
-            else:
-                pieces = [(PAD + 8 * t, 8, 2 + 8 * t) for t in range(width // 8)]
             for k in range(6):
-                for row, count, to in pieces:
-                    v = plain(cross[k], layer, row, count) if k < 5 else masks(0, layer, row, count)
-                    out[k * span + to : k * span + to + count, :] = v
+                ey = LINKS[cross[k]][1] if k < 5 else 0
+                extra = 2 if k == 5 else 1
+                below, above = extra + ey, extra - ey
+                pieces = [(PAD + 8 * t, 8) for t in range(width // 8)]
+                if at_edges:
+                    pieces = [(PAD - below, below), (PAD + width, above)]
+                for row, count in pieces:
+                    if count:
+                        at = place(k, cross, row, width)
+                        v = plain(cross[k], layer, row, count) if k < 5 else masks(0, layer, row, count)
+                        out[at : at + count, :] = v
 
     by_parity(emit, on_chip, across)
 
@@ -370,7 +384,7 @@
     middle,
     middle_moved,
     buffer,
-    sem,
+    sems,
 ):
     width = pop.shape[2]
     tiles = width // 8
@@ -386,6 +400,7 @@
             for q in range(19)
         ]
 
+    copies = []
     for layer in (1, 0, 2):
         for t in range(tiles):
             row, rows = PAD + 8 * t, slice(8 * t, 8 * t + 8)
@@ -415,9 +430,15 @@
                 middle[q, into, :] = relaxed[q]
             middle_moved[0, rows, :] = rolled(relaxed[5], 1)
             middle_moved[1, rows, :] = rolled(relaxed[6], -1)
-        if layer == 1:
-            copy = pltpu.make_async_copy(buffer, flow.at[:, 1], sem)
-            copy.start()
+            if t + 1 in (tiles // 2, tiles):
+                half = len(copies)
+                part_rows = pl.ds(half * (tiles // 2) * 8, (t + 1) * 8 - half * (tiles // 2) * 8)
+                copies.append(
+                    pltpu.make_async_copy(
+                        buffer.at[:, part_rows, :], flow.at[:, 1, part_rows, :], sems.at[half]
+                    )
+                )
+                copies[-1].start()
     for side, row, link, sign in ((0, PAD - 1, 3, 1.0), (1, PAD + width, 4, -1.0)):
         w = W7[link]
         for layer in range(3):
@@ -437,7 +458,8 @@
                 edge_part[1, at : at + 1, :] = my
                 edge_chem[0, at : at + 1, :] = base
                 edge_chem[1, at : at + 1, :] = slope
-    copy.wait()
+    for copy in copies:
+        copy.wait()
 
 
 def relax_solute(s, total, reaction, inverse, momenta):
@@ -479,7 +501,6 @@
     del flow_in
     width = pop.shape[2]
     tiles = width // 8
-    span = width + SPAN
     own = readers(moved, kept, mask)
     for layer in (0, 2):
         local = [q for q in range(19) if 0 <= layer - LINKS[q][0] <= 2]
@@ -497,7 +518,7 @@
     def body(above, below):
         def value(q, layer, row, count):
             ref, links = (below, UP) if layer == -1 else (above, DOWN)
-            at = links.index(q) * span + row - PAD + 2
+            at = place(links.index(q), links, row, width)
             return ref[at : at + count, :]
 
         def shifted(q, layer, row, count):
@@ -513,8 +534,36 @@
         def masks(ex, layer, row, count):
             if 0 <= layer <= 2:
                 return own[2](ex, layer, row, count)
-            at = 5 * span + row - PAD + 2
+            at = place(5, UP, row, width)
             return rolled((below if layer == -1 else above)[at : at + count, :], ex)
+
+        def solute_at(q, layer, row, count):
+            if layer == 1:
+                return middle[q, row : row + count, :]
+            return faces[q, layer // 2, row : row + count, :]
+
+        def finish(layer):
+            for t in range(tiles):
+                row, rows = PAD + 8 * t, slice(8 * t, 8 * t + 8)
+                rock = pore[layer, rows, :] == 0
+                for q in range(7):
+                    ez, ey, ex = LINKS[q]
+                    src = layer - ez
+                    if src == -1:
+                        v = cross_s[0, rows, :]
+                    elif src == 3:
+                        v = cross_s[1, rows, :]
+                    elif ex and layer == 1:
+                        v = middle_moved[q - 5, rows, :]
+                    elif ex:
+                        v = faces_moved[q - 5, layer // 2, rows, :]
+                    else:
+                        v = solute_at(q, src, row - ey, 8)
+                    if q:
+                        open_ = masks(ex, src, row - ey, 8) > 0.0
+                        v = jnp.where(open_, v, solute_at(REVERSE[q], layer, row, 8))
+                    sbuf[q, layer, rows, :] = jnp.where(rock, sol[q, layer, rows, :], v)
+            pltpu.make_async_copy(sbuf.at[:, layer], solute.at[:, layer], sems.at[1]).start()
 
         for side, ref, layer, outside, enter, leave in (
             (0, below, 0, -1, UP, DOWN),
@@ -553,8 +602,7 @@
                     streamed(q, outside, row, 8, shifted, plain, masks) for q in leave
                 )
                 base, partial, weight = (
-                    ref[6 * span + k * width + 8 * t : 6 * span + k * width + 8 * t + 8, :]
-                    for k in range(3)
+                    ref[field(k, row, width) : field(k, row, width) + 8, :] for k in range(3)
                 )
                 cross_s[side, rows, :] = base + weight / (partial + back)
             for k, q in enumerate(enter):
@@ -571,34 +619,8 @@
                 faces[link, side, row : row + 1, :] = edge_chem[0, line, :] + edge_chem[
                     1, line, :
                 ] * (my / density)
-
-        def solute_at(q, layer, row, count):
-            if layer == 1:
-                return middle[q, row : row + count, :]
-            return faces[q, layer // 2, row : row + count, :]
-
-        for layer in (1, 0, 2):
-            for t in range(tiles):
-                row, rows = PAD + 8 * t, slice(8 * t, 8 * t + 8)
-                rock = pore[layer, rows, :] == 0
-                for q in range(7):
-                    ez, ey, ex = LINKS[q]
-                    src = layer - ez
-                    if src == -1:
-                        v = cross_s[0, rows, :]
-                    elif src == 3:
-                        v = cross_s[1, rows, :]
-                    elif ex and layer == 1:
-                        v = middle_moved[q - 5, rows, :]
-                    elif ex:
-                        v = faces_moved[q - 5, layer // 2, rows, :]
-                    else:
-                        v = solute_at(q, src, row - ey, 8)
-                    if q:
-                        open_ = masks(ex, src, row - ey, 8) > 0.0
-                        v = jnp.where(open_, v, solute_at(REVERSE[q], layer, row, 8))
-                    sbuf[q, layer, rows, :] = jnp.where(rock, sol[q, layer, rows, :], v)
-            pltpu.make_async_copy(sbuf.at[:, layer], solute.at[:, layer], sems.at[1]).start()
+            finish(layer)
+        finish(1)
 
     by_parity(body, on_chip, across)
     pltpu.make_async_copy(outer_flow, flow.at[:, pl.ds(0, 2)], sems.at[0]).wait()
@@ -638,11 +660,11 @@
         [HBM] * 6,
         [((EDGE_ROWS, LX), VMEM)] * 2 + [((2 * kinds[0], LX), VMEM)],
         [
-            (2, 19, 3, 8, LX),
-            (2, 7, 3, 8, LX),
-            pltpu.VMEM((2, 3, 8, LX), jnp.int32),
-            pltpu.VMEM((2, 3, 8, LX), jnp.int32),
-            (2, 3, NEAR, 8, LX),
+            (2, 19, 8, LX),
+            (2, 7, 8, LX),
+            pltpu.VMEM((2, 8, LX), jnp.int32),
+            pltpu.VMEM((2, 8, LX), jnp.int32),
+            (2, NEAR, 8, LX),
             pltpu.SMEM(kinds, jnp.float32),
             pltpu.SMEM(kinds, jnp.float32),
             DMA((3,)),
@@ -658,7 +680,7 @@
 
     first = lax.ppermute(first, ("gz", "gy"), pairs(True))
     second = lax.ppermute(second, ("gz", "gy"), pairs(False))
-    rows = 9 * width + 6 * SPAN
+    rows = 9 * width + 16
     whole = ((19, 3, padded, LX), VMEM)
     masks = ((3, 3, padded, LX), VMEM)
     moved, kept, mask, chem, across, on_chip = call(
@@ -707,7 +729,7 @@
             ((7, padded, LX), VMEM),
             ((2, width, LX), VMEM),
         ],
-        [(19, width, LX), DMA],
+        [(19, width, LX), DMA((2,))],
         flops=6_000_000,
     )
     return tuple(

time: 31.6 us -> 31.4 us (level)
  no operation moved by 1% of the time
where the time goes in v6:
time: 31.4 us; the launch traced here: 31.2 us
  starting transfers between devices  25.8 us (82%)
  Pallas kernels  4.31 us (14%)
  between operations  0.77 us (2%)
  waiting for transfers between devices  0.36 us (1%)
    ppermute x1, starting transfers between devices, on_device(): lax.ppermute(on_chip, 'gz', [(i, i + 1 - 2 * (i % 2)) for i in range(gz)])  14.4 us
    ppermute x1, starting transfers between devices, on_device(): lax.ppermute(across, 'gz', [(i, (i + 1 if i % 2 else i - 1) % gz) for i i...  4.82 us
    pallas_call x5, Pallas kernels, call(): pl.pallas_call(kernel, out_shape=[jax.ShapeDtypeStruct(s, jnp.float32) fo...  4.31 us
    ppermute x1, starting transfers between devices, on_device(): second = lax.ppermute(second, ('gz', 'gy'), pairs(False))  4.19 us
    ppermute x1, starting transfers between devices, on_device(): first = lax.ppermute(first, ('gz', 'gy'), pairs(True))  2.31 us
  transfers between devices with their start and end apart: 4, of which 2 were waited for; matrix products, arithmetic and copies ran while one was open for 0% of the time, Pallas kernels for 6%

profile of v6, /device:TPU:33, one launch (start us, length us, event | category | flops | bytes accessed | tf_op | source)
XLA Modules:
  0.0 31.2 jit_solution(14342063084931318319)
XLA Ops:
  0.6 0.0 copy-start.1
  0.6 0.0 copy-start.2
  0.7 0.0 copy-start
  0.7 0.0 copy-start.3
  0.7 1.2 %pack_edges.1 = (f32[88,128]{1,0:T(8,128)S(1)}, f32[88,128]{1,0:T(8,128)S(1)}, f32[16,128]{1,0:T(8,128)S(1)}) custom-call(f32[19,3,48,128]{3,2,1,0:T(8,128)} %pop.7, f32[7,3,48,128]{3,2,1,0:T(8,128)} %sol.9, s32[3,48,128]{2,1,0:T(8,128)} %pore.7, s32[3,48,128]{2,1,0:T(8,128)} %ids.3, f32[8]{0:T(128)} %rates.1, f32[8]{0:T(128)} %target.1), custom_call_target="tpu_custom_call" | custom-call | flops 1000000 | bytes 1000000 | tf_op jit(solution)/shard_map/pack_edges/pallas_call | solution.py:637
  1.9 2.3 %collective-permute-start = (f32[88,128]{1,0:T(8,128)S(1)}, f32[88,128]{1,0:T(8,128)S(1)}, u32[]{:S(2)}, u32[]{:S(2)}) collective-permute-start(f32[88,128]{1,0:T(8,128)S(1)} %get-tuple-element.31), channel_id=1, source_target_pairs={{0,1},{1,2},{2,3},{3,4},{4,5},{5,6},{6,7},{8,9},{9,10},{10,11},{11... | collective-permute-start | bytes 135176 | tf_op jit(solution)/shard_map/ppermute | solution.py:681
  4.2 4.2 %collective-permute-start.1 = (f32[88,128]{1,0:T(8,128)S(1)}, f32[88,128]{1,0:T(8,128)S(1)}, u32[]{:S(2)}, u32[]{:S(2)}) collective-permute-start(f32[88,128]{1,0:T(8,128)S(1)} %get-tuple-element.32), channel_id=1, source_target_pairs={{1,0},{2,1},{3,2},{4,3},{5,4},{6,5},{7,6},{9,8},{10,9},{11,10},{12... | collective-permute-start | bytes 135176 | tf_op jit(solution)/shard_map/ppermute | solution.py:682
  8.4 0.0 copy-done.1
  8.4 0.0 copy-done.2
  8.4 0.0 copy-done
  8.4 0.0 copy-done.3
  8.4 0.8 %relax_kernel.1 = (f32[19,3,64,128]{3,2,1,0:T(8,128)S(1)}, f32[19,3,64,128]{3,2,1,0:T(8,128)S(1)}, f32[3,3,64,128]{3,2,1,0:T(8,128)S(1)}, f32[2,3,48,128]{3,2,1,...) custom-call(f32[19,3,48,128]{3,2,1,0:T(8,128)S(1)} %copy-done, f32[7,3,48,128]{3,2,1,0:T(8,128)S(1)} %copy-done.1, ...), custom_call_target="tpu_custom_call" | custom-call | flops 6000000 | bytes 1000000 | tf_op jit(solution)/shard_map/relax_kernel/pallas_call | solution.py:637
  9.2 0.0 collective-permute-done.first
  9.2 0.3 collective-permute-done.1.second
  9.5 0.2 face_kernel.1
  9.7 4.8 %collective-permute-start.2 = (f32[448,128]{1,0:T(8,128)S(1)}, f32[448,128]{1,0:T(8,128)S(1)}, u32[]{:S(2)}, u32[]{:S(2)}) collective-permute-start(f32[448,128]{1,0:T(8,128)S(1)} %get-tuple-element.42), channel_id=1, source_target_pairs={{0,760},{8,16},{16,8},{24,32},{32,24},{40,48},{48,40},{56,64},{64,... | collective-permute-start | bytes 688136 | tf_op jit(solution)/shard_map/ppermute | solution.py:715
  14.5 14.4 %collective-permute-start.3 = (f32[448,128]{1,0:T(8,128)S(1)}, f32[448,128]{1,0:T(8,128)S(1)}, u32[]{:S(2)}, u32[]{:S(2)}) collective-permute-start(f32[448,128]{1,0:T(8,128)S(1)} %get-tuple-element.43), channel_id=1, source_target_pairs={{0,8},{8,0},{16,24},{24,16},{32,40},{40,32},{48,56},{56,48},{64,72... | collective-permute-start | bytes 688136 | tf_op jit(solution)/shard_map/ppermute | solution.py:718
  29.0 1.0 %inner_kernel.1 = (f32[19,3,48,128]{3,2,1,0:T(8,128)}, f32[19,2,48,128]{3,2,1,0:T(8,128)S(1)}, f32[2,4,48,128]{3,2,1,0:T(8,128)S(1)}, f32[2,8,128]{2,1,0:T(8,128...) custom-call(f32[19,3,48,128]{3,2,1,0:T(8,128)S(1)} %copy-done, ...), custom_call_target="tpu_custom_call" | custom-call | flops 6000000 | bytes 1000000 | tf_op jit(solution)/shard_map/inner_kernel/pallas_call | solution.py:637
  29.9 0.0 collective-permute-done.2.across
  30.0 0.1 collective-permute-done.3.on_chip
  30.1 1.1 %outer_kernel.1 = (f32[19,3,48,128]{3,2,1,0:T(8,128)}, f32[7,3,48,128]{3,2,1,0:T(8,128)}) custom-call(f32[19,3,48,128]{3,2,1,0:T(8,128)S(1)} %copy-done, f32[7,3,48,128]{3,2,1,0:T(8,128)S(1)} %copy-done.1, s32[3,48,128]{2,1,0:T(8,128)S(1)} %copy-done.2, f32[2,3,48,128]{3,2,1,0:T(8,128)S(1)} %get-tuple-element.25.chem, ...), custom_call_target="tpu_custom_call", output_to_operand_aliasing={{0}: (15, {})} | custom-call | flops 1000000 | bytes 1000000 | tf_op jit(solution)/shard_map/outer_kernel/pallas_call | solution.py:637
Async XLA Ops:
  0.6 7.7 %copy-start.1 = (f32[7,3,48,128]{3,2,1,0:T(8,128)S(1)}, f32[7,3,48,128]{3,2,1,0:T(8,128)}, u32[]{:S(2)}) copy-start(f32[7,3,48,128]{3,2,1,0:T(8,128)} %sol.9) | copy-start | bytes 1548292
  0.6 7.7 %copy-start.2 = (s32[3,48,128]{2,1,0:T(8,128)S(1)}, s32[3,48,128]{2,1,0:T(8,128)}, u32[]{:S(2)}) copy-start(s32[3,48,128]{2,1,0:T(8,128)} %pore.7) | copy-start | bytes 221188
  0.7 7.7 %copy-start = (f32[19,3,48,128]{3,2,1,0:T(8,128)S(1)}, f32[19,3,48,128]{3,2,1,0:T(8,128)}, u32[]{:S(2)}) copy-start(f32[19,3,48,128]{3,2,1,0:T(8,128)} %pop.7) | copy-start | bytes 4202500
  0.7 7.7 %copy-start.3 = (s32[3,48,128]{2,1,0:T(8,128)S(1)}, s32[3,48,128]{2,1,0:T(8,128)}, u32[]{:S(2)}) copy-start(s32[3,48,128]{2,1,0:T(8,128)} %ids.3) | copy-start | bytes 221188
  1.9 7.4 %collective-permute-start = (f32[88,128]{1,0:T(8,128)S(1)}, f32[88,128]{1,0:T(8,128)S(1)}, u32[]{:S(2)}, u32[]{:S(2)}) collective-permute-start(f32[88,128]{1,0:T(8,128)S(1)} %get-tuple-element.31), channel_id=1, source_target_pairs={{0,1},{1,2},{2,3},{3,4},{4,5},{5,6},{6,7},{8,9},{9,10},{10,11},{11... | collective-permute-start | bytes 135176 | tf_op jit(solution)/shard_map/ppermute | solution.py:681
  4.2 5.3 %collective-permute-start.1 = (f32[88,128]{1,0:T(8,128)S(1)}, f32[88,128]{1,0:T(8,128)S(1)}, u32[]{:S(2)}, u32[]{:S(2)}) collective-permute-start(f32[88,128]{1,0:T(8,128)S(1)} %get-tuple-element.32), channel_id=1, source_target_pairs={{1,0},{2,1},{3,2},{4,3},{5,4},{6,5},{7,6},{9,8},{10,9},{11,10},{12... | collective-permute-start | bytes 135176 | tf_op jit(solution)/shard_map/ppermute | solution.py:682
  9.7 20.3 %collective-permute-start.2 = (f32[448,128]{1,0:T(8,128)S(1)}, f32[448,128]{1,0:T(8,128)S(1)}, u32[]{:S(2)}, u32[]{:S(2)}) collective-permute-start(f32[448,128]{1,0:T(8,128)S(1)} %get-tuple-element.42), channel_id=1, source_target_pairs={{0,760},{8,16},{16,8},{24,32},{32,24},{40,48},{48,40},{56,64},{64,... | collective-permute-start | bytes 688136 | tf_op jit(solution)/shard_map/ppermute | solution.py:715
  14.5 15.5 %collective-permute-start.3 = (f32[448,128]{1,0:T(8,128)S(1)}, f32[448,128]{1,0:T(8,128)S(1)}, u32[]{:S(2)}, u32[]{:S(2)}) collective-permute-start(f32[448,128]{1,0:T(8,128)S(1)} %get-tuple-element.43), channel_id=1, source_target_pairs={{0,8},{8,0},{16,24},{24,16},{32,40},{40,32},{48,56},{56,48},{64,72... | collective-permute-start | bytes 688136 | tf_op jit(solution)/shard_map/ppermute | solution.py:718

commit v7 on v6

--- a/solution.py
+++ b/solution.py
@@ -383,6 +383,7 @@
     edge_chem,
     middle,
     middle_moved,
+    level,
     buffer,
     sems,
 ):
@@ -458,6 +459,16 @@
                 edge_part[1, at : at + 1, :] = my
                 edge_chem[0, at : at + 1, :] = base
                 edge_chem[1, at : at + 1, :] = slope
+    for t in range(tiles):
+        row, rows = PAD + 8 * t, slice(8 * t, 8 * t + 8)
+        rock = pore[1, rows, :] == 0
+        for q in (0, 3, 4, 5, 6):
+            _, ey, ex = LINKS[q]
+            v = middle_moved[q - 5, rows, :] if ex else middle[q, row - ey : row - ey + 8, :]
+            if q:
+                open_ = masks(ex, 1, row - ey, 8) > 0.0
+                v = jnp.where(open_, v, middle[REVERSE[q], row : row + 8, :])
+            level[q, rows, :] = jnp.where(rock, sol[q, 1, rows, :], v)
     for copy in copies:
         copy.wait()
 
@@ -484,7 +495,7 @@
     edge_part,
     edge_chem,
     middle,
-    middle_moved,
+    level,
     across,
     on_chip,
     outer_flow,
@@ -502,6 +513,8 @@
     width = pop.shape[2]
     tiles = width // 8
     own = readers(moved, kept, mask)
+    for links in (pl.ds(0, 1), pl.ds(3, 4)):
+        pltpu.make_async_copy(level.at[links], solute.at[links, 1], sems.at[1]).start()
     for layer in (0, 2):
         local = [q for q in range(19) if 0 <= layer - LINKS[q][0] <= 2]
         start = 0
@@ -546,15 +559,13 @@
             for t in range(tiles):
                 row, rows = PAD + 8 * t, slice(8 * t, 8 * t + 8)
                 rock = pore[layer, rows, :] == 0
-                for q in range(7):
+                for q in (1, 2) if layer == 1 else range(7):
                     ez, ey, ex = LINKS[q]
                     src = layer - ez
                     if src == -1:
                         v = cross_s[0, rows, :]
                     elif src == 3:
                         v = cross_s[1, rows, :]
-                    elif ex and layer == 1:
-                        v = middle_moved[q - 5, rows, :]
                     elif ex:
                         v = faces_moved[q - 5, layer // 2, rows, :]
                     else:
@@ -563,7 +574,10 @@
                         open_ = masks(ex, src, row - ey, 8) > 0.0
                         v = jnp.where(open_, v, solute_at(REVERSE[q], layer, row, 8))
                     sbuf[q, layer, rows, :] = jnp.where(rock, sol[q, layer, rows, :], v)
-            pltpu.make_async_copy(sbuf.at[:, layer], solute.at[:, layer], sems.at[1]).start()
+            links = pl.ds(1, 2) if layer == 1 else pl.ds(0, 7)
+            pltpu.make_async_copy(
+                sbuf.at[links, layer], solute.at[links, layer], sems.at[1]
+            ).start()
 
         for side, ref, layer, outside, enter, leave in (
             (0, below, 0, -1, UP, DOWN),
@@ -716,7 +730,7 @@
         across, "gz", [(i, (i + 1 if i % 2 else i - 1) % gz) for i in range(gz)]
     )
     on_chip = lax.ppermute(on_chip, "gz", [(i, i + 1 - 2 * (i % 2)) for i in range(gz)])
-    flow, outer_flow, part, edge_part, edge_chem, middle, middle_moved = call(
+    flow, outer_flow, part, edge_part, edge_chem, middle, _, level = call(
         inner_kernel,
         (populations, solute, pore_mask, chem, moved, kept, mask, edges, table),
         [VMEM] * 9,
@@ -728,6 +742,7 @@
             ((2, 8, LX), VMEM),
             ((7, padded, LX), VMEM),
             ((2, width, LX), VMEM),
+            ((7, width, LX), VMEM),
         ],
         [(19, width, LX), DMA((2,))],
         flops=6_000_000,
@@ -736,7 +751,7 @@
         call(
             outer_kernel,
             cells[:3]
-            + (chem, moved, kept, mask, part, edge_part, edge_chem, middle, middle_moved)
+            + (chem, moved, kept, mask, part, edge_part, edge_chem, middle, level)
             + (across, on_chip, outer_flow, flow),
             [VMEM] * 15 + [ANY],
             [(populations.shape, ANY), (solute.shape, ANY)],

time: 31.4 us -> 31.9 us (1.016)
  Pallas kernels: 4.31 us -> 4.9 us
    pallas_call x5, Pallas kernels: 4.31 us -> 4.9 us  [call(): pl.pallas_call(kernel, out_shape=[jax.ShapeDtypeStruct(s, jnp.float32) fo...]
  transfers between devices with their start and end apart: 4 -> 4, of which waited for: 2 -> 1; matrix products, arithmetic and copies ran while one was open for 0% -> 0% of each run, Pallas kernels for 6% -> 7%
where the time goes in v7:
time: 31.9 us; the launch traced here: 31.7 us
  starting transfers between devices  25.8 us (81%)
  Pallas kernels  4.9 us (15%)
  between operations  0.78 us (2%)
    ppermute x1, starting transfers between devices, on_device(): lax.ppermute(on_chip, 'gz', [(i, i + 1 - 2 * (i % 2)) for i in range(gz)])  14.4 us
    pallas_call x5, Pallas kernels, call(): pl.pallas_call(kernel, out_shape=[jax.ShapeDtypeStruct(s, jnp.float32) fo...  4.9 us
    ppermute x1, starting transfers between devices, on_device(): lax.ppermute(across, 'gz', [(i, (i + 1 if i % 2 else i - 1) % gz) for i i...  4.82 us
    ppermute x1, starting transfers between devices, on_device(): second = lax.ppermute(second, ('gz', 'gy'), pairs(False))  4.19 us
    ppermute x1, starting transfers between devices, on_device(): first = lax.ppermute(first, ('gz', 'gy'), pairs(True))  2.31 us
  transfers between devices with their start and end apart: 4, of which 1 were waited for; matrix products, arithmetic and copies ran while one was open for 0% of the time, Pallas kernels for 7%

profile of v7, /device:TPU:33, one launch (start us, length us, event | category | flops | bytes accessed | tf_op | source)
XLA Modules:
  0.0 31.7 jit_solution(15410559185470098127)
XLA Ops:
  0.6 0.0 copy-start.1
  0.6 0.0 copy-start.2
  0.7 0.0 copy-start
  0.7 0.0 copy-start.3
  0.7 1.2 %pack_edges.1 = (f32[88,128]{1,0:T(8,128)S(1)}, f32[88,128]{1,0:T(8,128)S(1)}, f32[16,128]{1,0:T(8,128)S(1)}) custom-call(f32[19,3,48,128]{3,2,1,0:T(8,128)} %pop.7, f32[7,3,48,128]{3,2,1,0:T(8,128)} %sol.9, s32[3,48,128]{2,1,0:T(8,128)} %pore.7, s32[3,48,128]{2,1,0:T(8,128)} %ids.3, f32[8]{0:T(128)} %rates.1, f32[8]{0:T(128)} %target.1), custom_call_target="tpu_custom_call" | custom-call | flops 1000000 | bytes 1000000 | tf_op jit(solution)/shard_map/pack_edges/pallas_call | solution.py:651
  1.9 2.3 %collective-permute-start = (f32[88,128]{1,0:T(8,128)S(1)}, f32[88,128]{1,0:T(8,128)S(1)}, u32[]{:S(2)}, u32[]{:S(2)}) collective-permute-start(f32[88,128]{1,0:T(8,128)S(1)} %get-tuple-element.31), channel_id=1, source_target_pairs={{0,1},{1,2},{2,3},{3,4},{4,5},{5,6},{6,7},{8,9},{9,10},{10,11},{11... | collective-permute-start | bytes 135176 | tf_op jit(solution)/shard_map/ppermute | solution.py:695
  4.2 4.2 %collective-permute-start.1 = (f32[88,128]{1,0:T(8,128)S(1)}, f32[88,128]{1,0:T(8,128)S(1)}, u32[]{:S(2)}, u32[]{:S(2)}) collective-permute-start(f32[88,128]{1,0:T(8,128)S(1)} %get-tuple-element.32), channel_id=1, source_target_pairs={{1,0},{2,1},{3,2},{4,3},{5,4},{6,5},{7,6},{9,8},{10,9},{11,10},{12... | collective-permute-start | bytes 135176 | tf_op jit(solution)/shard_map/ppermute | solution.py:696
  8.4 0.0 copy-done.1
  8.4 0.0 copy-done.2
  8.4 0.0 copy-done
  8.4 0.0 copy-done.3
  8.4 0.8 %relax_kernel.1 = (f32[19,3,64,128]{3,2,1,0:T(8,128)S(1)}, f32[19,3,64,128]{3,2,1,0:T(8,128)S(1)}, f32[3,3,64,128]{3,2,1,0:T(8,128)S(1)}, f32[2,3,48,128]{3,2,1,...) custom-call(f32[19,3,48,128]{3,2,1,0:T(8,128)S(1)} %copy-done, f32[7,3,48,128]{3,2,1,0:T(8,128)S(1)} %copy-done.1, ...), custom_call_target="tpu_custom_call" | custom-call | flops 6000000 | bytes 1000000 | tf_op jit(solution)/shard_map/relax_kernel/pallas_call | solution.py:651
  9.2 0.0 collective-permute-done.first
  9.2 0.3 collective-permute-done.1.second
  9.5 0.2 face_kernel.1
  9.7 4.8 %collective-permute-start.2 = (f32[448,128]{1,0:T(8,128)S(1)}, f32[448,128]{1,0:T(8,128)S(1)}, u32[]{:S(2)}, u32[]{:S(2)}) collective-permute-start(f32[448,128]{1,0:T(8,128)S(1)} %get-tuple-element.42), channel_id=1, source_target_pairs={{0,760},{8,16},{16,8},{24,32},{32,24},{40,48},{48,40},{56,64},{64,... | collective-permute-start | bytes 688136 | tf_op jit(solution)/shard_map/ppermute | solution.py:729
  14.5 14.4 %collective-permute-start.3 = (f32[448,128]{1,0:T(8,128)S(1)}, f32[448,128]{1,0:T(8,128)S(1)}, u32[]{:S(2)}, u32[]{:S(2)}) collective-permute-start(f32[448,128]{1,0:T(8,128)S(1)} %get-tuple-element.43), channel_id=1, source_target_pairs={{0,8},{8,0},{16,24},{24,16},{32,40},{40,32},{48,56},{56,48},{64,72... | collective-permute-start | bytes 688136 | tf_op jit(solution)/shard_map/ppermute | solution.py:732
  29.0 1.6 %inner_kernel.1 = (f32[19,3,48,128]{3,2,1,0:T(8,128)}, f32[19,2,48,128]{3,2,1,0:T(8,128)S(1)}, f32[2,4,48,128]{3,2,1,0:T(8,128)S(1)}, f32[2,8,128]{2,1,0:T(8,128...) custom-call(f32[19,3,48,128]{3,2,1,0:T(8,128)S(1)} %copy-done, ...), custom_call_target="tpu_custom_call" | custom-call | flops 6000000 | bytes 1000000 | tf_op jit(solution)/shard_map/inner_kernel/pallas_call | solution.py:651
  30.6 0.0 collective-permute-done.2.across
  30.6 0.0 collective-permute-done.3.on_chip
  30.6 1.2 %outer_kernel.1 = (f32[19,3,48,128]{3,2,1,0:T(8,128)}, f32[7,3,48,128]{3,2,1,0:T(8,128)}) custom-call(f32[19,3,48,128]{3,2,1,0:T(8,128)S(1)} %copy-done, f32[7,3,48,128]{3,2,1,0:T(8,128)S(1)} %copy-done.1, s32[3,48,128]{2,1,0:T(8,128)S(1)} %copy-done.2, f32[2,3,48,128]{3,2,1,0:T(8,128)S(1)} %get-tuple-element.25.chem, ...), custom_call_target="tpu_custom_call", output_to_operand_aliasing={{0}: (15, {})} | custom-call | flops 1000000 | bytes 1000000 | tf_op jit(solution)/shard_map/outer_kernel/pallas_call | solution.py:651
Async XLA Ops:
  0.6 7.7 %copy-start.1 = (f32[7,3,48,128]{3,2,1,0:T(8,128)S(1)}, f32[7,3,48,128]{3,2,1,0:T(8,128)}, u32[]{:S(2)}) copy-start(f32[7,3,48,128]{3,2,1,0:T(8,128)} %sol.9) | copy-start | bytes 1548292
  0.6 7.7 %copy-start.2 = (s32[3,48,128]{2,1,0:T(8,128)S(1)}, s32[3,48,128]{2,1,0:T(8,128)}, u32[]{:S(2)}) copy-start(s32[3,48,128]{2,1,0:T(8,128)} %pore.7) | copy-start | bytes 221188
  0.7 7.7 %copy-start = (f32[19,3,48,128]{3,2,1,0:T(8,128)S(1)}, f32[19,3,48,128]{3,2,1,0:T(8,128)}, u32[]{:S(2)}) copy-start(f32[19,3,48,128]{3,2,1,0:T(8,128)} %pop.7) | copy-start | bytes 4202500
  0.7 7.7 %copy-start.3 = (s32[3,48,128]{2,1,0:T(8,128)S(1)}, s32[3,48,128]{2,1,0:T(8,128)}, u32[]{:S(2)}) copy-start(s32[3,48,128]{2,1,0:T(8,128)} %ids.3) | copy-start | bytes 221188
  1.9 7.3 %collective-permute-start = (f32[88,128]{1,0:T(8,128)S(1)}, f32[88,128]{1,0:T(8,128)S(1)}, u32[]{:S(2)}, u32[]{:S(2)}) collective-permute-start(f32[88,128]{1,0:T(8,128)S(1)} %get-tuple-element.31), channel_id=1, source_target_pairs={{0,1},{1,2},{2,3},{3,4},{4,5},{5,6},{6,7},{8,9},{9,10},{10,11},{11... | collective-permute-start | bytes 135176 | tf_op jit(solution)/shard_map/ppermute | solution.py:695
  4.2 5.3 %collective-permute-start.1 = (f32[88,128]{1,0:T(8,128)S(1)}, f32[88,128]{1,0:T(8,128)S(1)}, u32[]{:S(2)}, u32[]{:S(2)}) collective-permute-start(f32[88,128]{1,0:T(8,128)S(1)} %get-tuple-element.32), channel_id=1, source_target_pairs={{1,0},{2,1},{3,2},{4,3},{5,4},{6,5},{7,6},{9,8},{10,9},{11,10},{12... | collective-permute-start | bytes 135176 | tf_op jit(solution)/shard_map/ppermute | solution.py:696
  9.7 20.9 %collective-permute-start.2 = (f32[448,128]{1,0:T(8,128)S(1)}, f32[448,128]{1,0:T(8,128)S(1)}, u32[]{:S(2)}, u32[]{:S(2)}) collective-permute-start(f32[448,128]{1,0:T(8,128)S(1)} %get-tuple-element.42), channel_id=1, source_target_pairs={{0,760},{8,16},{16,8},{24,32},{32,24},{40,48},{48,40},{56,64},{64,... | collective-permute-start | bytes 688136 | tf_op jit(solution)/shard_map/ppermute | solution.py:729
  14.5 16.1 %collective-permute-start.3 = (f32[448,128]{1,0:T(8,128)S(1)}, f32[448,128]{1,0:T(8,128)S(1)}, u32[]{:S(2)}, u32[]{:S(2)}) collective-permute-start(f32[448,128]{1,0:T(8,128)S(1)} %get-tuple-element.43), channel_id=1, source_target_pairs={{0,8},{8,0},{16,24},{24,16},{32,40},{40,32},{48,56},{56,48},{64,72... | collective-permute-start | bytes 688136 | tf_op jit(solution)/shard_map/ppermute | solution.py:732
